TPU v7x, 256 devices: a whole 4x4x8 slice. The times are simulated.
256 devices in a mesh: frames: 32 (over z, x), cols: 8 (over y, core).
Axes of the slice: x: 4, y: 4, z: 8, core: 2. Of those that a mesh axis runs over, the one named last changes fastest.
Arguments:
- right_side: float32 [6, 65536], P(None, ('frames', 'cols')), may hold values from -6 to 6
- diag_blocks: float32 [6, 6, 65536], P(None, None, ('frames', 'cols')), may hold values from -0.6 to 24, as said below
- band_blocks: float32 [8, 6, 6, 65536], P(None, None, None, ('frames', 'cols')), may hold values from -0.6 to 0.6
- reach: int32 [65536], P(('frames', 'cols')), may hold values from 1 to 8
- tiles: float32 [32, 8, 8, 384, 384], P('frames', 'cols'), may hold values from -0.09185587 to 0.09185587
- tile_rows: int32 [32, 8, 8], P('frames', 'cols'), may hold values from 0 to 31
- tile_cols: int32 [32, 8, 8], P('frames', 'cols'), may hold values from 0 to 127
- tile_count: int32 [32, 8], P('frames', 'cols'), may hold values from 1 to 8
Outputs:
- solution: float32 [6, 65536], P(None, ('frames', 'cols'))
- residual: float32 [6, 65536], P(None, ('frames', 'cols'))
Inputs may be any that keep to these rules, and one draw needn't show every extreme that they name: `diag_blocks`: each block is symmetric, with diagonal entries at least 6 and larger than the sum of its other entries' magnitudes in that row, so each block is positive definite.
All inputs are finite; a program needn't handle non-finite values.
Results may differ from a plain program's by a relative error of at most 0.0003.
Values sent between devices are 32-bit elements; how exact they have to be, the bound alone decides.
No kernel may reach another device: no remote copies, remote signals or barrier semaphores. Data moves between devices by JAX's collectives and lax.ppermute only.
A program may use at most 64 MiB of HBM per device.

v0:
```python
import jax
import jax.numpy as jnp
from jax import lax
from jax.experimental import pallas as pl
from jax.experimental.pallas import tpu as pltpu
from jax.sharding import PartitionSpec as P


ITERS = 4
BAND = 8
LANES = 128
F32 = jnp.float32
ROWS = ("frames", "cols")


def lane_ids(rows):
    return lax.broadcasted_iota(jnp.int32, (rows, LANES), 1)


def half_turn(x):
    return pltpu.roll(x, 64, 1)


def left(x, by):
    return pltpu.roll(x, (x.shape[1] - by) % x.shape[1], 1) if by % x.shape[1] else x


def right(x, by):
    return pltpu.roll(x, by % x.shape[1], 1) if by % x.shape[1] else x


def store_as_tiles(ref, base, x):
    low = lane_ids(1) < 64
    for u in range(2):
        part = x[:, u * LANES : (u + 1) * LANES]
        turned = half_turn(part)
        for j in range(3):
            lanes = pl.ds(j * LANES, LANES)
            ref[pl.ds(base + 2 * u, 1), lanes] = jnp.where(
                low, part[2 * j : 2 * j + 1], turned[2 * j + 1 : 2 * j + 2]
            )
            ref[pl.ds(base + 2 * u + 1, 1), lanes] = jnp.where(
                low, turned[2 * j : 2 * j + 1], part[2 * j + 1 : 2 * j + 2]
            )


def store_as_natural(ref, t):
    low = lane_ids(1) < 64
    for j in range(3):
        part = t[:, j * LANES : (j + 1) * LANES]
        turned = half_turn(part)
        for u in range(2):
            lanes = pl.ds(u * LANES, LANES)
            ref[pl.ds(2 * j, 1), lanes] = jnp.where(
                low, part[2 * u : 2 * u + 1], turned[2 * u + 1 : 2 * u + 2]
            )
            ref[pl.ds(2 * j + 1, 1), lanes] = jnp.where(
                low, turned[2 * u : 2 * u + 1], part[2 * u + 1 : 2 * u + 2]
            )


def start_kernel(right_ref, diag_ref, band_ref, reach_ref, rows_ref, send_ref, masked_ref, pack):
    reach = reach_ref[...]
    for o in range(BAND):
        keep = (reach > o).astype(F32)
        for a in range(6):
            masked_ref[o * 6 + a] = band_ref[o, a] * keep
    sub = lax.broadcasted_iota(jnp.int32, (6, 256), 0)
    matrix = [diag_ref[a] for a in range(6)]
    inverse = [(sub == a).astype(F32) for a in range(6)]
    for p in range(6):
        pivot = matrix[p][p : p + 1]
        matrix[p] = matrix[p] / pivot
        inverse[p] = inverse[p] / pivot
        for a in range(6):
            if a != p:
                factor = matrix[a][p : p + 1]
                matrix[a] = matrix[a] - factor * matrix[p]
                inverse[a] = inverse[a] - factor * inverse[p]
    residual = right_ref[...]
    first = jnp.concatenate(
        [jnp.sum(inverse[a] * residual, axis=0, keepdims=True) for a in range(6)], axis=0
    )
    store_as_tiles(pack, 0, first)
    store_as_tiles(pack, 4, residual)
    for d in range(4):
        turned = jnp.concatenate(
            [inverse[a][(a + d) % 6 : (a + d) % 6 + 1] for a in range(6)], axis=0
        )
        store_as_tiles(pack, 8 + 4 * d, turned)
    ids = lane_ids(6)
    for j in range(3):
        packed = jnp.zeros((6, LANES), F32)
        for i in range(16):
            block = masked_ref[j * 16 + i, :, LANES : 2 * LANES]
            packed = jnp.where(ids // 8 == i, right(block, i * 8 + 8), packed)
        pack[24:30, j * LANES : (j + 1) * LANES] = packed
    pack[30:32, :] = jnp.zeros((2, 384), F32)
    rows = rows_ref[...]
    pack[30:31, 0:LANES] = ((rows // 4) * 8 + rows % 4).astype(F32)
    whole = pack[...]
    for c in range(8):
        send_ref[c] = whole


def own_edge(edge_ref, row_ref, col):
    last = row_ref[(col + 7) % 8][3:4]
    values = []
    for j in range(3):
        part = last[:, j * LANES : (j + 1) * LANES]
        values += [half_turn(part), part]
    total = jnp.zeros((6, LANES), F32)
    for o in range(BAND):
        z = edge_ref[o * 6] * values[0]
        for a in range(1, 6):
            z = z + edge_ref[o * 6 + a] * values[a]
        total = total + right(z, o + 1)
    total = jnp.where(lane_ids(6) < 8, total, 0.0)
    turned = half_turn(total)
    low = lane_ids(1) < 64
    return jnp.concatenate(
        [jnp.where(low, total[2 * j : 2 * j + 1], turned[2 * j + 1 : 2 * j + 2]) for j in range(3)],
        axis=1,
    )


def send_frames(row_ref, edge_ref, tiles_ref, rows_ref, cols_ref, count_ref, send_ref, edge_out, picked):
    frame = lax.axis_index("frames")
    col = lax.axis_index("cols")
    count = count_ref[0]
    own = row_ref[col]
    sub = lax.broadcasted_iota(jnp.int32, (8, 384), 0)
    chunk = jnp.where(sub < 4, own, 0.0)
    for f in range(32):
        send_ref[f] = chunk
    edge = own_edge(edge_ref, row_ref, col)
    edge_out[...] = jnp.where((sub == 0) & (col > 0), jnp.broadcast_to(edge, (8, 384)), 0.0)
    after = jnp.minimum(frame + 1, 31)
    cross = ((col == 0) & (frame < 31)).astype(F32)
    send_ref[after, 4:5, :] = edge * cross
    picked[...] = jnp.zeros((LANES, 384), F32)
    for s in range(8):
        r = rows_ref[s]
        picked[s : s + 1, :] = row_ref[r // 4, pl.ds(r % 4, 1), :]
    upright = [picked[:, j * LANES : (j + 1) * LANES].T for j in range(3)]
    for s in range(8):
        total = jnp.zeros((1, 384), F32)
        for j in range(3):
            column = upright[j][:, s : s + 1]
            tile = tiles_ref[s, j * LANES : (j + 1) * LANES, :]
            total = total + jnp.sum(tile * column, axis=0, keepdims=True)
        total = total * (s < count).astype(F32)
        q = cols_ref[s]
        send_ref[q // 4, pl.ds(4 + q % 4, 1), :] += total


def first_kernel(
    recv_ref, tiles_ref, rows_ref, cols_ref, count_ref,
    send_ref, edge_out, row_ref, edge_ref, pick_ref, inverse_ref, moment_ref, picked,
):
    col = lax.axis_index("cols")
    sub = lax.broadcasted_iota(jnp.int32, (8, 384), 0)
    moment = jnp.zeros((8, 384), F32)
    for c in range(8):
        both = recv_ref[c, 0:8, :]
        vector = jnp.where(sub < 4, both, 0.0)
        row_ref[c] = vector
        moment = moment + vector * pltpu.roll(both, 4, 0)
        block = [recv_ref[c, 8:16, :], recv_ref[c, 16:24, :]]
        parts = []
        for d in range(4):
            part = block[d // 2]
            part = pltpu.roll(part, 4, 0) if d % 2 else part
            parts.append(jnp.where(sub < 4, part, 0.0))
        parts += [left(parts[2], 256), left(parts[1], 320)]
        for d in range(6):
            inverse_ref[d, c] = parts[d]
    moment_ref[0] = moment[:, 0:128] + moment[:, 128:256] + moment[:, 256:384]
    prev = (col + 7) % 8
    ids = lane_ids(6)
    packed = recv_ref[prev, 24:32, :]
    for j in range(3):
        part = packed[0:6, j * LANES : (j + 1) * LANES]
        for i in range(16):
            edge_ref[j * 16 + i] = jnp.where(ids >= 120, right(part, 120 - i * 8), 0.0)
    lane = lane_ids(1)
    target = jnp.full((1, LANES), -1.0, F32)
    for c in range(8):
        at = lane - 16 * c
        target = jnp.where((at >= 0) & (at < 8), right(recv_ref[c, 30:31, 0:LANES], 16 * c), target)
        target = jnp.where((at >= 8) & (at < 12), (c * 8 + at - 8).astype(F32), target)
        target = jnp.where(at == 12, float(((c + 7) % 8) * 8 + 3), target)
    index = lax.broadcasted_iota(jnp.int32, (64, LANES), 0).astype(F32)
    pick_ref[...] = (index == jnp.broadcast_to(target, (64, LANES))).astype(F32)
    send_frames(row_ref, edge_ref, tiles_ref, rows_ref, cols_ref, count_ref, send_ref, edge_out, picked)


def row_image(recv_ref, pick_ref):
    received = recv_ref[...].reshape(LANES, 384)
    image = jnp.dot(
        pick_ref[...], received, precision=lax.Precision.HIGHEST, preferred_element_type=F32
    )
    return image.reshape(8, 8, 384)


def folded(x):
    x = jnp.sum(x, axis=0)
    return x[:, 0:128] + x[:, 128:256] + x[:, 256:384]


def next_kernel(
    recv_ref, pick_ref, inverse_ref, before_ref, edge_ref, tiles_ref, rows_ref, cols_ref, count_ref,
    send_ref, edge_out, row_ref, image_ref, moment_ref, picked,
):
    col = lax.axis_index("cols")
    image = row_image(recv_ref, pick_ref)
    flat = image.reshape(64, 384)
    vector = inverse_ref[0].reshape(64, 384) * flat
    for d in range(1, 6):
        vector = vector + inverse_ref[d].reshape(64, 384) * left(flat, 64 * d)
    vector = vector.reshape(8, 8, 384)
    row_ref[...] = vector
    moment_ref[0] = folded(before_ref[...] * image)
    moment_ref[1] = folded(vector * image)
    picked[0:64, :] = flat
    image_ref[...] = picked[pl.ds(pl.multiple_of(col * 8, 8), 8), :]
    send_frames(row_ref, edge_ref, tiles_ref, rows_ref, cols_ref, count_ref, send_ref, edge_out, picked)


def band_kernel(row_ref, masked_ref, edge_in, out_ref, natural, sums):
    col = lax.axis_index("cols")
    store_as_natural(natural, row_ref[col])
    lane = lax.broadcasted_iota(jnp.int32, (6, 256), 1)
    vector = natural[0:6, :]
    total = jnp.zeros((6, 256), F32)
    ahead = [jnp.zeros((6, 256), F32) for _ in range(6)]
    for o in range(BAND):
        shifted = jnp.where(lane < 255 - o, left(vector, o + 1), 0.0)
        z = jnp.zeros((6, 256), F32)
        for a in range(6):
            block = masked_ref[o * 6 + a]
            z = z + block * natural[a : a + 1, :]
            ahead[a] = ahead[a] + block * shifted
        total = total + jnp.where(lane > o, right(z, o + 1), 0.0)
    for a in range(6):
        sums[a : a + 1, :] = jnp.sum(ahead[a], axis=0, keepdims=True)
    out_ref[...] = jnp.zeros((8, 384), F32)
    store_as_tiles(out_ref, 0, total + sums[0:6, :])
    out_ref[0:1, :] = out_ref[0:1, :] + edge_in[0:1, :]


def cols_kernel(recv_ref, tiles_ref, row_ref, edge_ref, band_in, cols_ref, count_ref, send_ref, pack):
    frame = lax.axis_index("frames")
    col = lax.axis_index("cols")
    count = count_ref[0]
    total = recv_ref[0]
    for f in range(1, 32):
        total = total + recv_ref[f]
    sub = lax.broadcasted_iota(jnp.int32, (8, 384), 0)
    pack[8:16, :] = jnp.where(sub < 4, pltpu.roll(total, 4, 0) + band_in[...], 0.0)
    after = jnp.minimum(frame + 1, 31)
    here = (col > 0).astype(F32)
    there = ((col == 0) & (frame < 31)).astype(F32)
    start = row_ref[col][0:1] * here + recv_ref[after][0:1] * there
    parts = []
    for j in range(3):
        part = start[:, j * LANES : (j + 1) * LANES]
        parts += [part, half_turn(part)]
    ids = lane_ids(6)
    begin = jnp.concatenate(parts, axis=0)
    sums = [jnp.zeros((6, LANES), F32) for _ in range(6)]
    for o in range(BAND):
        shifted = jnp.where(ids >= 127 - o, left(begin, o + 1), 0.0)
        for a in range(6):
            sums[a] = sums[a] + edge_ref[o * 6 + a] * shifted
    sums = [jnp.sum(x, axis=0, keepdims=True) for x in sums]
    low = lane_ids(1) < 64
    for j in range(3):
        pack[12:13, j * LANES : (j + 1) * LANES] = jnp.where(
            low, half_turn(sums[2 * j]), sums[2 * j + 1]
        )
    for s in range(8):
        q = cols_ref[s]
        piece = recv_ref[q // 4, pl.ds(q % 4, 1), :] * (s < count).astype(F32)
        for j in range(3):
            rows = pl.ds(j * LANES, LANES)
            part = tiles_ref[s, rows, 0:LANES] * piece[:, 0:LANES]
            part = part + tiles_ref[s, rows, LANES : 2 * LANES] * piece[:, LANES : 2 * LANES]
            part = part + tiles_ref[s, rows, 2 * LANES : 384] * piece[:, 2 * LANES : 384]
            pack[s : s + 1, j * LANES : (j + 1) * LANES] = jnp.sum(part.T, axis=0, keepdims=True)
    whole = pack[...]
    for c in range(8):
        send_ref[c] = whole


def moments_kernel(recv_ref, pick_ref, before_ref, m0_ref, m1_ref, m2_ref, m3_ref, send_ref, image_ref, scratch):
    col = lax.axis_index("cols")
    image = row_image(recv_ref, pick_ref)
    scratch[...] = image.reshape(64, 384)
    image_ref[...] = scratch[pl.ds(pl.multiple_of(col * 8, 8), 8), :]
    parts = [m0_ref[0]]
    for ref in (m1_ref, m2_ref, m3_ref):
        parts += [ref[0], ref[1]]
    parts.append(folded(before_ref[...] * image))
    whole = jnp.concatenate([jnp.sum(x, axis=0, keepdims=True) for x in parts], axis=0)
    for f in range(32):
        send_ref[f] = whole


def end_kernel(recv_ref, right_ref, v0, v1, v2, v3, w0, w1, w2, w3, solution_ref, residual_ref, scratch):
    col = lax.axis_index("cols")
    total = recv_ref[0]
    for f in range(1, 32):
        total = total + recv_ref[f]
    sums = jnp.sum(total, axis=1, keepdims=True)
    mu = [jnp.broadcast_to(sums[i : i + 1], (1, LANES)) for i in range(8)]
    zero = jnp.zeros((1, LANES), F32)
    one = zero + 1.0

    def form(left_side, shift):
        value = zero
        for i in range(len(left_side)):
            for k in range(i, len(left_side)):
                term = left_side[i] * left_side[k]
                value = value + (term if i == k else term + term) * mu[i + k + shift]
        return value

    def ratio(top, bottom):
        return jnp.where(top == 0.0, 0.0, top / jnp.where(top == 0.0, one, bottom))

    direction, residual, solution = [one], [one], []
    gamma = mu[0]
    for it in range(ITERS):
        alpha = ratio(gamma, form(direction, 0) + form(direction, 1))
        solution = solution + [zero] * (len(direction) - len(solution))
        solution = [x + alpha * p for x, p in zip(solution, direction)]
        image = [p + q for p, q in zip(direction + [zero], [zero] + direction)]
        residual = residual + [zero] * (len(image) - len(residual))
        residual = [r - alpha * y for r, y in zip(residual, image)]
        if it + 1 < ITERS:
            fresh = form(residual, 0)
            beta = ratio(fresh, gamma)
            direction = direction + [zero] * (len(residual) - len(direction))
            direction = [r + beta * p for r, p in zip(residual, direction)]
            gamma = fresh

    def wide(x):
        return jnp.concatenate([x, x, x], axis=1)

    total = wide(solution[0]) * v0[col]
    for x, ref in zip(solution[1:], (v1, v2, v3)):
        total = total + wide(x) * ref[col]
    store_as_natural(solution_ref, total)
    total = wide(residual[1]) * w0[...]
    for x, ref in zip(residual[2:], (w1, w2, w3)):
        total = total + wide(x) * ref[...]
    store_as_natural(scratch, total)
    residual_ref[...] = scratch[0:6, :] + jnp.concatenate([residual[0]] * 2, axis=1) * right_ref[...]


VM = pl.BlockSpec(memory_space=pltpu.VMEM)
SM = pl.BlockSpec(memory_space=pltpu.SMEM)


def shape(*dims):
    return jax.ShapeDtypeStruct(dims, F32)


def call(kernel, specs, outs, scratch, name):
    return pl.pallas_call(
        kernel,
        in_specs=specs,
        out_specs=[VM] * len(outs),
        out_shape=outs,
        scratch_shapes=[pltpu.VMEM(s, F32) for s in scratch],
        compiler_params=pltpu.CompilerParams(vmem_limit_bytes=24 * 1024 * 1024),
        name=name,
    )


def per_device(right_side, diag_blocks, band_blocks, reach, tiles, tile_rows, tile_cols, tile_count):
    local = tiles.reshape(tiles.shape[2:])
    row_ids = tile_rows.reshape(-1)
    col_ids = tile_cols.reshape(-1)
    count = tile_count.reshape(-1)
    rows_wide = jnp.pad(row_ids, (0, LANES - 8)).reshape(1, LANES)

    def exchange(x, axis):
        return lax.all_to_all(x, axis, 0, 0, tiled=True)

    send, masked = call(
        start_kernel, [VM] * 5, [shape(8, 32, 384), shape(48, 6, 256)], [(32, 384)], "start"
    )(right_side, diag_blocks, band_blocks, reach.reshape(1, -1), rows_wide)
    recv = exchange(send, "cols")
    frames_out = [shape(32, 8, 384), shape(8, 384), shape(8, 8, 384)]
    send, edge, row, edges, pick, inverse, moment = call(
        first_kernel,
        [VM, VM, SM, SM, SM],
        frames_out + [shape(48, 6, LANES), shape(64, LANES), shape(6, 8, 8, 384), shape(1, 8, LANES)],
        [(LANES, 384)],
        "first",
    )(recv, local, row_ids, col_ids, count)
    vectors, images, moments = [row], [], [moment]
    for it in range(ITERS):
        recv = exchange(send, "frames")
        (band,) = call(band_kernel, [VM] * 3, [shape(8, 384)], [(8, 256), (8, 256)], "band")(
            row, masked, edge
        )
        (send,) = call(
            cols_kernel, [VM] * 5 + [SM] * 2, [shape(8, 16, 384)], [(16, 384)], "products"
        )(recv, local, row, edges, band, col_ids, count)
        recv = exchange(send, "cols")
        if it + 1 < ITERS:
            send, edge, row, image, moment = call(
                next_kernel,
                [VM] * 6 + [SM] * 3,
                frames_out + [shape(8, 384), shape(2, 8, LANES)],
                [(LANES, 384)],
                "next",
            )(recv, pick, inverse, row, edges, local, row_ids, col_ids, count)
            vectors.append(row)
            images.append(image)
            moments.append(moment)
    send, image = call(
        moments_kernel, [VM] * 7, [shape(32, 8, LANES), shape(8, 384)], [(64, 384)], "moments"
    )(recv, pick, row, *moments)
    images.append(image)
    recv = exchange(send, "frames")
    return tuple(
        call(end_kernel, [VM] * 10, [shape(6, 256), shape(6, 256)], [(8, 256)], "end")(
            recv, right_side, *vectors, *images
        )
    )


def solution(mesh):
    return jax.shard_map(
        per_device,
        mesh=mesh,
        in_specs=(
            P(None, ROWS),
            P(None, None, ROWS),
            P(None, None, None, ROWS),
            P(ROWS),
            P("frames", "cols", None, None, None),
            P("frames", "cols", None),
            P("frames", "cols", None),
            P("frames", "cols"),
        ),
        out_specs=(P(None, ROWS), P(None, ROWS)),
        check_vma=False,
    )
```

profile of v0, /device:TPU:1, one launch (start us, length us, event | category | flops | bytes accessed | tf_op | source)
XLA Modules:
  0.0 182.3 jit_solution(12375590329804440798)
XLA Ops:
  1.3 1.1 copy.10.band_ref
  2.4 0.8 copy-done.5
  4.5 1.0 start.1
  5.5 6.6 %all-to-all-start = ((f32[8,32,384]{2,1,0:T(8,128)}), f32[8,32,384]{2,1,0:T(8,128)S(1)}, u32[]{:S(2)}, u32[]{:S(2)}) async-start(f32[8,32,384]{2,1,0:T(8,128)} %get-tuple-element.28), calls=%async_computation | async-start | bytes 786432 | tf_op jit(solution)/shard_map/all_to_all | solution.py:389
  12.7 7.1 %all-to-all-done.recv_ref = f32[8,32,384]{2,1,0:T(8,128)S(1)} async-done(((f32[8,32,384]{2,1,0:T(8,128)}), f32[8,32,384]{2,1,0:T(8,128)S(1)}, u32[]{:S(2)}, u32[]{:S(2)}) %all-to-all-start) | async-done | bytes 393248 | tf_op jit(solution)/shard_map/all_to_all | solution.py:389
  19.8 2.3 %copy-done = f32[1,1,8,384,384]{4,3,2,1,0:T(8,128)S(1)} copy-done((f32[1,1,8,384,384]{4,3,2,1,0:T(8,128)S(1)}, f32[1,1,8,384,384]{4,3,2,1,0:T(8,128)}, u32[]{:S(2)}) %copy-start) | copy-done | bytes 4718616
  23.5 2.2 %first.1 = (f32[32,8,384]{2,1,0:T(8,128)}, f32[8,384]{1,0:T(8,128)S(1)}, f32[8,8,384]{2,1,0:T(8,128)S(1)}, f32[48,6,128]{2,1,0:T(8,128)S(1)}, f32[64,128]{1,0:T(...) custom-call(f32[8,32,384]{2,1,0:T(8,128)S(1)} %all-to-all-done.recv_ref, f32[8,384,384]{2,1,0:T(8,128)S(1)} %bitcast.15, ...), custom_call_target="tpu_custom_call" | custom-call | tf_op jit(solution)/shard_map/first/pallas_call | solution.py:396
  25.6 10.5 %all-to-all-start.1 = ((f32[32,8,384]{2,1,0:T(8,128)}), f32[32,8,384]{2,1,0:T(8,128)S(1)}, u32[]{:S(2)}, u32[]{:S(2)}) async-start(f32[32,8,384]{2,1,0:T(8,128)} %get-tuple-element.29), calls=%async_computation.1 | async-start | bytes 786432 | tf_op jit(solution)/shard_map/all_to_all | solution.py:389
  36.5 12.9 %all-to-all-done.1.recv_ref = f32[32,8,384]{2,1,0:T(8,128)S(1)} async-done(((f32[32,8,384]{2,1,0:T(8,128)}), f32[32,8,384]{2,1,0:T(8,128)S(1)}, u32[]{:S(2)}, u32[]{:S(2)}) %all-to-all-start.1) | async-done | bytes 393248 | tf_op jit(solution)/shard_map/all_to_all | solution.py:389
  49.4 2.3 %copy-done.1 = f32[1,1,8,384,384]{4,3,2,1,0:T(8,128)S(1)} copy-done((f32[1,1,8,384,384]{4,3,2,1,0:T(8,128)S(1)}, f32[1,1,8,384,384]{4,3,2,1,0:T(8,128)}, u32[]{:S(2)}) %copy-start.1) | copy-done | bytes 4718616
  51.8 1.2 products.4
  53.0 11.4 %all_to_all.50.recv_ref = f32[8,16,384]{2,1,0:T(8,128)S(1)} all-to-all(f32[8,16,384]{2,1,0:T(8,128)S(1)} %products.4), channel_id=1, replica_groups=mesh['frames'=32,'cols'=8] {'cols'}, dimensions={0} | all-to-all | bytes 393216 | tf_op jit(solution)/shard_map/all_to_all | solution.py:389
  64.4 2.4 %next.3 = (f32[32,8,384]{2,1,0:T(8,128)}, f32[8,384]{1,0:T(8,128)S(1)}, f32[8,8,384]{2,1,0:T(8,128)S(1)}, f32[8,384]{1,0:T(8,128)S(1)}, f32[2,8,128]{2,1,0:T(8,128)S(1)}) custom-call(f32[8,16,384]{2,1,0:T(8,128)S(1)} %all_to_all.50.recv_ref, f32[64,128]{1,0:T(8,128)S(1)} %get-tuple-element.34.pick_ref, f32[6,8,8,384]{3,2,1,0:T(8,128)S(1)} %get-tuple-element.35.inverse_ref, ...), custom_call_target="tpu_custom_call" | custom-call | tf_op jit(solution)/shard_map/next/pallas_call | solution.py:414
  66.8 3.9 %all-to-all-start.3 = ((f32[32,8,384]{2,1,0:T(8,128)}), f32[32,8,384]{2,1,0:T(8,128)S(1)}, u32[]{:S(2)}, u32[]{:S(2)}) async-start(f32[32,8,384]{2,1,0:T(8,128)} %get-tuple-element.36), calls=%async_computation.3 | async-start | bytes 786432 | tf_op jit(solution)/shard_map/all_to_all | solution.py:389
  71.0 13.5 %all-to-all-done.3.recv_ref = f32[32,8,384]{2,1,0:T(8,128)S(1)} async-done(((f32[32,8,384]{2,1,0:T(8,128)}), f32[32,8,384]{2,1,0:T(8,128)S(1)}, u32[]{:S(2)}, u32[]{:S(2)}) %all-to-all-start.3) | async-done | bytes 393248 | tf_op jit(solution)/shard_map/all_to_all | solution.py:389
  84.5 2.3 %copy-done.2 = f32[1,1,8,384,384]{4,3,2,1,0:T(8,128)S(1)} copy-done((f32[1,1,8,384,384]{4,3,2,1,0:T(8,128)S(1)}, f32[1,1,8,384,384]{4,3,2,1,0:T(8,128)}, u32[]{:S(2)}) %copy-start.2) | copy-done | bytes 4718616
  86.8 1.2 products.5
  88.0 10.8 %all_to_all.51.recv_ref = f32[8,16,384]{2,1,0:T(8,128)S(1)} all-to-all(f32[8,16,384]{2,1,0:T(8,128)S(1)} %products.5), channel_id=1, replica_groups=mesh['frames'=32,'cols'=8] {'cols'}, dimensions={0} | all-to-all | bytes 393216 | tf_op jit(solution)/shard_map/all_to_all | solution.py:389
  98.9 2.4 %next.4 = (f32[32,8,384]{2,1,0:T(8,128)}, f32[8,384]{1,0:T(8,128)S(1)}, f32[8,8,384]{2,1,0:T(8,128)S(1)}, f32[8,384]{1,0:T(8,128)S(1)}, f32[2,8,128]{2,1,0:T(8,128)S(1)}) custom-call(f32[8,16,384]{2,1,0:T(8,128)S(1)} %all_to_all.51.recv_ref, f32[64,128]{1,0:T(8,128)S(1)} %get-tuple-element.34.pick_ref, f32[6,8,8,384]{3,2,1,0:T(8,128)S(1)} %get-tuple-element.35.inverse_ref, ...), custom_call_target="tpu_custom_call" | custom-call | tf_op jit(solution)/shard_map/next/pallas_call | solution.py:414
  101.3 3.9 %all-to-all-start.5 = ((f32[32,8,384]{2,1,0:T(8,128)}), f32[32,8,384]{2,1,0:T(8,128)S(1)}, u32[]{:S(2)}, u32[]{:S(2)}) async-start(f32[32,8,384]{2,1,0:T(8,128)} %get-tuple-element.39), calls=%async_computation.5 | async-start | bytes 786432 | tf_op jit(solution)/shard_map/all_to_all | solution.py:389
  105.5 13.5 %all-to-all-done.5.recv_ref = f32[32,8,384]{2,1,0:T(8,128)S(1)} async-done(((f32[32,8,384]{2,1,0:T(8,128)}), f32[32,8,384]{2,1,0:T(8,128)S(1)}, u32[]{:S(2)}, u32[]{:S(2)}) %all-to-all-start.5) | async-done | bytes 393248 | tf_op jit(solution)/shard_map/all_to_all | solution.py:389
  119.0 2.3 %copy-done.3 = f32[1,1,8,384,384]{4,3,2,1,0:T(8,128)S(1)} copy-done((f32[1,1,8,384,384]{4,3,2,1,0:T(8,128)S(1)}, f32[1,1,8,384,384]{4,3,2,1,0:T(8,128)}, u32[]{:S(2)}) %copy-start.3) | copy-done | bytes 4718616
  121.3 1.2 products.6
  122.5 10.8 %all_to_all.52.recv_ref = f32[8,16,384]{2,1,0:T(8,128)S(1)} all-to-all(f32[8,16,384]{2,1,0:T(8,128)S(1)} %products.6), channel_id=1, replica_groups=mesh['frames'=32,'cols'=8] {'cols'}, dimensions={0} | all-to-all | bytes 393216 | tf_op jit(solution)/shard_map/all_to_all | solution.py:389
  133.4 2.4 %next.5 = (f32[32,8,384]{2,1,0:T(8,128)}, f32[8,384]{1,0:T(8,128)S(1)}, f32[8,8,384]{2,1,0:T(8,128)S(1)}, f32[8,384]{1,0:T(8,128)S(1)}, f32[2,8,128]{2,1,0:T(8,128)S(1)}) custom-call(f32[8,16,384]{2,1,0:T(8,128)S(1)} %all_to_all.52.recv_ref, f32[64,128]{1,0:T(8,128)S(1)} %get-tuple-element.34.pick_ref, f32[6,8,8,384]{3,2,1,0:T(8,128)S(1)} %get-tuple-element.35.inverse_ref, ...), custom_call_target="tpu_custom_call" | custom-call | tf_op jit(solution)/shard_map/next/pallas_call | solution.py:414
  135.8 4.0 %all-to-all-start.7 = ((f32[32,8,384]{2,1,0:T(8,128)}), f32[32,8,384]{2,1,0:T(8,128)S(1)}, u32[]{:S(2)}, u32[]{:S(2)}) async-start(f32[32,8,384]{2,1,0:T(8,128)} %get-tuple-element.42), calls=%async_computation.7 | async-start | bytes 786432 | tf_op jit(solution)/shard_map/all_to_all | solution.py:389
  140.1 13.5 %all-to-all-done.7.recv_ref = f32[32,8,384]{2,1,0:T(8,128)S(1)} async-done(((f32[32,8,384]{2,1,0:T(8,128)}), f32[32,8,384]{2,1,0:T(8,128)S(1)}, u32[]{:S(2)}, u32[]{:S(2)}) %all-to-all-start.7) | async-done | bytes 393248 | tf_op jit(solution)/shard_map/all_to_all | solution.py:389
  153.6 2.3 %copy-done.4 = f32[1,1,8,384,384]{4,3,2,1,0:T(8,128)S(1)} copy-done((f32[1,1,8,384,384]{4,3,2,1,0:T(8,128)S(1)}, f32[1,1,8,384,384]{4,3,2,1,0:T(8,128)}, u32[]{:S(2)}) %copy-start.4) | copy-done | bytes 4718616
  155.9 1.2 products.7
  157.2 10.8 %all_to_all.53.recv_ref = f32[8,16,384]{2,1,0:T(8,128)S(1)} all-to-all(f32[8,16,384]{2,1,0:T(8,128)S(1)} %products.7), channel_id=1, replica_groups=mesh['frames'=32,'cols'=8] {'cols'}, dimensions={0} | all-to-all | bytes 393216 | tf_op jit(solution)/shard_map/all_to_all | solution.py:389
  168.3 13.1 %all_to_all.54.recv_ref = f32[32,8,128]{2,1,0:T(8,128)S(1)} all-to-all(f32[32,8,128]{2,1,0:T(8,128)S(1)} %get-tuple-element.49), channel_id=1, replica_groups=mesh['frames'=32,'cols'=8] {'frames'}, dimensions={0} | all-to-all | bytes 262144 | tf_op jit(solution)/shard_map/all_to_all | solution.py:389
  181.4 0.9 end.1
  (26 shorter events, 4.8 us)
Async XLA Ops:
  0.6 48.8 %copy-start.9 = (s32[1,1,8]{2,1,0:T(1,128)S(1)}, s32[1,1,8]{2,1,0:T(1,128)}, u32[]{:S(2)}) copy-start(s32[1,1,8]{2,1,0:T(1,128)} %param.14) | copy-start | bytes 100
  2.4 0.8 copy-start.5
  3.2 0.7 copy-start.6
  3.9 0.7 copy-start.12
  5.5 14.3 %all-to-all-start = ((f32[8,32,384]{2,1,0:T(8,128)}), f32[8,32,384]{2,1,0:T(8,128)S(1)}, u32[]{:S(2)}, u32[]{:S(2)}) async-start(f32[8,32,384]{2,1,0:T(8,128)} %get-tuple-element.28), calls=%async_computation | async-start | bytes 786432 | tf_op jit(solution)/shard_map/all_to_all | solution.py:389
  19.8 2.3 %copy-start = (f32[1,1,8,384,384]{4,3,2,1,0:T(8,128)S(1)}, f32[1,1,8,384,384]{4,3,2,1,0:T(8,128)}, u32[]{:S(2)}) copy-start(f32[1,1,8,384,384]{4,3,2,1,0:T(8,128)} %param.12) | copy-start | bytes 14155780
  22.2 0.7 copy-start.8
  22.8 0.7 copy-start.10
  25.6 38.8 %copy-start.11 = (s32[1,1,8]{2,1,0:T(1,128)S(1)}, s32[1,1,8]{2,1,0:T(1,128)}, u32[]{:S(2)}) copy-start(s32[1,1,8]{2,1,0:T(1,128)} %param.13) | copy-start | bytes 100
  25.6 23.8 %all-to-all-start.1 = ((f32[32,8,384]{2,1,0:T(8,128)}), f32[32,8,384]{2,1,0:T(8,128)S(1)}, u32[]{:S(2)}, u32[]{:S(2)}) async-start(f32[32,8,384]{2,1,0:T(8,128)} %get-tuple-element.29), calls=%async_computation.1 | async-start | bytes 786432 | tf_op jit(solution)/shard_map/all_to_all | solution.py:389
  49.4 2.3 %copy-start.1 = (f32[1,1,8,384,384]{4,3,2,1,0:T(8,128)S(1)}, f32[1,1,8,384,384]{4,3,2,1,0:T(8,128)}, u32[]{:S(2)}) copy-start(f32[1,1,8,384,384]{4,3,2,1,0:T(8,128)} %param.12) | copy-start | bytes 14155780
  66.8 17.6 %all-to-all-start.3 = ((f32[32,8,384]{2,1,0:T(8,128)}), f32[32,8,384]{2,1,0:T(8,128)S(1)}, u32[]{:S(2)}, u32[]{:S(2)}) async-start(f32[32,8,384]{2,1,0:T(8,128)} %get-tuple-element.36), calls=%async_computation.3 | async-start | bytes 786432 | tf_op jit(solution)/shard_map/all_to_all | solution.py:389
  84.5 2.3 %copy-start.2 = (f32[1,1,8,384,384]{4,3,2,1,0:T(8,128)S(1)}, f32[1,1,8,384,384]{4,3,2,1,0:T(8,128)}, u32[]{:S(2)}) copy-start(f32[1,1,8,384,384]{4,3,2,1,0:T(8,128)} %param.12) | copy-start | bytes 14155780
  101.3 17.7 %all-to-all-start.5 = ((f32[32,8,384]{2,1,0:T(8,128)}), f32[32,8,384]{2,1,0:T(8,128)S(1)}, u32[]{:S(2)}, u32[]{:S(2)}) async-start(f32[32,8,384]{2,1,0:T(8,128)} %get-tuple-element.39), calls=%async_computation.5 | async-start | bytes 786432 | tf_op jit(solution)/shard_map/all_to_all | solution.py:389
  119.0 2.3 %copy-start.3 = (f32[1,1,8,384,384]{4,3,2,1,0:T(8,128)S(1)}, f32[1,1,8,384,384]{4,3,2,1,0:T(8,128)}, u32[]{:S(2)}) copy-start(f32[1,1,8,384,384]{4,3,2,1,0:T(8,128)} %param.12) | copy-start | bytes 14155780
  135.8 45.6 %copy-start.7 = (f32[6,256]{1,0:T(8,128)S(1)}, f32[6,256]{1,0:T(8,128)}, u32[]{:S(2)}) copy-start(f32[6,256]{1,0:T(8,128)} %right_ref.3) | copy-start | bytes 18436
  135.8 17.8 %all-to-all-start.7 = ((f32[32,8,384]{2,1,0:T(8,128)}), f32[32,8,384]{2,1,0:T(8,128)S(1)}, u32[]{:S(2)}, u32[]{:S(2)}) async-start(f32[32,8,384]{2,1,0:T(8,128)} %get-tuple-element.42), calls=%async_computation.7 | async-start | bytes 786432 | tf_op jit(solution)/shard_map/all_to_all | solution.py:389
  153.6 2.3 %copy-start.4 = (f32[1,1,8,384,384]{4,3,2,1,0:T(8,128)S(1)}, f32[1,1,8,384,384]{4,3,2,1,0:T(8,128)}, u32[]{:S(2)}) copy-start(f32[1,1,8,384,384]{4,3,2,1,0:T(8,128)} %param.12) | copy-start | bytes 14155780
where the time goes:
time: 183 us; the launch traced here: 182 us
  waiting for transfers between devices  60.4 us (33%)
  blocking collectives  57 us (31%)
  starting transfers between devices  28.9 us (16%)
  Pallas kernels  17.6 us (10%)
  local copies, waits for them, and re-layouts  16.9 us (9%)
    all_to_all x5, waiting for transfers between devices, exchange(): return lax.all_to_all(x, axis, 0, 0, tiled=True)  60.4 us
    all_to_all x5, blocking collectives, exchange(): return lax.all_to_all(x, axis, 0, 0, tiled=True)  57 us
    all_to_all x5, starting transfers between devices, exchange(): return lax.all_to_all(x, axis, 0, 0, tiled=True)  28.9 us
    unnamed x27, local copies, waits for them, and re-layouts  16.2 us
    pallas_call x3, Pallas kernels, per_device(): call(next_kernel, [VM] * 6 + [SM] * 3, frames_out + [shape(8, 384), shape...  7.15 us
    pallas_call x4, Pallas kernels, per_device(): call(cols_kernel, [VM] * 5 + [SM] * 2, [shape(8, 16, 384)], [(16, 384)],...  4.99 us
  transfers between devices with their start and end apart: 5, of which 5 were waited for; matrix products, arithmetic and copies ran while one was open for 0% of the time, Pallas kernels for 1%

commit v1 on v0

v1 whole, which is shorter than its diff:
```python
import jax
import jax.numpy as jnp
from jax import lax
from jax.experimental import pallas as pl
from jax.experimental.pallas import tpu as pltpu
from jax.sharding import PartitionSpec as P


ITERS = 4
BAND = 8
LANES = 128
F32 = jnp.float32
ROWS = ("frames", "cols")


def lane_ids(rows):
    return lax.broadcasted_iota(jnp.int32, (rows, LANES), 1)


def half_turn(x):
    return pltpu.roll(x, 64, 1)


def left(x, by):
    return pltpu.roll(x, (x.shape[1] - by) % x.shape[1], 1) if by % x.shape[1] else x


def right(x, by):
    return pltpu.roll(x, by % x.shape[1], 1) if by % x.shape[1] else x


def store_as_tiles(ref, base, x):
    low = lane_ids(1) < 64
    for u in range(2):
        part = x[:, u * LANES : (u + 1) * LANES]
        turned = half_turn(part)
        for j in range(3):
            lanes = pl.ds(j * LANES, LANES)
            ref[pl.ds(base + 2 * u, 1), lanes] = jnp.where(
                low, part[2 * j : 2 * j + 1], turned[2 * j + 1 : 2 * j + 2]
            )
            ref[pl.ds(base + 2 * u + 1, 1), lanes] = jnp.where(
                low, turned[2 * j : 2 * j + 1], part[2 * j + 1 : 2 * j + 2]
            )


def store_as_natural(ref, t):
    low = lane_ids(1) < 64
    for j in range(3):
        part = t[:, j * LANES : (j + 1) * LANES]
        turned = half_turn(part)
        for u in range(2):
            lanes = pl.ds(u * LANES, LANES)
            ref[pl.ds(2 * j, 1), lanes] = jnp.where(
                low, part[2 * u : 2 * u + 1], turned[2 * u + 1 : 2 * u + 2]
            )
            ref[pl.ds(2 * j + 1, 1), lanes] = jnp.where(
                low, turned[2 * u : 2 * u + 1], part[2 * u + 1 : 2 * u + 2]
            )


def start_kernel(
    right_hbm, diag_hbm, band_hbm, reach_hbm, rows_hbm, cols_hbm, tiles_hbm,
    send_ref, masked_ref, rows_ref, cols_ref, tiles_ref,
    right_ref, diag_ref, band_ref, reach_ref, pack, *sems,
):
    copies = [
        pltpu.make_async_copy(source, to, sem)
        for source, to, sem in zip(
            (diag_hbm, right_hbm, reach_hbm, band_hbm, rows_hbm, cols_hbm),
            (diag_ref, right_ref, reach_ref, band_ref, rows_ref, cols_ref),
            sems,
        )
    ]
    copies += [
        pltpu.make_async_copy(tiles_hbm.at[s], tiles_ref.at[s], sems[6 + s]) for s in range(4)
    ]
    for copy in copies:
        copy.start()
    for copy in copies[:2]:
        copy.wait()
    sub = lax.broadcasted_iota(jnp.int32, (6, 256), 0)
    matrix = [diag_ref[a] for a in range(6)]
    inverse = [(sub == a).astype(F32) for a in range(6)]
    for p in range(6):
        pivot = matrix[p][p : p + 1]
        matrix[p] = matrix[p] / pivot
        inverse[p] = inverse[p] / pivot
        for a in range(6):
            if a != p:
                factor = matrix[a][p : p + 1]
                matrix[a] = matrix[a] - factor * matrix[p]
                inverse[a] = inverse[a] - factor * inverse[p]
    residual = right_ref[...]
    first = jnp.concatenate(
        [jnp.sum(inverse[a] * residual, axis=0, keepdims=True) for a in range(6)], axis=0
    )
    store_as_tiles(pack, 0, first)
    store_as_tiles(pack, 4, residual)
    for d in range(4):
        turned = jnp.concatenate(
            [inverse[a][(a + d) % 6 : (a + d) % 6 + 1] for a in range(6)], axis=0
        )
        store_as_tiles(pack, 8 + 4 * d, turned)
    for copy in copies[2:6]:
        copy.wait()
    reach = reach_ref[...]
    for o in range(BAND):
        keep = (reach > o).astype(F32)
        for a in range(6):
            masked_ref[o * 6 + a] = band_ref[a, :, o, :] * keep
    ids = lane_ids(6)
    for j in range(3):
        packed = jnp.zeros((6, LANES), F32)
        for i in range(16):
            block = masked_ref[j * 16 + i, :, LANES : 2 * LANES]
            packed = jnp.where(ids // 8 == i, right(block, i * 8 + 8), packed)
        pack[24:30, j * LANES : (j + 1) * LANES] = packed
    pack[30:32, :] = jnp.zeros((2, 384), F32)
    rows = rows_ref[...]
    pack[30:31, 0:8] = ((rows // 4) * 8 + rows % 4).astype(F32)
    whole = pack[...]
    for c in range(8):
        send_ref[c] = whole
    for copy in copies[6:]:
        copy.wait()


def own_edge(edge_ref, row_ref, col):
    last = row_ref[(col + 7) % 8][3:4]
    values = []
    for j in range(3):
        part = last[:, j * LANES : (j + 1) * LANES]
        values += [half_turn(part), part]
    total = jnp.zeros((6, LANES), F32)
    for o in range(BAND):
        z = edge_ref[o * 6] * values[0]
        for a in range(1, 6):
            z = z + edge_ref[o * 6 + a] * values[a]
        total = total + right(z, o + 1)
    total = jnp.where(lane_ids(6) < 8, total, 0.0)
    turned = half_turn(total)
    low = lane_ids(1) < 64
    return jnp.concatenate(
        [jnp.where(low, total[2 * j : 2 * j + 1], turned[2 * j + 1 : 2 * j + 2]) for j in range(3)],
        axis=1,
    )


def transposed_products(row_ref, tiles_refs, ids_refs, picked):
    rows_ref, _, count_ref = ids_refs
    count = count_ref[0, 0]
    picked[...] = jnp.zeros((LANES, 384), F32)
    for s in range(8):
        r = rows_ref[0, s]
        picked[s : s + 1, :] = row_ref[r // 4, pl.ds(r % 4, 1), :]
    upright = [picked[:, j * LANES : (j + 1) * LANES].T for j in range(3)]
    products = []
    for s in range(8):
        total = jnp.zeros((1, 384), F32)
        for j in range(3):
            column = upright[j][:, s : s + 1]
            tile = tiles_refs[s // 4][s % 4, j * LANES : (j + 1) * LANES, :]
            total = total + jnp.sum(tile * column, axis=0, keepdims=True)
        products.append(total * (s < count).astype(F32))
    return products


def edge_terms(row_ref, edge_ref):
    frame = lax.axis_index("frames")
    col = lax.axis_index("cols")
    edge = own_edge(edge_ref, row_ref, col)
    cross = ((col == 0) & (frame < 31)).astype(F32)
    return edge * (col > 0).astype(F32), edge * cross


def band_terms(row_ref, masked_ref, edge, out_ref, natural, sums):
    col = lax.axis_index("cols")
    store_as_natural(natural, row_ref[col])
    lane = lax.broadcasted_iota(jnp.int32, (6, 256), 1)
    vector = natural[0:6, :]
    total = jnp.zeros((6, 256), F32)
    ahead = [jnp.zeros((6, 256), F32) for _ in range(6)]
    for o in range(BAND):
        shifted = jnp.where(lane < 255 - o, left(vector, o + 1), 0.0)
        z = jnp.zeros((6, 256), F32)
        for a in range(6):
            block = masked_ref[o * 6 + a]
            z = z + block * natural[a : a + 1, :]
            ahead[a] = ahead[a] + block * shifted
        total = total + jnp.where(lane > o, right(z, o + 1), 0.0)
    for a in range(6):
        sums[a : a + 1, :] = jnp.sum(ahead[a], axis=0, keepdims=True)
    out_ref[...] = jnp.zeros((8, 384), F32)
    store_as_tiles(out_ref, 0, total + sums[0:6, :])
    out_ref[0:1, :] = out_ref[0:1, :] + edge


def send_frames(row_ref, edge_ref, masked_ref, tiles_refs, ids_refs, send_ref, band_ref, scratch, copies=()):
    picked, natural, sums = scratch
    col = lax.axis_index("cols")
    sub = lax.broadcasted_iota(jnp.int32, (8, 384), 0)
    chunk = jnp.where(sub < 4, row_ref[col], 0.0)
    for f in range(32):
        send_ref[f] = chunk
    mine, onward = edge_terms(row_ref, edge_ref)
    send_ref[jnp.minimum(lax.axis_index("frames") + 1, 31), 4:5, :] = onward
    band_terms(row_ref, masked_ref, mine, band_ref, natural, sums)
    for copy in copies:
        copy.wait()
    for s, product in enumerate(transposed_products(row_ref, tiles_refs, ids_refs, picked)):
        q = ids_refs[1][0, s]
        send_ref[q // 4, pl.ds(4 + q % 4, 1), :] += product


def send_last(row_ref, edge_ref, masked_ref, tiles_refs, ids_refs, known, send_ref, band_ref, scratch):
    picked, natural, sums, pack = scratch
    col = lax.axis_index("cols")
    mine, onward = edge_terms(row_ref, edge_ref)
    band_terms(row_ref, masked_ref, mine, band_ref, natural, sums)
    own = row_ref[col]
    products = transposed_products(row_ref, tiles_refs, ids_refs, picked)
    for j in range(3):
        lanes = slice(j * LANES, (j + 1) * LANES)
        for s in range(8):
            pack[8 * j + s : 8 * j + s + 1, :] = products[s][:, lanes]
        pack[24 + 4 * j : 28 + 4 * j, :] = own[0:4, lanes]
        pack[36 + j : 37 + j, :] = onward[:, lanes]
    part = own * band_ref[...]
    quad = jnp.sum(part[:, 0:128] + part[:, 128:256] + part[:, 256:384], axis=0, keepdims=True)
    part = own[0:1] * mine
    quad = quad + part[:, 0:128] + part[:, 128:256] + part[:, 256:384]
    rows = [jnp.sum(x, axis=0, keepdims=True) for x in known] + [quad]
    lane = lax.broadcasted_iota(jnp.int32, (8, LANES), 1)
    sub = lax.broadcasted_iota(jnp.int32, (8, LANES), 0)
    totals = jnp.sum(jnp.concatenate(rows, axis=0), axis=1, keepdims=True)
    misc = jnp.sum(jnp.where(lane == sub + 8, totals, 0.0), axis=0, keepdims=True)
    for s in range(8):
        misc = jnp.where(lane_ids(1) == s, ids_refs[1][0, s].astype(F32), misc)
    pack[39:40, :] = misc
    whole = pack[...]
    for f in range(32):
        send_ref[f] = whole


def first_kernel(
    recv_ref, masked_ref, tiles_hbm, early_ref, rows_ref, cols_ref, count_ref,
    send_ref, band_ref, row_ref, edge_ref, pick_ref, inverse_ref, moment_ref, late_ref,
    picked, natural, sums, *sems,
):
    copies = [
        pltpu.make_async_copy(tiles_hbm.at[4 + s], late_ref.at[s], sems[s]) for s in range(4)
    ]
    for copy in copies:
        copy.start()
    col = lax.axis_index("cols")
    sub = lax.broadcasted_iota(jnp.int32, (8, 384), 0)
    moment = jnp.zeros((8, 384), F32)
    for c in range(8):
        both = recv_ref[c, 0:8, :]
        vector = jnp.where(sub < 4, both, 0.0)
        row_ref[c] = vector
        moment = moment + vector * pltpu.roll(both, 4, 0)
        block = [recv_ref[c, 8:16, :], recv_ref[c, 16:24, :]]
        parts = []
        for d in range(4):
            part = block[d // 2]
            part = pltpu.roll(part, 4, 0) if d % 2 else part
            parts.append(jnp.where(sub < 4, part, 0.0))
        parts += [left(parts[2], 256), left(parts[1], 320)]
        for d in range(6):
            inverse_ref[d, c] = parts[d]
    moment_ref[0] = moment[:, 0:128] + moment[:, 128:256] + moment[:, 256:384]
    prev = (col + 7) % 8
    ids = lane_ids(6)
    packed = recv_ref[prev, 24:32, :]
    for j in range(3):
        part = packed[0:6, j * LANES : (j + 1) * LANES]
        for i in range(16):
            edge_ref[j * 16 + i] = jnp.where(ids >= 120, right(part, 120 - i * 8), 0.0)
    lane = lane_ids(1)
    target = jnp.full((1, LANES), -1.0, F32)
    for c in range(8):
        at = lane - 16 * c
        target = jnp.where((at >= 0) & (at < 8), right(recv_ref[c, 30:31, 0:LANES], 16 * c), target)
        target = jnp.where((at >= 8) & (at < 12), (c * 8 + at - 8).astype(F32), target)
        target = jnp.where(at == 12, float(((c + 7) % 8) * 8 + 3), target)
    index = lax.broadcasted_iota(jnp.int32, (64, LANES), 0).astype(F32)
    pick_ref[...] = (index == jnp.broadcast_to(target, (64, LANES))).astype(F32)
    ids_refs = (rows_ref, cols_ref, count_ref)
    scratch = (picked, natural, sums)
    tiles_refs = (early_ref, late_ref)
    send_frames(
        row_ref, edge_ref, masked_ref, tiles_refs, ids_refs, send_ref, band_ref, scratch, copies
    )


def row_image(recv_ref, pick_ref):
    received = recv_ref[...].reshape(LANES, 384)
    image = jnp.dot(
        pick_ref[...], received, precision=lax.Precision.HIGHEST, preferred_element_type=F32
    )
    return image.reshape(8, 8, 384)


def folded(x):
    x = jnp.sum(x, axis=0)
    return x[:, 0:128] + x[:, 128:256] + x[:, 256:384]


def advance(recv_ref, pick_ref, inverse_ref, before_ref, row_ref, image_ref, moment_ref, picked):
    col = lax.axis_index("cols")
    image = row_image(recv_ref, pick_ref)
    flat = image.reshape(64, 384)
    vector = inverse_ref[0].reshape(64, 384) * flat
    for d in range(1, 6):
        vector = vector + inverse_ref[d].reshape(64, 384) * left(flat, 64 * d)
    vector = vector.reshape(8, 8, 384)
    row_ref[...] = vector
    moments = [folded(before_ref[...] * image), folded(vector * image)]
    if moment_ref is not None:
        moment_ref[0], moment_ref[1] = moments
    picked[0:64, :] = flat
    image_ref[...] = picked[pl.ds(pl.multiple_of(col * 8, 8), 8), :]
    return moments


def next_kernel(
    recv_ref, pick_ref, inverse_ref, before_ref, edge_ref, masked_ref, early_ref, late_ref, rows_ref, cols_ref, count_ref,
    send_ref, band_ref, row_ref, image_ref, moment_ref, *scratch,
):
    advance(recv_ref, pick_ref, inverse_ref, before_ref, row_ref, image_ref, moment_ref, scratch[0])
    ids_refs = (rows_ref, cols_ref, count_ref)
    tiles_refs = (early_ref, late_ref)
    send_frames(row_ref, edge_ref, masked_ref, tiles_refs, ids_refs, send_ref, band_ref, scratch)


def last_kernel(
    recv_ref, pick_ref, inverse_ref, before_ref, edge_ref, masked_ref, early_ref, late_ref, rows_ref, cols_ref, count_ref,
    m0_ref, m1_ref, m2_ref, send_ref, band_ref, row_ref, image_ref, *scratch,
):
    moments = advance(recv_ref, pick_ref, inverse_ref, before_ref, row_ref, image_ref, None, scratch[0])
    known = [m0_ref[0], m1_ref[0], m1_ref[1], m2_ref[0], m2_ref[1]] + moments
    ids_refs = (rows_ref, cols_ref, count_ref)
    tiles_refs = (early_ref, late_ref)
    send_last(row_ref, edge_ref, masked_ref, tiles_refs, ids_refs, known, send_ref, band_ref, scratch)


def onward_terms(edge_ref, start):
    parts = []
    for j in range(3):
        part = start[:, j * LANES : (j + 1) * LANES]
        parts += [part, half_turn(part)]
    ids = lane_ids(6)
    begin = jnp.concatenate(parts, axis=0)
    sums = [jnp.zeros((6, LANES), F32) for _ in range(6)]
    for o in range(BAND):
        shifted = jnp.where(ids >= 127 - o, left(begin, o + 1), 0.0)
        for a in range(6):
            sums[a] = sums[a] + edge_ref[o * 6 + a] * shifted
    sums = [jnp.sum(x, axis=0, keepdims=True) for x in sums]
    low = lane_ids(1) < 64
    return jnp.concatenate(
        [jnp.where(low, half_turn(sums[2 * j]), sums[2 * j + 1]) for j in range(3)], axis=1
    )


def tile_products(tiles_refs, piece_of, count, pack):
    for s in range(8):
        piece = piece_of(s) * (s < count).astype(F32)
        for j in range(3):
            rows = pl.ds(j * LANES, LANES)
            tile = tiles_refs[s // 4]
            part = tile[s % 4, rows, 0:LANES] * piece[:, 0:LANES]
            part = part + tile[s % 4, rows, LANES : 2 * LANES] * piece[:, LANES : 2 * LANES]
            part = part + tile[s % 4, rows, 2 * LANES : 384] * piece[:, 2 * LANES : 384]
            pack[s : s + 1, j * LANES : (j + 1) * LANES] = jnp.sum(part.T, axis=0, keepdims=True)


def cols_kernel(recv_ref, early_ref, late_ref, row_ref, edge_ref, band_ref, cols_ref, count_ref, send_ref, pack):
    frame = lax.axis_index("frames")
    col = lax.axis_index("cols")
    total = recv_ref[0]
    for f in range(1, 32):
        total = total + recv_ref[f]
    sub = lax.broadcasted_iota(jnp.int32, (8, 384), 0)
    pack[8:16, :] = jnp.where(sub < 4, pltpu.roll(total, 4, 0) + band_ref[...], 0.0)
    here = (col > 0).astype(F32)
    there = ((col == 0) & (frame < 31)).astype(F32)
    start = row_ref[col][0:1] * here + recv_ref[jnp.minimum(frame + 1, 31)][0:1] * there
    pack[12:13, :] = onward_terms(edge_ref, start)

    def piece_of(s):
        q = cols_ref[0, s]
        return recv_ref[q // 4, pl.ds(q % 4, 1), :]

    tile_products((early_ref, late_ref), piece_of, count_ref[0, 0], pack)
    whole = pack[...]
    for c in range(8):
        send_ref[c] = whole


def finish_kernel(
    recv_ref, early_ref, late_ref, row_ref, edge_ref, band_ref, cols_ref, count_ref, send_ref, known_ref, pack
):
    frame = lax.axis_index("frames")
    col = lax.axis_index("cols")
    lane = lane_ids(1)
    misc = [recv_ref[f, 39:40, :] for f in range(32)]
    total = misc[0]
    for x in misc[1:]:
        total = total + x
    known_ref[...] = jnp.broadcast_to(total, (8, LANES))
    halves = []
    for h in range(2):
        tags = jnp.zeros((1, LANES), F32)
        for i in range(16):
            tags = jnp.where(lane // 8 == i, right(misc[16 * h + i], 8 * i), tags)
        halves.append(tags)
    tags = jnp.concatenate(halves, axis=1)
    products = jnp.concatenate(
        [recv_ref[:, 8 * j : 8 * j + 8, :].reshape(256, LANES) for j in range(3)], axis=1
    )

    def dot(a, b):
        return jnp.dot(a, b, precision=lax.Precision.HIGHEST, preferred_element_type=F32)

    at = lax.broadcasted_iota(jnp.int32, (256, 256), 0)
    wanted = ((at // 8) * 4 + at % 4).astype(F32)
    sums = dot((wanted == jnp.broadcast_to(tags, (256, 256))).astype(F32), products)
    low = lax.broadcasted_iota(jnp.int32, (8, LANES), 0) < 4
    quad = jnp.zeros((8, LANES), F32)
    for f in range(32):
        here = sums[8 * f : 8 * f + 8]
        quad = quad + jnp.where(low, here[:, 0:128], here[:, 128:256]) * recv_ref[f, 24:32, :]
        quad = quad + jnp.where(low, here[:, 256:384] * recv_ref[f, 32:40, :], 0.0)
    quad = jnp.sum(quad, axis=0, keepdims=True)
    for f in range(31):
        for j in range(3):
            quad = quad + recv_ref[f, 36 + j : 37 + j, :] * recv_ref[f + 1, 24 + 4 * j : 25 + 4 * j, :]
    quad = quad + quad + jnp.where(lane == 15, total, 0.0)

    sub = lax.broadcasted_iota(jnp.int32, (8, 256), 0)
    mine = dot((jnp.broadcast_to(tags, (8, 256)) == (4 * frame + sub % 4).astype(F32)).astype(F32), products)
    sub = lax.broadcasted_iota(jnp.int32, (8, 384), 0)
    pack[8:16, :] = jnp.where(sub < 4, mine + band_ref[...], 0.0)
    before = jnp.maximum(frame - 1, 0)
    for j in range(3):
        lanes = slice(j * LANES, (j + 1) * LANES)
        edge = recv_ref[before, 36 + j : 37 + j, :] * (frame > 0).astype(F32)
        pack[8:9, lanes] = pack[8:9, lanes] + edge
    here = (col > 0).astype(F32)
    there = ((col == 0) & (frame < 31)).astype(F32)
    after = jnp.minimum(frame + 1, 31)

    def row_of(f, i):
        return jnp.concatenate([recv_ref[f, pl.ds(24 + 4 * j + i, 1), :] for j in range(3)], axis=1)

    pack[12:13, :] = onward_terms(edge_ref, row_ref[col][0:1] * here + row_of(after, 0) * there)
    pack[13:14, 0:LANES] = quad

    def piece_of(s):
        q = cols_ref[0, s]
        return row_of(q // 4, q % 4)

    tile_products((early_ref, late_ref), piece_of, count_ref[0, 0], pack)
    whole = pack[...]
    for c in range(8):
        send_ref[c] = whole


def end_kernel(
    recv_ref, pick_ref, known_ref, right_ref, v0, v1, v2, v3, w0, w1, w2, solution_ref, residual_ref, scratch
):
    col = lax.axis_index("cols")
    last = jnp.dot(
        pick_ref[pl.ds(pl.multiple_of(col * 8, 8), 8), :],
        recv_ref[...].reshape(LANES, 384),
        precision=lax.Precision.HIGHEST,
        preferred_element_type=F32,
    )
    total = recv_ref[0, 13:14, 0:LANES]
    for c in range(1, 8):
        total = total + recv_ref[c, 13:14, 0:LANES]
    known = known_ref[0:1, :]
    mu = [jnp.broadcast_to(known[:, 8 + i : 9 + i], (1, LANES)) for i in range(7)]
    mu.append(jnp.broadcast_to(jnp.sum(total, axis=1, keepdims=True), (1, LANES)))
    zero = jnp.zeros((1, LANES), F32)
    one = zero + 1.0

    def form(left_side, shift):
        value = zero
        for i in range(len(left_side)):
            for k in range(i, len(left_side)):
                term = left_side[i] * left_side[k]
                value = value + (term if i == k else term + term) * mu[i + k + shift]
        return value

    def ratio(top, bottom):
        return jnp.where(top == 0.0, 0.0, top / jnp.where(top == 0.0, one, bottom))

    direction, residual, solution = [one], [one], []
    gamma = mu[0]
    for it in range(ITERS):
        alpha = ratio(gamma, form(direction, 0) + form(direction, 1))
        solution = solution + [zero] * (len(direction) - len(solution))
        solution = [x + alpha * p for x, p in zip(solution, direction)]
        image = [p + q for p, q in zip(direction + [zero], [zero] + direction)]
        residual = residual + [zero] * (len(image) - len(residual))
        residual = [r - alpha * y for r, y in zip(residual, image)]
        if it + 1 < ITERS:
            fresh = form(residual, 0)
            beta = ratio(fresh, gamma)
            direction = direction + [zero] * (len(residual) - len(direction))
            direction = [r + beta * p for r, p in zip(residual, direction)]
            gamma = fresh

    def wide(x):
        return jnp.concatenate([x, x, x], axis=1)

    total = wide(solution[0]) * v0[col]
    for x, ref in zip(solution[1:], (v1, v2, v3)):
        total = total + wide(x) * ref[col]
    store_as_natural(solution_ref, total)
    total = wide(residual[4]) * last
    for x, ref in zip(residual[1:4], (w0, w1, w2)):
        total = total + wide(x) * ref[...]
    store_as_natural(scratch, total)
    residual_ref[...] = scratch[0:6, :] + jnp.concatenate([residual[0]] * 2, axis=1) * right_ref[...]


VM = pl.BlockSpec(memory_space=pltpu.VMEM)
SM = pl.BlockSpec(memory_space=pltpu.SMEM)
HB = pl.BlockSpec(memory_space=pltpu.HBM)


def shape(*dims, kind=F32):
    return jax.ShapeDtypeStruct(dims, kind)


def call(kernel, specs, outs, scratch, name):
    return pl.pallas_call(
        kernel,
        in_specs=specs,
        out_specs=[VM] * len(outs),
        out_shape=outs,
        scratch_shapes=[pltpu.VMEM(s, F32) if isinstance(s, tuple) else s for s in scratch],
        compiler_params=pltpu.CompilerParams(vmem_limit_bytes=24 * 1024 * 1024),
        name=name,
    )


def per_device(right_side, diag_blocks, band_blocks, reach, tiles, tile_rows, tile_cols, tile_count):
    def exchange(x, axis):
        return lax.all_to_all(x, axis, 0, 0, tiled=True)

    def in_hbm(x):
        return pltpu.with_memory_space_constraint(x, pltpu.HBM)

    sem = pltpu.SemaphoreType.DMA(())
    stored = in_hbm(tiles.reshape(tiles.shape[2:]))
    inputs = (right_side, diag_blocks, jnp.transpose(band_blocks, (1, 2, 0, 3)), reach.reshape(1, -1))
    inputs += (tile_rows.reshape(1, 8), tile_cols.reshape(1, 8))
    send, masked, *ids, early = call(
        start_kernel,
        [HB] * 7,
        [shape(8, 32, 384), shape(48, 6, 256)]
        + [shape(1, 8, kind=jnp.int32)] * 2
        + [shape(4, 384, 384)],
        [(6, 256), (6, 6, 256), (6, 6, 8, 256), pltpu.VMEM((1, 256), jnp.int32), (32, 384)]
        + [sem] * 10,
        "start",
    )(*[in_hbm(x) for x in inputs], stored)
    ids.append(tile_count)
    recv = exchange(send, "cols")
    frames_out = [shape(32, 8, 384), shape(8, 384), shape(8, 8, 384)]
    scratch = [(LANES, 384), (8, 256), (8, 256)]
    send, band, row, edges, pick, inverse, moment, late = call(
        first_kernel,
        [VM] * 2 + [HB, VM] + [SM] * 3,
        frames_out
        + [shape(48, 6, LANES), shape(64, LANES), shape(6, 8, 8, 384), shape(1, 8, LANES)]
        + [shape(4, 384, 384)],
        scratch + [sem] * 4,
        "first",
    )(recv, masked, stored, early, *ids)
    vectors, images, moments = [row], [], [moment]
    for it in range(ITERS - 1):
        recv = exchange(send, "frames")
        (send,) = call(
            cols_kernel, [VM] * 6 + [SM] * 2, [shape(8, 16, 384)], [(16, 384)], "products"
        )(recv, early, late, row, edges, band, *ids[1:])
        recv = exchange(send, "cols")
        given = (recv, pick, inverse, row, edges, masked, early, late, *ids)
        if it + 2 < ITERS:
            send, band, row, image, moment = call(
                next_kernel,
                [VM] * 8 + [SM] * 3,
                frames_out + [shape(8, 384), shape(2, 8, LANES)],
                scratch,
                "next",
            )(*given)
            moments.append(moment)
        else:
            send, band, row, image = call(
                last_kernel,
                [VM] * 8 + [SM] * 3 + [VM] * 3,
                [shape(32, 40, LANES), shape(8, 384), shape(8, 8, 384), shape(8, 384)],
                scratch + [(40, LANES)],
                "last",
            )(*given, *moments)
        vectors.append(row)
        images.append(image)
    recv = exchange(send, "frames")
    send, known = call(
        finish_kernel, [VM] * 6 + [SM] * 2, [shape(8, 16, 384), shape(8, LANES)], [(16, 384)], "finish"
    )(recv, early, late, row, edges, band, *ids[1:])
    recv = exchange(send, "cols")
    return tuple(
        call(end_kernel, [VM] * 11, [shape(6, 256), shape(6, 256)], [(8, 256)], "end")(
            recv, pick, known, right_side, *vectors, *images
        )
    )


def solution(mesh):
    return jax.shard_map(
        per_device,
        mesh=mesh,
        in_specs=(
            P(None, ROWS),
            P(None, None, ROWS),
            P(None, None, None, ROWS),
            P(ROWS),
            P("frames", "cols", None, None, None),
            P("frames", "cols", None),
            P("frames", "cols", None),
            P("frames", "cols"),
        ),
        out_specs=(P(None, ROWS), P(None, ROWS)),
        check_vma=False,
    )
```

time: 183 us -> 157 us (0.86)
  blocking collectives: 57 us -> 125 us
  waiting for transfers between devices: 60.4 us -> 7.07 us
  starting transfers between devices: 28.9 us -> 6.57 us
  local copies, waits for them, and re-layouts: 16.9 us -> 0.01 us
    all_to_all x5 -> x8, blocking collectives: 57 us -> 125 us  [exchange(): return lax.all_to_all(x, axis, 0, 0, tiled=True)]
    all_to_all x5 -> x1, waiting for transfers between devices: 60.4 us -> 7.07 us  [exchange(): return lax.all_to_all(x, axis, 0, 0, tiled=True)]
    all_to_all x5 -> x1, starting transfers between devices: 28.9 us -> 6.57 us  [exchange(): return lax.all_to_all(x, axis, 0, 0, tiled=True)]
    unnamed x27 -> x2, local copies, waits for them, and re-layouts: 16.2 us -> 0.01 us
    pallas_call x15 -> x10, Pallas kernels: 17.6 us -> 17.2 us  [the longest x3 3.76 us: per_device(): call(cols_kernel, [VM] * 6 + [SM] * 2, [shape(8, 16, 384)], [(16, 384)],...]
  transfers between devices with their start and end apart: 5 -> 1, of which waited for: 5 -> 1; matrix products, arithmetic and copies ran while one was open for 0% -> 0% of each run, Pallas kernels for 1% -> 0%
where the time goes in v1:
time: 157 us
  blocking collectives  125 us (80%)
  Pallas kernels  17.2 us (11%)
  waiting for transfers between devices  7.07 us (5%)
  starting transfers between devices  6.57 us (4%)
    all_to_all x8, blocking collectives, exchange(): return lax.all_to_all(x, axis, 0, 0, tiled=True)  125 us
    all_to_all x1, waiting for transfers between devices, exchange(): return lax.all_to_all(x, axis, 0, 0, tiled=True)  7.07 us
    all_to_all x1, starting transfers between devices, exchange(): return lax.all_to_all(x, axis, 0, 0, tiled=True)  6.57 us
    pallas_call x3, Pallas kernels, per_device(): call(cols_kernel, [VM] * 6 + [SM] * 2, [shape(8, 16, 384)], [(16, 384)],...  3.76 us
    pallas_call x2, Pallas kernels, per_device(): call(next_kernel, [VM] * 8 + [SM] * 3, frames_out + [shape(8, 384), shape...  3.52 us
  transfers between devices with their start and end apart: 1, of which 1 were waited for; matrix products, arithmetic and copies ran while one was open for 0% of the time, Pallas kernels for 0%

profile of v1, /device:TPU:1, one launch (start us, length us, event | category | flops | bytes accessed | tf_op | source)
XLA Modules:
  0.0 156.8 jit_solution(389474483385655081)
XLA Ops:
  0.6 2.6 %start.1 = (f32[8,32,384]{2,1,0:T(8,128)}, f32[48,6,256]{2,1,0:T(8,128)S(1)}, s32[1,8]{1,0:T(1,128)S(1)}, s32[1,8]{1,0:T(1,128)S(1)}, f32[4,384,384]{2,1,0:T(8,128)S(1)}) custom-call(f32[6,256]{1,0:T(8,128)} %right_ref.1, f32[6,6,256]{2,1,0:T(8,128)} %diag_hbm.1, f32[6,6,8,256]{3,2,1,0:T(8,128)} %bitcast.7, s32[1,256]{1,0:T(1,128)} %bitcast.8, ...), custom_call_target="tpu_custom_call" | custom-call | tf_op jit(solution)/shard_map/start/pallas_call | solution.py:564
  3.3 6.6 %all-to-all-start = ((f32[8,32,384]{2,1,0:T(8,128)}), f32[8,32,384]{2,1,0:T(8,128)S(1)}, u32[]{:S(2)}, u32[]{:S(2)}) async-start(f32[8,32,384]{2,1,0:T(8,128)} %get-tuple-element.31), calls=%async_computation | async-start | bytes 786432 | tf_op jit(solution)/shard_map/all_to_all | solution.py:555
  10.5 7.1 %all-to-all-done.recv_ref = f32[8,32,384]{2,1,0:T(8,128)S(1)} async-done(((f32[8,32,384]{2,1,0:T(8,128)}), f32[8,32,384]{2,1,0:T(8,128)S(1)}, u32[]{:S(2)}, u32[]{:S(2)}) %all-to-all-start) | async-done | bytes 393248 | tf_op jit(solution)/shard_map/all_to_all | solution.py:555
  17.5 3.0 %first.1 = (f32[32,8,384]{2,1,0:T(8,128)S(1)}, f32[8,384]{1,0:T(8,128)S(1)}, f32[8,8,384]{2,1,0:T(8,128)S(1)}, f32[48,6,128]{2,1,0:T(8,128)S(1)}, f32[64,128]{1,...) custom-call(f32[8,32,384]{2,1,0:T(8,128)S(1)} %all-to-all-done.recv_ref, ...), custom_call_target="tpu_custom_call" | custom-call | tf_op jit(solution)/shard_map/first/pallas_call | solution.py:578
  20.6 23.4 %all_to_all.45.recv_ref = f32[32,8,384]{2,1,0:T(8,128)S(1)} all-to-all(f32[32,8,384]{2,1,0:T(8,128)S(1)} %get-tuple-element.36), channel_id=1, replica_groups=mesh['frames'=32,'cols'=8] {'frames'}, dimensions={0} | all-to-all | bytes 786432 | tf_op jit(solution)/shard_map/all_to_all | solution.py:555
  44.0 1.3 products.3
  45.3 11.4 %all_to_all.46.recv_ref = f32[8,16,384]{2,1,0:T(8,128)S(1)} all-to-all(f32[8,16,384]{2,1,0:T(8,128)S(1)} %products.3), channel_id=1, replica_groups=mesh['frames'=32,'cols'=8] {'cols'}, dimensions={0} | all-to-all | bytes 393216 | tf_op jit(solution)/shard_map/all_to_all | solution.py:555
  56.7 1.8 %next.2 = (f32[32,8,384]{2,1,0:T(8,128)S(1)}, f32[8,384]{1,0:T(8,128)S(1)}, f32[8,8,384]{2,1,0:T(8,128)S(1)}, f32[8,384]{1,0:T(8,128)S(1)}, f32[2,8,128]{2,1,0:T(8,128)S(1)}) custom-call(f32[8,16,384]{2,1,0:T(8,128)S(1)} %all_to_all.46.recv_ref, f32[64,128]{1,0:T(8,128)S(1)} %get-tuple-element.41.pick_ref, ...), custom_call_target="tpu_custom_call" | custom-call | tf_op jit(solution)/shard_map/next/pallas_call | solution.py:596
  58.5 17.4 %all_to_all.47.recv_ref = f32[32,8,384]{2,1,0:T(8,128)S(1)} all-to-all(f32[32,8,384]{2,1,0:T(8,128)S(1)} %get-tuple-element.43), channel_id=1, replica_groups=mesh['frames'=32,'cols'=8] {'frames'}, dimensions={0} | all-to-all | bytes 786432 | tf_op jit(solution)/shard_map/all_to_all | solution.py:555
  75.9 1.2 products.4
  77.2 10.8 %all_to_all.48.recv_ref = f32[8,16,384]{2,1,0:T(8,128)S(1)} all-to-all(f32[8,16,384]{2,1,0:T(8,128)S(1)} %products.4), channel_id=1, replica_groups=mesh['frames'=32,'cols'=8] {'cols'}, dimensions={0} | all-to-all | bytes 393216 | tf_op jit(solution)/shard_map/all_to_all | solution.py:555
  88.0 1.8 %next.3 = (f32[32,8,384]{2,1,0:T(8,128)S(1)}, f32[8,384]{1,0:T(8,128)S(1)}, f32[8,8,384]{2,1,0:T(8,128)S(1)}, f32[8,384]{1,0:T(8,128)S(1)}, f32[2,8,128]{2,1,0:T(8,128)S(1)}) custom-call(f32[8,16,384]{2,1,0:T(8,128)S(1)} %all_to_all.48.recv_ref, f32[64,128]{1,0:T(8,128)S(1)} %get-tuple-element.41.pick_ref, ...), custom_call_target="tpu_custom_call" | custom-call | tf_op jit(solution)/shard_map/next/pallas_call | solution.py:596
  89.8 17.5 %all_to_all.49.recv_ref = f32[32,8,384]{2,1,0:T(8,128)S(1)} all-to-all(f32[32,8,384]{2,1,0:T(8,128)S(1)} %get-tuple-element.46), channel_id=1, replica_groups=mesh['frames'=32,'cols'=8] {'frames'}, dimensions={0} | all-to-all | bytes 786432 | tf_op jit(solution)/shard_map/all_to_all | solution.py:555
  107.3 1.2 products.5
  108.5 10.8 %all_to_all.50.recv_ref = f32[8,16,384]{2,1,0:T(8,128)S(1)} all-to-all(f32[8,16,384]{2,1,0:T(8,128)S(1)} %products.5), channel_id=1, replica_groups=mesh['frames'=32,'cols'=8] {'cols'}, dimensions={0} | all-to-all | bytes 393216 | tf_op jit(solution)/shard_map/all_to_all | solution.py:555
  119.3 1.8 %last.1 = (f32[32,40,128]{2,1,0:T(8,128)S(1)}, f32[8,384]{1,0:T(8,128)S(1)}, f32[8,8,384]{2,1,0:T(8,128)S(1)}, f32[8,384]{1,0:T(8,128)S(1)}) custom-call(f32[8,16,384]{2,1,0:T(8,128)S(1)} %all_to_all.50.recv_ref, f32[64,128]{1,0:T(8,128)S(1)} %get-tuple-element.41.pick_ref, f32[6,8,8,384]{3,2,1,0:T(8,128)S(1)} %get-tuple-element.42.inverse_ref, ...), custom_call_target="tpu_custom_call" | custom-call | tf_op jit(solution)/shard_map/last/pallas_call | solution.py:605
  121.2 22.1 %all_to_all.51.recv_ref = f32[32,40,128]{2,1,0:T(8,128)S(1)} all-to-all(f32[32,40,128]{2,1,0:T(8,128)S(1)} %get-tuple-element.52), channel_id=1, replica_groups=mesh['frames'=32,'cols'=8] {'frames'}, dimensions={0} | all-to-all | bytes 1310720 | tf_op jit(solution)/shard_map/all_to_all | solution.py:555
  143.3 0.0 copy-start
  143.3 1.5 finish.1
  144.8 11.0 %all_to_all.52.recv_ref = f32[8,16,384]{2,1,0:T(8,128)S(1)} all-to-all(f32[8,16,384]{2,1,0:T(8,128)S(1)} %get-tuple-element.55), channel_id=1, replica_groups=mesh['frames'=32,'cols'=8] {'cols'}, dimensions={0} | all-to-all | bytes 393216 | tf_op jit(solution)/shard_map/all_to_all | solution.py:555
  155.8 0.0 copy-done
  155.8 0.9 end.1
Async XLA Ops:
  3.3 14.3 %all-to-all-start = ((f32[8,32,384]{2,1,0:T(8,128)}), f32[8,32,384]{2,1,0:T(8,128)S(1)}, u32[]{:S(2)}, u32[]{:S(2)}) async-start(f32[8,32,384]{2,1,0:T(8,128)} %get-tuple-element.31), calls=%async_computation | async-start | bytes 786432 | tf_op jit(solution)/shard_map/all_to_all | solution.py:555
  143.3 12.6 %copy-start = (f32[6,256]{1,0:T(8,128)S(1)}, f32[6,256]{1,0:T(8,128)}, u32[]{:S(2)}) copy-start(f32[6,256]{1,0:T(8,128)} %right_ref.1) | copy-start | bytes 18436

commit v2 on v1

--- a/solution.py
+++ b/solution.py
@@ -11,6 +11,7 @@
 LANES = 128
 F32 = jnp.float32
 ROWS = ("frames", "cols")
+EARLY = 3
 
 
 def lane_ids(rows):
@@ -61,8 +62,8 @@
 
 def start_kernel(
     right_hbm, diag_hbm, band_hbm, reach_hbm, rows_hbm, cols_hbm, tiles_hbm,
-    send_ref, masked_ref, rows_ref, cols_ref, tiles_ref,
-    right_ref, diag_ref, band_ref, reach_ref, pack, *sems,
+    send_ref, masked_ref, extra_ref, rows_ref, cols_ref, tiles_ref,
+    right_ref, diag_ref, band_ref, reach_ref, pack, lines, *sems,
 ):
     copies = [
         pltpu.make_async_copy(source, to, sem)
@@ -73,7 +74,7 @@
         )
     ]
     copies += [
-        pltpu.make_async_copy(tiles_hbm.at[s], tiles_ref.at[s], sems[6 + s]) for s in range(4)
+        pltpu.make_async_copy(tiles_hbm.at[s], tiles_ref.at[s], sems[6 + s]) for s in range(EARLY)
     ]
     for copy in copies:
         copy.start()
@@ -96,12 +97,20 @@
         [jnp.sum(inverse[a] * residual, axis=0, keepdims=True) for a in range(6)], axis=0
     )
     store_as_tiles(pack, 0, first)
-    store_as_tiles(pack, 4, residual)
+    for j in range(3):
+        lines[4 * j : 4 * j + 4, :] = pack[0:4, j * LANES : (j + 1) * LANES]
     for d in range(4):
         turned = jnp.concatenate(
             [inverse[a][(a + d) % 6 : (a + d) % 6 + 1] for a in range(6)], axis=0
         )
-        store_as_tiles(pack, 8 + 4 * d, turned)
+        store_as_tiles(pack, 0, turned)
+        for j in range(3):
+            at = (3 * d + j) * 4
+            extra_ref[at : at + 4, :] = pack[0:4, j * LANES : (j + 1) * LANES]
+    product = first * residual
+    product = jnp.sum(product[:, 0:LANES] + product[:, LANES:256], axis=0, keepdims=True)
+    product = jnp.sum(product, axis=1, keepdims=True)
+    extra_ref[48:49, :] = jnp.where(lane_ids(1) == 8, product, 0.0)
     for copy in copies[2:6]:
         copy.wait()
     reach = reach_ref[...]
@@ -115,11 +124,9 @@
         for i in range(16):
             block = masked_ref[j * 16 + i, :, LANES : 2 * LANES]
             packed = jnp.where(ids // 8 == i, right(block, i * 8 + 8), packed)
-        pack[24:30, j * LANES : (j + 1) * LANES] = packed
-    pack[30:32, :] = jnp.zeros((2, 384), F32)
-    rows = rows_ref[...]
-    pack[30:31, 0:8] = ((rows // 4) * 8 + rows % 4).astype(F32)
-    whole = pack[...]
+        lines[12 + 6 * j : 18 + 6 * j, :] = packed
+    lines[30:32, :] = jnp.zeros((2, LANES), F32)
+    whole = lines[...]
     for c in range(8):
         send_ref[c] = whole
     for copy in copies[6:]:
@@ -147,7 +154,11 @@
     )
 
 
-def transposed_products(row_ref, tiles_refs, ids_refs, picked):
+def slot_of(tiles_refs, s):
+    return tiles_refs[0].at[s] if s < EARLY else tiles_refs[1].at[s - EARLY]
+
+
+def transposed_products(row_ref, tiles_refs, ids_refs, picked, copies=()):
     rows_ref, _, count_ref = ids_refs
     count = count_ref[0, 0]
     picked[...] = jnp.zeros((LANES, 384), F32)
@@ -157,10 +168,12 @@
     upright = [picked[:, j * LANES : (j + 1) * LANES].T for j in range(3)]
     products = []
     for s in range(8):
+        if copies and s >= EARLY:
+            copies[s - EARLY].wait()
         total = jnp.zeros((1, 384), F32)
         for j in range(3):
             column = upright[j][:, s : s + 1]
-            tile = tiles_refs[s // 4][s % 4, j * LANES : (j + 1) * LANES, :]
+            tile = slot_of(tiles_refs, s)[j * LANES : (j + 1) * LANES, :]
             total = total + jnp.sum(tile * column, axis=0, keepdims=True)
         products.append(total * (s < count).astype(F32))
     return products
@@ -206,9 +219,7 @@
     mine, onward = edge_terms(row_ref, edge_ref)
     send_ref[jnp.minimum(lax.axis_index("frames") + 1, 31), 4:5, :] = onward
     band_terms(row_ref, masked_ref, mine, band_ref, natural, sums)
-    for copy in copies:
-        copy.wait()
-    for s, product in enumerate(transposed_products(row_ref, tiles_refs, ids_refs, picked)):
+    for s, product in enumerate(transposed_products(row_ref, tiles_refs, ids_refs, picked, copies)):
         q = ids_refs[1][0, s]
         send_ref[q // 4, pl.ds(4 + q % 4, 1), :] += product
 
@@ -245,62 +256,72 @@
 
 def first_kernel(
     recv_ref, masked_ref, tiles_hbm, early_ref, rows_ref, cols_ref, count_ref,
-    send_ref, band_ref, row_ref, edge_ref, pick_ref, inverse_ref, moment_ref, late_ref,
-    picked, natural, sums, *sems,
+    send_ref, band_ref, row_ref, edge_ref, late_ref, picked, natural, sums, *sems,
 ):
     copies = [
-        pltpu.make_async_copy(tiles_hbm.at[4 + s], late_ref.at[s], sems[s]) for s in range(4)
+        pltpu.make_async_copy(tiles_hbm.at[EARLY + s], late_ref.at[s], sems[s])
+        for s in range(8 - EARLY)
     ]
     for copy in copies:
         copy.start()
     col = lax.axis_index("cols")
-    sub = lax.broadcasted_iota(jnp.int32, (8, 384), 0)
-    moment = jnp.zeros((8, 384), F32)
+    row_ref[...] = jnp.zeros((8, 8, 384), F32)
     for c in range(8):
-        both = recv_ref[c, 0:8, :]
-        vector = jnp.where(sub < 4, both, 0.0)
-        row_ref[c] = vector
-        moment = moment + vector * pltpu.roll(both, 4, 0)
-        block = [recv_ref[c, 8:16, :], recv_ref[c, 16:24, :]]
+        for j in range(3):
+            row_ref[c, 0:4, j * LANES : (j + 1) * LANES] = recv_ref[c, 4 * j : 4 * j + 4, :]
+    prev = (col + 7) % 8
+    ids = lane_ids(6)
+    for j in range(3):
+        part = recv_ref[prev, 12 + 6 * j : 18 + 6 * j, :]
+        for i in range(16):
+            edge_ref[j * 16 + i] = jnp.where(ids >= 120, right(part, 120 - i * 8), 0.0)
+    scratch = (picked, natural, sums)
+    send_frames(
+        row_ref, edge_ref, masked_ref, (early_ref, late_ref), (rows_ref, cols_ref, count_ref),
+        send_ref, band_ref, scratch, copies,
+    )
+
+
+def unpack(recv_ref, pick_ref, inverse_ref):
+    lane = lane_ids(1)
+    target = jnp.full((1, LANES), -1.0, F32)
+    for c in range(8):
+        target = jnp.where(lane // 8 == c, right(recv_ref[c, 39:40, :], 8 * c), target)
+    index = lax.broadcasted_iota(jnp.int32, (64, LANES), 0).astype(F32)
+    found = (index == jnp.broadcast_to(target, (64, LANES))).astype(F32)
+    pick_ref[...] = jnp.where(lax.broadcasted_iota(jnp.int32, (64, LANES), 1) < 64, found, 0.0)
+    low = lax.broadcasted_iota(jnp.int32, (8, LANES), 0) < 4
+    for c in range(8):
         parts = []
-        for d in range(4):
-            part = block[d // 2]
-            part = pltpu.roll(part, 4, 0) if d % 2 else part
-            parts.append(jnp.where(sub < 4, part, 0.0))
+        for g in range(12):
+            part = recv_ref[c, 40 + 8 * (g // 2) : 48 + 8 * (g // 2), :]
+            part = pltpu.roll(part, 4, 0) if g % 2 else part
+            parts.append(jnp.where(low, part, 0.0))
+        parts = [jnp.concatenate(parts[3 * d : 3 * d + 3], axis=1) for d in range(4)]
         parts += [left(parts[2], 256), left(parts[1], 320)]
         for d in range(6):
             inverse_ref[d, c] = parts[d]
-    moment_ref[0] = moment[:, 0:128] + moment[:, 128:256] + moment[:, 256:384]
-    prev = (col + 7) % 8
-    ids = lane_ids(6)
-    packed = recv_ref[prev, 24:32, :]
-    for j in range(3):
-        part = packed[0:6, j * LANES : (j + 1) * LANES]
-        for i in range(16):
-            edge_ref[j * 16 + i] = jnp.where(ids >= 120, right(part, 120 - i * 8), 0.0)
-    lane = lane_ids(1)
-    target = jnp.full((1, LANES), -1.0, F32)
+
+
+def row_image(recv_ref, pick_ref):
+    products = jnp.concatenate(
+        [recv_ref[:, 8 * j : 8 * j + 8, :].reshape(64, LANES) for j in range(3)], axis=1
+    )
+    image = jnp.dot(
+        pick_ref[:, 0:64], products, precision=lax.Precision.HIGHEST, preferred_element_type=F32
+    )
+    sub = lax.broadcasted_iota(jnp.int32, (8, LANES), 0)
+    rows = []
     for c in range(8):
-        at = lane - 16 * c
-        target = jnp.where((at >= 0) & (at < 8), right(recv_ref[c, 30:31, 0:LANES], 16 * c), target)
-        target = jnp.where((at >= 8) & (at < 12), (c * 8 + at - 8).astype(F32), target)
-        target = jnp.where(at == 12, float(((c + 7) % 8) * 8 + 3), target)
-    index = lax.broadcasted_iota(jnp.int32, (64, LANES), 0).astype(F32)
-    pick_ref[...] = (index == jnp.broadcast_to(target, (64, LANES))).astype(F32)
-    ids_refs = (rows_ref, cols_ref, count_ref)
-    scratch = (picked, natural, sums)
-    tiles_refs = (early_ref, late_ref)
-    send_frames(
-        row_ref, edge_ref, masked_ref, tiles_refs, ids_refs, send_ref, band_ref, scratch, copies
-    )
-
-
-def row_image(recv_ref, pick_ref):
-    received = recv_ref[...].reshape(LANES, 384)
-    image = jnp.dot(
-        pick_ref[...], received, precision=lax.Precision.HIGHEST, preferred_element_type=F32
-    )
-    return image.reshape(8, 8, 384)
+        one, two = recv_ref[c, 24:32, :], recv_ref[c, 32:40, :]
+        after = recv_ref[(c + 1) % 8, 32:40, :]
+        parts = [one, pltpu.roll(one, 4, 0), two]
+        onward = [pltpu.roll(after, 7 - j, 0) for j in range(3)]
+        parts = [
+            jnp.where(sub < 4, x, 0.0) + jnp.where(sub == 3, y, 0.0) for x, y in zip(parts, onward)
+        ]
+        rows.append(image[8 * c : 8 * c + 8] + jnp.concatenate(parts, axis=1))
+    return jnp.concatenate(rows, axis=0).reshape(8, 8, 384)
 
 
 def folded(x):
@@ -325,9 +346,26 @@
     return moments
 
 
+def second_kernel(
+    recv_ref, before_ref, edge_ref, masked_ref, early_ref, late_ref, rows_ref, cols_ref, count_ref,
+    send_ref, band_ref, row_ref, image_ref, moment_ref, pick_ref, inverse_ref, *scratch,
+):
+    unpack(recv_ref, pick_ref, inverse_ref)
+    total = recv_ref[0, 39:40, :]
+    for c in range(1, 8):
+        total = total + recv_ref[c, 39:40, :]
+    sub = lax.broadcasted_iota(jnp.int32, (8, LANES), 0)
+    lane = lax.broadcasted_iota(jnp.int32, (8, LANES), 1)
+    moment_ref[2] = jnp.where((sub == 0) & (lane == 8), jnp.broadcast_to(total, (8, LANES)), 0.0)
+    advance(recv_ref, pick_ref, inverse_ref, before_ref, row_ref, image_ref, moment_ref, scratch[0])
+    ids_refs = (rows_ref, cols_ref, count_ref)
+    tiles_refs = (early_ref, late_ref)
+    send_frames(row_ref, edge_ref, masked_ref, tiles_refs, ids_refs, send_ref, band_ref, scratch)
+
+
 def next_kernel(
-    recv_ref, pick_ref, inverse_ref, before_ref, edge_ref, masked_ref, early_ref, late_ref, rows_ref, cols_ref, count_ref,
-    send_ref, band_ref, row_ref, image_ref, moment_ref, *scratch,
+    recv_ref, before_ref, edge_ref, masked_ref, early_ref, late_ref, rows_ref, cols_ref, count_ref,
+    pick_ref, inverse_ref, send_ref, band_ref, row_ref, image_ref, moment_ref, *scratch,
 ):
     advance(recv_ref, pick_ref, inverse_ref, before_ref, row_ref, image_ref, moment_ref, scratch[0])
     ids_refs = (rows_ref, cols_ref, count_ref)
@@ -336,11 +374,11 @@
 
 
 def last_kernel(
-    recv_ref, pick_ref, inverse_ref, before_ref, edge_ref, masked_ref, early_ref, late_ref, rows_ref, cols_ref, count_ref,
-    m0_ref, m1_ref, m2_ref, send_ref, band_ref, row_ref, image_ref, *scratch,
+    recv_ref, before_ref, edge_ref, masked_ref, early_ref, late_ref, rows_ref, cols_ref, count_ref,
+    pick_ref, inverse_ref, m1_ref, m2_ref, send_ref, band_ref, row_ref, image_ref, *scratch,
 ):
     moments = advance(recv_ref, pick_ref, inverse_ref, before_ref, row_ref, image_ref, None, scratch[0])
-    known = [m0_ref[0], m1_ref[0], m1_ref[1], m2_ref[0], m2_ref[1]] + moments
+    known = [m1_ref[2], m1_ref[0], m1_ref[1], m2_ref[0], m2_ref[1]] + moments
     ids_refs = (rows_ref, cols_ref, count_ref)
     tiles_refs = (early_ref, late_ref)
     send_last(row_ref, edge_ref, masked_ref, tiles_refs, ids_refs, known, send_ref, band_ref, scratch)
@@ -370,25 +408,37 @@
         piece = piece_of(s) * (s < count).astype(F32)
         for j in range(3):
             rows = pl.ds(j * LANES, LANES)
-            tile = tiles_refs[s // 4]
-            part = tile[s % 4, rows, 0:LANES] * piece[:, 0:LANES]
-            part = part + tile[s % 4, rows, LANES : 2 * LANES] * piece[:, LANES : 2 * LANES]
-            part = part + tile[s % 4, rows, 2 * LANES : 384] * piece[:, 2 * LANES : 384]
-            pack[s : s + 1, j * LANES : (j + 1) * LANES] = jnp.sum(part.T, axis=0, keepdims=True)
-
-
-def cols_kernel(recv_ref, early_ref, late_ref, row_ref, edge_ref, band_ref, cols_ref, count_ref, send_ref, pack):
+            tile = slot_of(tiles_refs, s)
+            part = tile[rows, 0:LANES] * piece[:, 0:LANES]
+            part = part + tile[rows, LANES : 2 * LANES] * piece[:, LANES : 2 * LANES]
+            part = part + tile[rows, 2 * LANES : 384] * piece[:, 2 * LANES : 384]
+            pack[8 * j + s : 8 * j + s + 1, :] = jnp.sum(part.T, axis=0, keepdims=True)
+
+
+def cols_kernel(recv_ref, early_ref, late_ref, row_ref, edge_ref, band_ref, cols_ref, count_ref, *rest):
+    extra_ref, rows_ref = rest[:2] if len(rest) == 4 else (None, None)
+    send_ref, pack = rest[-2:]
     frame = lax.axis_index("frames")
     col = lax.axis_index("cols")
     total = recv_ref[0]
     for f in range(1, 32):
         total = total + recv_ref[f]
-    sub = lax.broadcasted_iota(jnp.int32, (8, 384), 0)
-    pack[8:16, :] = jnp.where(sub < 4, pltpu.roll(total, 4, 0) + band_ref[...], 0.0)
+    terms = pltpu.roll(total, 4, 0) + band_ref[...]
     here = (col > 0).astype(F32)
     there = ((col == 0) & (frame < 31)).astype(F32)
     start = row_ref[col][0:1] * here + recv_ref[jnp.minimum(frame + 1, 31)][0:1] * there
-    pack[12:13, :] = onward_terms(edge_ref, start)
+    onward = onward_terms(edge_ref, start)
+    for j in range(3):
+        lanes = slice(j * LANES, (j + 1) * LANES)
+        pack[24 + 4 * j : 28 + 4 * j, :] = terms[0:4, lanes]
+        pack[36 + j : 37 + j, :] = onward[:, lanes]
+    misc = jnp.zeros((1, LANES), F32)
+    if extra_ref is not None:
+        misc = extra_ref[48:49, :]
+        for s in range(8):
+            r = rows_ref[0, s]
+            misc = jnp.where(lane_ids(1) == s, ((r // 4) * 8 + r % 4).astype(F32), misc)
+    pack[39:40, :] = misc
 
     def piece_of(s):
         q = cols_ref[0, s]
@@ -397,11 +447,14 @@
     tile_products((early_ref, late_ref), piece_of, count_ref[0, 0], pack)
     whole = pack[...]
     for c in range(8):
-        send_ref[c] = whole
+        send_ref[c, 0:40, :] = whole
+        if extra_ref is not None:
+            send_ref[c, 40:88, :] = extra_ref[0:48, :]
 
 
 def finish_kernel(
-    recv_ref, early_ref, late_ref, row_ref, edge_ref, band_ref, cols_ref, count_ref, send_ref, known_ref, pack
+    recv_ref, early_ref, late_ref, row_ref, edge_ref, band_ref, cols_ref, count_ref, rows_ref,
+    send_ref, known_ref, mine_ref, pack,
 ):
     frame = lax.axis_index("frames")
     col = lax.axis_index("cols")
@@ -442,13 +495,12 @@
 
     sub = lax.broadcasted_iota(jnp.int32, (8, 256), 0)
     mine = dot((jnp.broadcast_to(tags, (8, 256)) == (4 * frame + sub % 4).astype(F32)).astype(F32), products)
-    sub = lax.broadcasted_iota(jnp.int32, (8, 384), 0)
-    pack[8:16, :] = jnp.where(sub < 4, mine + band_ref[...], 0.0)
+    mine_ref[...] = mine + band_ref[...]
     before = jnp.maximum(frame - 1, 0)
     for j in range(3):
         lanes = slice(j * LANES, (j + 1) * LANES)
         edge = recv_ref[before, 36 + j : 37 + j, :] * (frame > 0).astype(F32)
-        pack[8:9, lanes] = pack[8:9, lanes] + edge
+        mine_ref[0:1, lanes] = mine_ref[0:1, lanes] + edge
     here = (col > 0).astype(F32)
     there = ((col == 0) & (frame < 31)).astype(F32)
     after = jnp.minimum(frame + 1, 31)
@@ -456,35 +508,36 @@
     def row_of(f, i):
         return jnp.concatenate([recv_ref[f, pl.ds(24 + 4 * j + i, 1), :] for j in range(3)], axis=1)
 
-    pack[12:13, :] = onward_terms(edge_ref, row_ref[col][0:1] * here + row_of(after, 0) * there)
-    pack[13:14, 0:LANES] = quad
+    onward = onward_terms(edge_ref, row_ref[col][0:1] * here + row_of(after, 0) * there)
+    empty = jnp.where(lax.broadcasted_iota(jnp.int32, (16, LANES), 0) == 12, quad, 0.0)
+    for c in range(8):
+        send_ref[c] = empty
+    for j in range(3):
+        send_ref[(col + 7) % 8, 4 * j + 3 : 4 * j + 4, :] = onward[:, j * LANES : (j + 1) * LANES]
 
     def piece_of(s):
         q = cols_ref[0, s]
         return row_of(q // 4, q % 4)
 
     tile_products((early_ref, late_ref), piece_of, count_ref[0, 0], pack)
-    whole = pack[...]
-    for c in range(8):
-        send_ref[c] = whole
+    for s in range(8):
+        r = rows_ref[0, s]
+        for j in range(3):
+            send_ref[r // 4, pl.ds(4 * j + r % 4, 1), :] += pack[8 * j + s : 8 * j + s + 1, :]
 
 
 def end_kernel(
-    recv_ref, pick_ref, known_ref, right_ref, v0, v1, v2, v3, w0, w1, w2, solution_ref, residual_ref, scratch
+    recv_ref, mine_ref, known_ref, right_ref, v0, v1, v2, v3, w0, w1, w2, solution_ref, residual_ref, scratch
 ):
     col = lax.axis_index("cols")
-    last = jnp.dot(
-        pick_ref[pl.ds(pl.multiple_of(col * 8, 8), 8), :],
-        recv_ref[...].reshape(LANES, 384),
-        precision=lax.Precision.HIGHEST,
-        preferred_element_type=F32,
-    )
-    total = recv_ref[0, 13:14, 0:LANES]
+    total = recv_ref[0]
     for c in range(1, 8):
-        total = total + recv_ref[c, 13:14, 0:LANES]
+        total = total + recv_ref[c]
+    parts = [total[0:8], pltpu.roll(total[0:8], 4, 0), total[8:16]]
+    last = jnp.concatenate(parts, axis=1) + mine_ref[...]
     known = known_ref[0:1, :]
     mu = [jnp.broadcast_to(known[:, 8 + i : 9 + i], (1, LANES)) for i in range(7)]
-    mu.append(jnp.broadcast_to(jnp.sum(total, axis=1, keepdims=True), (1, LANES)))
+    mu.append(jnp.broadcast_to(jnp.sum(total[12:13], axis=1, keepdims=True), (1, LANES)))
     zero = jnp.zeros((1, LANES), F32)
     one = zero + 1.0
 
@@ -561,64 +614,81 @@
     stored = in_hbm(tiles.reshape(tiles.shape[2:]))
     inputs = (right_side, diag_blocks, jnp.transpose(band_blocks, (1, 2, 0, 3)), reach.reshape(1, -1))
     inputs += (tile_rows.reshape(1, 8), tile_cols.reshape(1, 8))
-    send, masked, *ids, early = call(
+    send, masked, extra, *ids, early = call(
         start_kernel,
         [HB] * 7,
-        [shape(8, 32, 384), shape(48, 6, 256)]
+        [shape(8, 32, LANES), shape(48, 6, 256), shape(56, LANES)]
         + [shape(1, 8, kind=jnp.int32)] * 2
-        + [shape(4, 384, 384)],
-        [(6, 256), (6, 6, 256), (6, 6, 8, 256), pltpu.VMEM((1, 256), jnp.int32), (32, 384)]
-        + [sem] * 10,
+        + [shape(EARLY, 384, 384)],
+        [(6, 256), (6, 6, 256), (6, 6, 8, 256), pltpu.VMEM((1, 256), jnp.int32), (8, 384), (32, LANES)]
+        + [sem] * (6 + EARLY),
         "start",
     )(*[in_hbm(x) for x in inputs], stored)
     ids.append(tile_count)
     recv = exchange(send, "cols")
     frames_out = [shape(32, 8, 384), shape(8, 384), shape(8, 8, 384)]
     scratch = [(LANES, 384), (8, 256), (8, 256)]
-    send, band, row, edges, pick, inverse, moment, late = call(
+    send, band, row, edges, late = call(
         first_kernel,
         [VM] * 2 + [HB, VM] + [SM] * 3,
-        frames_out
-        + [shape(48, 6, LANES), shape(64, LANES), shape(6, 8, 8, 384), shape(1, 8, LANES)]
-        + [shape(4, 384, 384)],
-        scratch + [sem] * 4,
+        frames_out + [shape(48, 6, LANES), shape(8 - EARLY, 384, 384)],
+        scratch + [sem] * (8 - EARLY),
         "first",
     )(recv, masked, stored, early, *ids)
-    vectors, images, moments = [row], [], [moment]
+    vectors, images, moments = [row], [], []
     for it in range(ITERS - 1):
         recv = exchange(send, "frames")
         (send,) = call(
-            cols_kernel, [VM] * 6 + [SM] * 2, [shape(8, 16, 384)], [(16, 384)], "products"
-        )(recv, early, late, row, edges, band, *ids[1:])
+            cols_kernel,
+            [VM] * 6 + [SM] * 2 + ([VM, SM] if it == 0 else []),
+            [shape(8, 88 if it == 0 else 40, LANES)],
+            [(40, LANES)],
+            "products",
+        )(recv, early, late, row, edges, band, *ids[1:], *((extra, ids[0]) if it == 0 else ()))
         recv = exchange(send, "cols")
-        given = (recv, pick, inverse, row, edges, masked, early, late, *ids)
-        if it + 2 < ITERS:
+        given = (recv, row, edges, masked, early, late, *ids)
+        specs = [VM] * 6 + [SM] * 3
+        if it == 0:
+            send, band, row, image, moment, pick, inverse = call(
+                second_kernel,
+                specs,
+                frames_out
+                + [shape(8, 384), shape(3, 8, LANES), shape(64, LANES), shape(6, 8, 8, 384)],
+                scratch,
+                "second",
+            )(*given)
+            moments.append(moment)
+        elif it + 2 < ITERS:
             send, band, row, image, moment = call(
                 next_kernel,
-                [VM] * 8 + [SM] * 3,
+                specs + [VM] * 2,
                 frames_out + [shape(8, 384), shape(2, 8, LANES)],
                 scratch,
                 "next",
-            )(*given)
+            )(*given, pick, inverse)
             moments.append(moment)
         else:
             send, band, row, image = call(
                 last_kernel,
-                [VM] * 8 + [SM] * 3 + [VM] * 3,
+                specs + [VM] * 4,
                 [shape(32, 40, LANES), shape(8, 384), shape(8, 8, 384), shape(8, 384)],
                 scratch + [(40, LANES)],
                 "last",
-            )(*given, *moments)
+            )(*given, pick, inverse, *moments)
         vectors.append(row)
         images.append(image)
     recv = exchange(send, "frames")
-    send, known = call(
-        finish_kernel, [VM] * 6 + [SM] * 2, [shape(8, 16, 384), shape(8, LANES)], [(16, 384)], "finish"
-    )(recv, early, late, row, edges, band, *ids[1:])
+    send, known, mine = call(
+        finish_kernel,
+        [VM] * 6 + [SM] * 3,
+        [shape(8, 16, LANES), shape(8, LANES), shape(8, 384)],
+        [(24, LANES)],
+        "finish",
+    )(recv, early, late, row, edges, band, *ids[1:], ids[0])
     recv = exchange(send, "cols")
     return tuple(
         call(end_kernel, [VM] * 11, [shape(6, 256), shape(6, 256)], [(8, 256)], "end")(
-            recv, pick, known, right_side, *vectors, *images
+            recv, mine, known, right_side, *vectors, *images
         )
     )
 

time: 157 us -> 155 us (0.987)
  waiting for transfers between devices: 7.07 us -> 4.62 us
    all_to_all x1, waiting for transfers between devices: 7.07 us -> 4.62 us  [exchange(): return lax.all_to_all(x, axis, 0, 0, tiled=True)]
where the time goes in v2:
time: 155 us; the launch traced here: 154 us
  blocking collectives  125 us (81%)
  Pallas kernels  16.9 us (11%)
  starting transfers between devices  6.48 us (4%)
  waiting for transfers between devices  4.62 us (3%)
    all_to_all x8, blocking collectives, exchange(): return lax.all_to_all(x, axis, 0, 0, tiled=True)  125 us
    all_to_all x1, starting transfers between devices, exchange(): return lax.all_to_all(x, axis, 0, 0, tiled=True)  6.48 us
    all_to_all x1, waiting for transfers between devices, exchange(): return lax.all_to_all(x, axis, 0, 0, tiled=True)  4.62 us
    pallas_call x3, Pallas kernels, per_device(): call(cols_kernel, [VM] * 6 + [SM] * 2 + ([VM, SM] if it == 0 else []), [s...  3.77 us
  transfers between devices with their start and end apart: 1, of which 1 were waited for; matrix products, arithmetic and copies ran while one was open for 0% of the time, Pallas kernels for 0%

profile of v2, /device:TPU:1, one launch (start us, length us, event | category | flops | bytes accessed | tf_op | source)
XLA Modules:
  0.0 154.2 jit_solution(5806826310296336886)
XLA Ops:
  0.6 2.3 %start.1 = (f32[8,32,128]{2,1,0:T(8,128)}, f32[48,6,256]{2,1,0:T(8,128)S(1)}, f32[56,128]{1,0:T(8,128)S(1)}, s32[1,8]{1,0:T(1,128)S(1)}, s32[1,8]{1,0:T(1,128)S(1)}, /*index=5*/f32[3,384,384]{2,1,0:T(8,128)S(1)}) custom-call(f32[6,256]{1,0:T(8,128)} %right_ref.1, f32[6,6,256]{2,1,0:T(8,128)} %diag_hbm.1, f32[6,6,8,256]{3,2,1,0:T(8,128)} %bitcast.7, ...), custom_call_target="tpu_custom_call" | custom-call | tf_op jit(solution)/shard_map/start/pallas_call | solution.py:617
  3.0 6.5 %all-to-all-start = ((f32[8,32,128]{2,1,0:T(8,128)}), f32[8,32,128]{2,1,0:T(8,128)S(1)}, u32[]{:S(2)}, u32[]{:S(2)}) async-start(f32[8,32,128]{2,1,0:T(8,128)} %get-tuple-element.32), calls=%async_computation | async-start | bytes 262144 | tf_op jit(solution)/shard_map/all_to_all | solution.py:608
  10.1 4.6 %all-to-all-done.recv_ref = f32[8,32,128]{2,1,0:T(8,128)S(1)} async-done(((f32[8,32,128]{2,1,0:T(8,128)}), f32[8,32,128]{2,1,0:T(8,128)S(1)}, u32[]{:S(2)}, u32[]{:S(2)}) %all-to-all-start) | async-done | bytes 131104 | tf_op jit(solution)/shard_map/all_to_all | solution.py:608
  14.7 2.9 %first.1 = (f32[32,8,384]{2,1,0:T(8,128)S(1)}, f32[8,384]{1,0:T(8,128)S(1)}, f32[8,8,384]{2,1,0:T(8,128)S(1)}, f32[48,6,128]{2,1,0:T(8,128)S(1)}, f32[5,384,384]{2,1,0:T(8,128)S(1)}) custom-call(f32[8,32,128]{2,1,0:T(8,128)S(1)} %all-to-all-done.recv_ref, f32[48,6,256]{2,1,0:T(8,128)S(1)} %get-tuple-element.33.masked_ref, f32[8,384,384]{2,1,0:T(8,128)} %bitcast.6, ...), custom_call_target="tpu_custom_call" | custom-call | tf_op jit(solution)/shard_map/first/pallas_call | solution.py:631
  17.7 24.2 %all_to_all.45.recv_ref = f32[32,8,384]{2,1,0:T(8,128)S(1)} all-to-all(f32[32,8,384]{2,1,0:T(8,128)S(1)} %get-tuple-element.37), channel_id=1, replica_groups=mesh['frames'=32,'cols'=8] {'frames'}, dimensions={0} | all-to-all | bytes 786432 | tf_op jit(solution)/shard_map/all_to_all | solution.py:608
  41.8 1.3 products.3
  43.1 12.6 %all_to_all.46.recv_ref = f32[8,88,128]{2,1,0:T(8,128)S(1)} all-to-all(f32[8,88,128]{2,1,0:T(8,128)S(1)} %products.3), channel_id=1, replica_groups=mesh['frames'=32,'cols'=8] {'cols'}, dimensions={0} | all-to-all | bytes 720896 | tf_op jit(solution)/shard_map/all_to_all | solution.py:608
  55.7 1.8 %second.1 = (f32[32,8,384]{2,1,0:T(8,128)S(1)}, f32[8,384]{1,0:T(8,128)S(1)}, f32[8,8,384]{2,1,0:T(8,128)S(1)}, f32[8,384]{1,0:T(8,128)S(1)}, f32[3,8,128]{2,1,0...) custom-call(f32[8,88,128]{2,1,0:T(8,128)S(1)} %all_to_all.46.recv_ref, ...), custom_call_target="tpu_custom_call" | custom-call | tf_op jit(solution)/shard_map/second/pallas_call | solution.py:652
  57.5 17.6 %all_to_all.47.recv_ref = f32[32,8,384]{2,1,0:T(8,128)S(1)} all-to-all(f32[32,8,384]{2,1,0:T(8,128)S(1)} %get-tuple-element.43), channel_id=1, replica_groups=mesh['frames'=32,'cols'=8] {'frames'}, dimensions={0} | all-to-all | bytes 786432 | tf_op jit(solution)/shard_map/all_to_all | solution.py:608
  75.1 1.3 products.4
  76.4 10.4 %all_to_all.48.recv_ref = f32[8,40,128]{2,1,0:T(8,128)S(1)} all-to-all(f32[8,40,128]{2,1,0:T(8,128)S(1)} %products.4), channel_id=1, replica_groups=mesh['frames'=32,'cols'=8] {'cols'}, dimensions={0} | all-to-all | bytes 327680 | tf_op jit(solution)/shard_map/all_to_all | solution.py:608
  86.8 1.8 %next.1 = (f32[32,8,384]{2,1,0:T(8,128)S(1)}, f32[8,384]{1,0:T(8,128)S(1)}, f32[8,8,384]{2,1,0:T(8,128)S(1)}, f32[8,384]{1,0:T(8,128)S(1)}, f32[2,8,128]{2,1,0:T(8,128)S(1)}) custom-call(f32[8,40,128]{2,1,0:T(8,128)S(1)} %all_to_all.48.recv_ref, f32[8,8,384]{2,1,0:T(8,128)S(1)} %get-tuple-element.44.row_ref.before_ref.v1, ...), custom_call_target="tpu_custom_call" | custom-call | tf_op jit(solution)/shard_map/next/pallas_call | solution.py:662
  88.5 17.5 %all_to_all.49.recv_ref = f32[32,8,384]{2,1,0:T(8,128)S(1)} all-to-all(f32[32,8,384]{2,1,0:T(8,128)S(1)} %get-tuple-element.48), channel_id=1, replica_groups=mesh['frames'=32,'cols'=8] {'frames'}, dimensions={0} | all-to-all | bytes 786432 | tf_op jit(solution)/shard_map/all_to_all | solution.py:608
  106.0 1.3 products.5
  107.3 10.5 %all_to_all.50.recv_ref = f32[8,40,128]{2,1,0:T(8,128)S(1)} all-to-all(f32[8,40,128]{2,1,0:T(8,128)S(1)} %products.5), channel_id=1, replica_groups=mesh['frames'=32,'cols'=8] {'cols'}, dimensions={0} | all-to-all | bytes 327680 | tf_op jit(solution)/shard_map/all_to_all | solution.py:608
  117.8 1.8 %last.1 = (f32[32,40,128]{2,1,0:T(8,128)S(1)}, f32[8,384]{1,0:T(8,128)S(1)}, f32[8,8,384]{2,1,0:T(8,128)S(1)}, f32[8,384]{1,0:T(8,128)S(1)}) custom-call(f32[8,40,128]{2,1,0:T(8,128)S(1)} %all_to_all.50.recv_ref, f32[8,8,384]{2,1,0:T(8,128)S(1)} %get-tuple-element.49.row_ref.before_ref.v2, f32[48,6,128]{2,1,0:T(8,128)S(1)} %get-tuple-element.40.edge_ref, ...), custom_call_target="tpu_custom_call" | custom-call | tf_op jit(solution)/shard_map/last/pallas_call | solution.py:671
  119.6 22.2 %all_to_all.51.recv_ref = f32[32,40,128]{2,1,0:T(8,128)S(1)} all-to-all(f32[32,40,128]{2,1,0:T(8,128)S(1)} %get-tuple-element.53), channel_id=1, replica_groups=mesh['frames'=32,'cols'=8] {'frames'}, dimensions={0} | all-to-all | bytes 1310720 | tf_op jit(solution)/shard_map/all_to_all | solution.py:608
  141.8 0.0 copy-start
  141.8 1.6 %finish.1 = (f32[8,16,128]{2,1,0:T(8,128)S(1)}, f32[8,128]{1,0:T(8,128)S(1)}, f32[8,384]{1,0:T(8,128)S(1)}) custom-call(f32[32,40,128]{2,1,0:T(8,128)S(1)} %all_to_all.51.recv_ref, f32[3,384,384]{2,1,0:T(8,128)S(1)} %get-tuple-element.34.early_ref, f32[5,384,384]{2,1,0:T(8,128)S(1)} %get-tuple-element.38.late_ref, ...), custom_call_target="tpu_custom_call" | custom-call | tf_op jit(solution)/shard_map/finish/pallas_call | solution.py:681
  143.4 9.9 %all_to_all.52.recv_ref = f32[8,16,128]{2,1,0:T(8,128)S(1)} all-to-all(f32[8,16,128]{2,1,0:T(8,128)S(1)} %get-tuple-element.56), channel_id=1, replica_groups=mesh['frames'=32,'cols'=8] {'cols'}, dimensions={0} | all-to-all | bytes 131072 | tf_op jit(solution)/shard_map/all_to_all | solution.py:608
  153.3 0.0 copy-done
  153.3 0.9 end.1
Async XLA Ops:
  3.0 11.8 %all-to-all-start = ((f32[8,32,128]{2,1,0:T(8,128)}), f32[8,32,128]{2,1,0:T(8,128)S(1)}, u32[]{:S(2)}, u32[]{:S(2)}) async-start(f32[8,32,128]{2,1,0:T(8,128)} %get-tuple-element.32), calls=%async_computation | async-start | bytes 262144 | tf_op jit(solution)/shard_map/all_to_all | solution.py:608
  141.8 11.5 %copy-start = (f32[6,256]{1,0:T(8,128)S(1)}, f32[6,256]{1,0:T(8,128)}, u32[]{:S(2)}) copy-start(f32[6,256]{1,0:T(8,128)} %right_ref.1) | copy-start | bytes 18436

commit v3 on v2

--- a/solution.py
+++ b/solution.py
@@ -11,7 +11,7 @@
 LANES = 128
 F32 = jnp.float32
 ROWS = ("frames", "cols")
-EARLY = 3
+EARLY = 4
 
 
 def lane_ids(rows):
@@ -61,8 +61,8 @@
 
 
 def start_kernel(
-    right_hbm, diag_hbm, band_hbm, reach_hbm, rows_hbm, cols_hbm, tiles_hbm,
-    send_ref, masked_ref, extra_ref, rows_ref, cols_ref, tiles_ref,
+    right_hbm, diag_hbm, band_hbm, reach_hbm, rows_hbm, cols_hbm,
+    send_ref, masked_ref, extra_ref, rows_ref, cols_ref,
     right_ref, diag_ref, band_ref, reach_ref, pack, lines, *sems,
 ):
     copies = [
@@ -72,9 +72,6 @@
             (diag_ref, right_ref, reach_ref, band_ref, rows_ref, cols_ref),
             sems,
         )
-    ]
-    copies += [
-        pltpu.make_async_copy(tiles_hbm.at[s], tiles_ref.at[s], sems[6 + s]) for s in range(EARLY)
     ]
     for copy in copies:
         copy.start()
@@ -129,7 +126,13 @@
     whole = lines[...]
     for c in range(8):
         send_ref[c] = whole
-    for copy in copies[6:]:
+
+
+def load_kernel(tiles_hbm, tiles_ref, *sems):
+    copies = [pltpu.make_async_copy(tiles_hbm.at[s], tiles_ref.at[s], sems[s]) for s in range(EARLY)]
+    for copy in copies:
+        copy.start()
+    for copy in copies:
         copy.wait()
 
 
@@ -154,27 +157,61 @@
     )
 
 
+def bfloat16_parts(x):
+    high = x.astype(jnp.bfloat16)
+    rest = x - high.astype(F32)
+    middle = rest.astype(jnp.bfloat16)
+    return high, middle, (rest - middle.astype(F32)).astype(jnp.bfloat16)
+
+
+def select_sum(pick, x):
+    pick = pick.astype(jnp.bfloat16)
+    high, middle, low = [
+        jnp.dot(pick, part, preferred_element_type=F32) for part in bfloat16_parts(x)
+    ]
+    return low + middle + high
+
+
 def slot_of(tiles_refs, s):
     return tiles_refs[0].at[s] if s < EARLY else tiles_refs[1].at[s - EARLY]
 
 
-def transposed_products(row_ref, tiles_refs, ids_refs, picked, copies=()):
+def transposed_products(row_ref, tiles_refs, ids_refs, picked, spread, copies=()):
     rows_ref, _, count_ref = ids_refs
     count = count_ref[0, 0]
     picked[...] = jnp.zeros((LANES, 384), F32)
     for s in range(8):
         r = rows_ref[0, s]
         picked[s : s + 1, :] = row_ref[r // 4, pl.ds(r % 4, 1), :]
+    for i, part in enumerate(bfloat16_parts(picked[4:8, :])):
+        picked[8 + 4 * i : 12 + 4 * i, :] = part.astype(F32)
     upright = [picked[:, j * LANES : (j + 1) * LANES].T for j in range(3)]
+    at = lax.broadcasted_iota(jnp.int32, (LANES, 512), 0)
+    to = lax.broadcasted_iota(jnp.int32, (LANES, 512), 1)
+    ones = ((at >= 8) & (at < 20) & (at % 4 == to // LANES)).astype(jnp.bfloat16)
+    for j in range(3):
+        spread[j * LANES : (j + 1) * LANES, :] = jnp.dot(
+            upright[j].astype(jnp.bfloat16), ones, preferred_element_type=F32
+        )
     products = []
     for s in range(8):
         if copies and s >= EARLY:
             copies[s - EARLY].wait()
-        total = jnp.zeros((1, 384), F32)
-        for j in range(3):
-            column = upright[j][:, s : s + 1]
-            tile = slot_of(tiles_refs, s)[j * LANES : (j + 1) * LANES, :]
-            total = total + jnp.sum(tile * column, axis=0, keepdims=True)
+        tile = slot_of(tiles_refs, s)
+        sums = [[None] * 3, [None] * 3]
+        for i in range(48):
+            if s < 4:
+                column = upright[i // 16][8 * (i % 16) : 8 * (i % 16) + 8, s : s + 1]
+                column = jnp.broadcast_to(column, (8, LANES))
+            else:
+                column = spread[8 * i : 8 * i + 8, (s - 4) * LANES : (s - 3) * LANES]
+            for j in range(3):
+                part = tile[8 * i : 8 * i + 8, j * LANES : (j + 1) * LANES] * column
+                before = sums[i % 2][j]
+                sums[i % 2][j] = part if before is None else before + part
+        total = jnp.concatenate(
+            [jnp.sum(x + y, axis=0, keepdims=True) for x, y in zip(*sums)], axis=1
+        )
         products.append(total * (s < count).astype(F32))
     return products
 
@@ -210,7 +247,7 @@
 
 
 def send_frames(row_ref, edge_ref, masked_ref, tiles_refs, ids_refs, send_ref, band_ref, scratch, copies=()):
-    picked, natural, sums = scratch
+    picked, natural, sums, spread = scratch
     col = lax.axis_index("cols")
     sub = lax.broadcasted_iota(jnp.int32, (8, 384), 0)
     chunk = jnp.where(sub < 4, row_ref[col], 0.0)
@@ -219,18 +256,18 @@
     mine, onward = edge_terms(row_ref, edge_ref)
     send_ref[jnp.minimum(lax.axis_index("frames") + 1, 31), 4:5, :] = onward
     band_terms(row_ref, masked_ref, mine, band_ref, natural, sums)
-    for s, product in enumerate(transposed_products(row_ref, tiles_refs, ids_refs, picked, copies)):
+    for s, product in enumerate(transposed_products(row_ref, tiles_refs, ids_refs, picked, spread, copies)):
         q = ids_refs[1][0, s]
         send_ref[q // 4, pl.ds(4 + q % 4, 1), :] += product
 
 
 def send_last(row_ref, edge_ref, masked_ref, tiles_refs, ids_refs, known, send_ref, band_ref, scratch):
-    picked, natural, sums, pack = scratch
+    picked, natural, sums, spread, pack = scratch
     col = lax.axis_index("cols")
     mine, onward = edge_terms(row_ref, edge_ref)
     band_terms(row_ref, masked_ref, mine, band_ref, natural, sums)
     own = row_ref[col]
-    products = transposed_products(row_ref, tiles_refs, ids_refs, picked)
+    products = transposed_products(row_ref, tiles_refs, ids_refs, picked, spread)
     for j in range(3):
         lanes = slice(j * LANES, (j + 1) * LANES)
         for s in range(8):
@@ -256,7 +293,7 @@
 
 def first_kernel(
     recv_ref, masked_ref, tiles_hbm, early_ref, rows_ref, cols_ref, count_ref,
-    send_ref, band_ref, row_ref, edge_ref, late_ref, picked, natural, sums, *sems,
+    send_ref, band_ref, row_ref, edge_ref, late_ref, picked, natural, sums, spread, *sems,
 ):
     copies = [
         pltpu.make_async_copy(tiles_hbm.at[EARLY + s], late_ref.at[s], sems[s])
@@ -275,7 +312,7 @@
         part = recv_ref[prev, 12 + 6 * j : 18 + 6 * j, :]
         for i in range(16):
             edge_ref[j * 16 + i] = jnp.where(ids >= 120, right(part, 120 - i * 8), 0.0)
-    scratch = (picked, natural, sums)
+    scratch = (picked, natural, sums, spread)
     send_frames(
         row_ref, edge_ref, masked_ref, (early_ref, late_ref), (rows_ref, cols_ref, count_ref),
         send_ref, band_ref, scratch, copies,
@@ -307,9 +344,7 @@
     products = jnp.concatenate(
         [recv_ref[:, 8 * j : 8 * j + 8, :].reshape(64, LANES) for j in range(3)], axis=1
     )
-    image = jnp.dot(
-        pick_ref[:, 0:64], products, precision=lax.Precision.HIGHEST, preferred_element_type=F32
-    )
+    image = select_sum(pick_ref[:, 0:64], products)
     sub = lax.broadcasted_iota(jnp.int32, (8, LANES), 0)
     rows = []
     for c in range(8):
@@ -454,7 +489,7 @@
 
 def finish_kernel(
     recv_ref, early_ref, late_ref, row_ref, edge_ref, band_ref, cols_ref, count_ref, rows_ref,
-    send_ref, known_ref, mine_ref, pack,
+    send_ref, known_ref, mine_ref, pack, columns,
 ):
     frame = lax.axis_index("frames")
     col = lax.axis_index("cols")
@@ -475,12 +510,10 @@
         [recv_ref[:, 8 * j : 8 * j + 8, :].reshape(256, LANES) for j in range(3)], axis=1
     )
 
-    def dot(a, b):
-        return jnp.dot(a, b, precision=lax.Precision.HIGHEST, preferred_element_type=F32)
-
     at = lax.broadcasted_iota(jnp.int32, (256, 256), 0)
     wanted = ((at // 8) * 4 + at % 4).astype(F32)
-    sums = dot((wanted == jnp.broadcast_to(tags, (256, 256))).astype(F32), products)
+    sums = select_sum((wanted == jnp.broadcast_to(tags, (256, 256))).astype(F32), products)
+    columns[...] = sums
     low = lax.broadcasted_iota(jnp.int32, (8, LANES), 0) < 4
     quad = jnp.zeros((8, LANES), F32)
     for f in range(32):
@@ -493,8 +526,7 @@
             quad = quad + recv_ref[f, 36 + j : 37 + j, :] * recv_ref[f + 1, 24 + 4 * j : 25 + 4 * j, :]
     quad = quad + quad + jnp.where(lane == 15, total, 0.0)
 
-    sub = lax.broadcasted_iota(jnp.int32, (8, 256), 0)
-    mine = dot((jnp.broadcast_to(tags, (8, 256)) == (4 * frame + sub % 4).astype(F32)).astype(F32), products)
+    mine = columns[pl.ds(pl.multiple_of(frame * 8, 8), 8), :]
     mine_ref[...] = mine + band_ref[...]
     before = jnp.maximum(frame - 1, 0)
     for j in range(3):
@@ -614,20 +646,20 @@
     stored = in_hbm(tiles.reshape(tiles.shape[2:]))
     inputs = (right_side, diag_blocks, jnp.transpose(band_blocks, (1, 2, 0, 3)), reach.reshape(1, -1))
     inputs += (tile_rows.reshape(1, 8), tile_cols.reshape(1, 8))
-    send, masked, extra, *ids, early = call(
+    send, masked, extra, *ids = call(
         start_kernel,
-        [HB] * 7,
+        [HB] * 6,
         [shape(8, 32, LANES), shape(48, 6, 256), shape(56, LANES)]
-        + [shape(1, 8, kind=jnp.int32)] * 2
-        + [shape(EARLY, 384, 384)],
+        + [shape(1, 8, kind=jnp.int32)] * 2,
         [(6, 256), (6, 6, 256), (6, 6, 8, 256), pltpu.VMEM((1, 256), jnp.int32), (8, 384), (32, LANES)]
-        + [sem] * (6 + EARLY),
+        + [sem] * 6,
         "start",
-    )(*[in_hbm(x) for x in inputs], stored)
+    )(*[in_hbm(x) for x in inputs])
     ids.append(tile_count)
     recv = exchange(send, "cols")
+    (early,) = call(load_kernel, [HB], [shape(EARLY, 384, 384)], [sem] * EARLY, "load")(stored)
     frames_out = [shape(32, 8, 384), shape(8, 384), shape(8, 8, 384)]
-    scratch = [(LANES, 384), (8, 256), (8, 256)]
+    scratch = [(LANES, 384), (8, 256), (8, 256), (384, 512)]
     send, band, row, edges, late = call(
         first_kernel,
         [VM] * 2 + [HB, VM] + [SM] * 3,
@@ -682,7 +714,7 @@
         finish_kernel,
         [VM] * 6 + [SM] * 3,
         [shape(8, 16, LANES), shape(8, LANES), shape(8, 384)],
-        [(24, LANES)],
+        [(24, LANES), (256, 384)],
         "finish",
     )(recv, early, late, row, edges, band, *ids[1:], ids[0])
     recv = exchange(send, "cols")

time: 155 us -> 153 us (0.987)
  waiting for transfers between devices: 4.62 us -> 2.97 us
    all_to_all x1, waiting for transfers between devices: 4.62 us -> 2.97 us  [exchange(): return lax.all_to_all(x, axis, 0, 0, tiled=True)]
    pallas_call x1 -> x2, Pallas kernels: 2.34 us -> 3.6 us  [the longest x1 1.96 us: per_device(): call(start_kernel, [HB] * 6, [shape(8, 32, LANES), shape(48, 6, 256), sha...]
  transfers between devices with their start and end apart: 1 -> 1, of which waited for: 1 -> 1; matrix products, arithmetic and copies ran while one was open for 0% -> 0% of each run, Pallas kernels for 0% -> 1%
where the time goes in v3:
time: 153 us
  blocking collectives  125 us (82%)
  Pallas kernels  17.2 us (11%)
  starting transfers between devices  6.48 us (4%)
  waiting for transfers between devices  2.97 us (2%)
    all_to_all x8, blocking collectives, exchange(): return lax.all_to_all(x, axis, 0, 0, tiled=True)  125 us
    all_to_all x1, starting transfers between devices, exchange(): return lax.all_to_all(x, axis, 0, 0, tiled=True)  6.48 us
    pallas_call x3, Pallas kernels, per_device(): call(cols_kernel, [VM] * 6 + [SM] * 2 + ([VM, SM] if it == 0 else []), [s...  3.76 us
  transfers between devices with their start and end apart: 1, of which 1 were waited for; matrix products, arithmetic and copies ran while one was open for 0% of the time, Pallas kernels for 1%

profile of v3, /device:TPU:1, one launch (start us, length us, event | category | flops | bytes accessed | tf_op | source)
XLA Modules:
  0.0 152.9 jit_solution(16086409339051596228)
XLA Ops:
  0.6 2.0 %start.1 = (f32[8,32,128]{2,1,0:T(8,128)}, f32[48,6,256]{2,1,0:T(8,128)S(1)}, f32[56,128]{1,0:T(8,128)S(1)}, s32[1,8]{1,0:T(1,128)S(1)}, s32[1,8]{1,0:T(1,128)S(1)}) custom-call(f32[6,256]{1,0:T(8,128)} %right_ref.1, f32[6,6,256]{2,1,0:T(8,128)} %diag_hbm.1, f32[6,6,8,256]{3,2,1,0:T(8,128)} %bitcast.7, s32[1,256]{1,0:T(1,128)} %bitcast.8, s32[1,8]{1,0:T(1,128)} %bitcast.9, ...), custom_call_target="tpu_custom_call" | custom-call | tf_op jit(solution)/shard_map/start/pallas_call | solution.py:649
  2.6 6.5 %all-to-all-start = ((f32[8,32,128]{2,1,0:T(8,128)}), f32[8,32,128]{2,1,0:T(8,128)S(1)}, u32[]{:S(2)}, u32[]{:S(2)}) async-start(f32[8,32,128]{2,1,0:T(8,128)} %get-tuple-element.31), calls=%async_computation | async-start | bytes 262144 | tf_op jit(solution)/shard_map/all_to_all | solution.py:640
  9.7 1.6 %load.1.early_ref = f32[4,384,384]{2,1,0:T(8,128)S(1)} custom-call(f32[8,384,384]{2,1,0:T(8,128)} %bitcast.5), custom_call_target="tpu_custom_call" | custom-call | tf_op jit(solution)/shard_map/load/pallas_call | solution.py:660
  11.4 3.0 %all-to-all-done.recv_ref = f32[8,32,128]{2,1,0:T(8,128)S(1)} async-done(((f32[8,32,128]{2,1,0:T(8,128)}), f32[8,32,128]{2,1,0:T(8,128)S(1)}, u32[]{:S(2)}, u32[]{:S(2)}) %all-to-all-start) | async-done | bytes 131104 | tf_op jit(solution)/shard_map/all_to_all | solution.py:640
  14.4 2.7 %first.1 = (f32[32,8,384]{2,1,0:T(8,128)S(1)}, f32[8,384]{1,0:T(8,128)S(1)}, f32[8,8,384]{2,1,0:T(8,128)S(1)}, f32[48,6,128]{2,1,0:T(8,128)S(1)}, f32[4,384,384]{2,1,0:T(8,128)S(1)}) custom-call(f32[8,32,128]{2,1,0:T(8,128)S(1)} %all-to-all-done.recv_ref, f32[48,6,256]{2,1,0:T(8,128)S(1)} %get-tuple-element.32.masked_ref, f32[8,384,384]{2,1,0:T(8,128)} %bitcast.6, ...), custom_call_target="tpu_custom_call" | custom-call | tf_op jit(solution)/shard_map/first/pallas_call | solution.py:663
  17.0 24.2 %all_to_all.45.recv_ref = f32[32,8,384]{2,1,0:T(8,128)S(1)} all-to-all(f32[32,8,384]{2,1,0:T(8,128)S(1)} %get-tuple-element.35), channel_id=1, replica_groups=mesh['frames'=32,'cols'=8] {'frames'}, dimensions={0} | all-to-all | bytes 786432 | tf_op jit(solution)/shard_map/all_to_all | solution.py:640
  41.2 1.3 products.3
  42.5 12.6 %all_to_all.46.recv_ref = f32[8,88,128]{2,1,0:T(8,128)S(1)} all-to-all(f32[8,88,128]{2,1,0:T(8,128)S(1)} %products.3), channel_id=1, replica_groups=mesh['frames'=32,'cols'=8] {'cols'}, dimensions={0} | all-to-all | bytes 720896 | tf_op jit(solution)/shard_map/all_to_all | solution.py:640
  55.1 1.7 %second.1 = (f32[32,8,384]{2,1,0:T(8,128)S(1)}, f32[8,384]{1,0:T(8,128)S(1)}, f32[8,8,384]{2,1,0:T(8,128)S(1)}, f32[8,384]{1,0:T(8,128)S(1)}, f32[3,8,128]{2,1,0...) custom-call(f32[8,88,128]{2,1,0:T(8,128)S(1)} %all_to_all.46.recv_ref, ...), custom_call_target="tpu_custom_call" | custom-call | tf_op jit(solution)/shard_map/second/pallas_call | solution.py:684
  56.7 17.6 %all_to_all.47.recv_ref = f32[32,8,384]{2,1,0:T(8,128)S(1)} all-to-all(f32[32,8,384]{2,1,0:T(8,128)S(1)} %get-tuple-element.41), channel_id=1, replica_groups=mesh['frames'=32,'cols'=8] {'frames'}, dimensions={0} | all-to-all | bytes 786432 | tf_op jit(solution)/shard_map/all_to_all | solution.py:640
  74.4 1.3 products.4
  75.6 10.4 %all_to_all.48.recv_ref = f32[8,40,128]{2,1,0:T(8,128)S(1)} all-to-all(f32[8,40,128]{2,1,0:T(8,128)S(1)} %products.4), channel_id=1, replica_groups=mesh['frames'=32,'cols'=8] {'cols'}, dimensions={0} | all-to-all | bytes 327680 | tf_op jit(solution)/shard_map/all_to_all | solution.py:640
  86.0 1.6 %next.1 = (f32[32,8,384]{2,1,0:T(8,128)S(1)}, f32[8,384]{1,0:T(8,128)S(1)}, f32[8,8,384]{2,1,0:T(8,128)S(1)}, f32[8,384]{1,0:T(8,128)S(1)}, f32[2,8,128]{2,1,0:T(8,128)S(1)}) custom-call(f32[8,40,128]{2,1,0:T(8,128)S(1)} %all_to_all.48.recv_ref, f32[8,8,384]{2,1,0:T(8,128)S(1)} %get-tuple-element.42.row_ref.before_ref.v1, ...), custom_call_target="tpu_custom_call" | custom-call | tf_op jit(solution)/shard_map/next/pallas_call | solution.py:694
  87.6 17.5 %all_to_all.49.recv_ref = f32[32,8,384]{2,1,0:T(8,128)S(1)} all-to-all(f32[32,8,384]{2,1,0:T(8,128)S(1)} %get-tuple-element.46), channel_id=1, replica_groups=mesh['frames'=32,'cols'=8] {'frames'}, dimensions={0} | all-to-all | bytes 786432 | tf_op jit(solution)/shard_map/all_to_all | solution.py:640
  105.1 1.3 products.5
  106.4 10.5 %all_to_all.50.recv_ref = f32[8,40,128]{2,1,0:T(8,128)S(1)} all-to-all(f32[8,40,128]{2,1,0:T(8,128)S(1)} %products.5), channel_id=1, replica_groups=mesh['frames'=32,'cols'=8] {'cols'}, dimensions={0} | all-to-all | bytes 327680 | tf_op jit(solution)/shard_map/all_to_all | solution.py:640
  116.8 1.6 %last.1 = (f32[32,40,128]{2,1,0:T(8,128)S(1)}, f32[8,384]{1,0:T(8,128)S(1)}, f32[8,8,384]{2,1,0:T(8,128)S(1)}, f32[8,384]{1,0:T(8,128)S(1)}) custom-call(f32[8,40,128]{2,1,0:T(8,128)S(1)} %all_to_all.50.recv_ref, f32[8,8,384]{2,1,0:T(8,128)S(1)} %get-tuple-element.47.row_ref.before_ref.v2, f32[48,6,128]{2,1,0:T(8,128)S(1)} %get-tuple-element.38.edge_ref, ...), custom_call_target="tpu_custom_call" | custom-call | tf_op jit(solution)/shard_map/last/pallas_call | solution.py:703
  118.5 22.2 %all_to_all.51.recv_ref = f32[32,40,128]{2,1,0:T(8,128)S(1)} all-to-all(f32[32,40,128]{2,1,0:T(8,128)S(1)} %get-tuple-element.51), channel_id=1, replica_groups=mesh['frames'=32,'cols'=8] {'frames'}, dimensions={0} | all-to-all | bytes 1310720 | tf_op jit(solution)/shard_map/all_to_all | solution.py:640
  140.7 0.0 copy-start
  140.7 1.4 finish.1
  142.1 9.9 %all_to_all.52.recv_ref = f32[8,16,128]{2,1,0:T(8,128)S(1)} all-to-all(f32[8,16,128]{2,1,0:T(8,128)S(1)} %get-tuple-element.54), channel_id=1, replica_groups=mesh['frames'=32,'cols'=8] {'cols'}, dimensions={0} | all-to-all | bytes 131072 | tf_op jit(solution)/shard_map/all_to_all | solution.py:640
  152.0 0.0 copy-done
  152.0 0.9 end.1
Async XLA Ops:
  2.6 11.8 %all-to-all-start = ((f32[8,32,128]{2,1,0:T(8,128)}), f32[8,32,128]{2,1,0:T(8,128)S(1)}, u32[]{:S(2)}, u32[]{:S(2)}) async-start(f32[8,32,128]{2,1,0:T(8,128)} %get-tuple-element.31), calls=%async_computation | async-start | bytes 262144 | tf_op jit(solution)/shard_map/all_to_all | solution.py:640
  140.7 11.3 %copy-start = (f32[6,256]{1,0:T(8,128)S(1)}, f32[6,256]{1,0:T(8,128)}, u32[]{:S(2)}) copy-start(f32[6,256]{1,0:T(8,128)} %right_ref.1) | copy-start | bytes 18436

commit v4 on v3

--- a/solution.py
+++ b/solution.py
@@ -11,7 +11,7 @@
 LANES = 128
 F32 = jnp.float32
 ROWS = ("frames", "cols")
-EARLY = 4
+EARLY = 5
 
 
 def lane_ids(rows):
@@ -63,7 +63,7 @@
 def start_kernel(
     right_hbm, diag_hbm, band_hbm, reach_hbm, rows_hbm, cols_hbm,
     send_ref, masked_ref, extra_ref, rows_ref, cols_ref,
-    right_ref, diag_ref, band_ref, reach_ref, pack, lines, *sems,
+    right_ref, diag_ref, band_ref, reach_ref, pack, *sems,
 ):
     copies = [
         pltpu.make_async_copy(source, to, sem)
@@ -95,7 +95,7 @@
     )
     store_as_tiles(pack, 0, first)
     for j in range(3):
-        lines[4 * j : 4 * j + 4, :] = pack[0:4, j * LANES : (j + 1) * LANES]
+        send_ref[4 * j : 4 * j + 4, :] = pack[0:4, j * LANES : (j + 1) * LANES]
     for d in range(4):
         turned = jnp.concatenate(
             [inverse[a][(a + d) % 6 : (a + d) % 6 + 1] for a in range(6)], axis=0
@@ -121,11 +121,18 @@
         for i in range(16):
             block = masked_ref[j * 16 + i, :, LANES : 2 * LANES]
             packed = jnp.where(ids // 8 == i, right(block, i * 8 + 8), packed)
-        lines[12 + 6 * j : 18 + 6 * j, :] = packed
-    lines[30:32, :] = jnp.zeros((2, LANES), F32)
-    whole = lines[...]
-    for c in range(8):
-        send_ref[c] = whole
+        send_ref[12 + 6 * j : 18 + 6 * j, :] = packed
+    send_ref[30:32, :] = jnp.zeros((2, LANES), F32)
+
+
+def blocks(refs):
+    col = lax.axis_index("cols")
+    rows = refs[0].shape[0] // 2
+    return [
+        (((col // 2 + 4 - d) % 4) * 2 + (col + i) % 2, refs[d], i * rows)
+        for d in range(4)
+        for i in range(2)
+    ]
 
 
 def load_kernel(tiles_hbm, tiles_ref, *sems):
@@ -292,7 +299,7 @@
 
 
 def first_kernel(
-    recv_ref, masked_ref, tiles_hbm, early_ref, rows_ref, cols_ref, count_ref,
+    recv0, recv1, recv2, recv3, masked_ref, tiles_hbm, early_ref, rows_ref, cols_ref, count_ref,
     send_ref, band_ref, row_ref, edge_ref, late_ref, picked, natural, sums, spread, *sems,
 ):
     copies = [
@@ -303,13 +310,13 @@
         copy.start()
     col = lax.axis_index("cols")
     row_ref[...] = jnp.zeros((8, 8, 384), F32)
-    for c in range(8):
+    for c, ref, at in blocks((recv0, recv1, recv2, recv3)):
         for j in range(3):
-            row_ref[c, 0:4, j * LANES : (j + 1) * LANES] = recv_ref[c, 4 * j : 4 * j + 4, :]
-    prev = (col + 7) % 8
+            row_ref[c, 0:4, j * LANES : (j + 1) * LANES] = ref[at + 4 * j : at + 4 * j + 4, :]
     ids = lane_ids(6)
     for j in range(3):
-        part = recv_ref[prev, 12 + 6 * j : 18 + 6 * j, :]
+        at = 32 + 12 + 6 * j
+        part = jnp.where(col % 2 == 1, recv0[at : at + 6, :], recv1[at : at + 6, :])
         for i in range(16):
             edge_ref[j * 16 + i] = jnp.where(ids >= 120, right(part, 120 - i * 8), 0.0)
     scratch = (picked, natural, sums, spread)
@@ -319,44 +326,44 @@
     )
 
 
-def unpack(recv_ref, pick_ref, inverse_ref):
+def unpack(refs, pick_ref, inverse_ref):
     lane = lane_ids(1)
-    target = jnp.full((1, LANES), -1.0, F32)
-    for c in range(8):
-        target = jnp.where(lane // 8 == c, right(recv_ref[c, 39:40, :], 8 * c), target)
-    index = lax.broadcasted_iota(jnp.int32, (64, LANES), 0).astype(F32)
-    found = (index == jnp.broadcast_to(target, (64, LANES))).astype(F32)
-    pick_ref[...] = jnp.where(lax.broadcasted_iota(jnp.int32, (64, LANES), 1) < 64, found, 0.0)
+    group = lane % 64 // 8
+    device = jnp.zeros((1, LANES), jnp.int32)
+    target = jnp.zeros((1, LANES), F32)
     low = lax.broadcasted_iota(jnp.int32, (8, LANES), 0) < 4
-    for c in range(8):
+    for b, (c, ref, at) in enumerate(blocks(refs)):
+        device = jnp.where(group == b, c, device)
+        target = jnp.where(group == b, right(ref[at + 39 : at + 40, :], 8 * b), target)
         parts = []
         for g in range(12):
-            part = recv_ref[c, 40 + 8 * (g // 2) : 48 + 8 * (g // 2), :]
+            first = at + 40 + 8 * (g // 2)
+            part = ref[first : first + 8, :]
             part = pltpu.roll(part, 4, 0) if g % 2 else part
             parts.append(jnp.where(low, part, 0.0))
         parts = [jnp.concatenate(parts[3 * d : 3 * d + 3], axis=1) for d in range(4)]
         parts += [left(parts[2], 256), left(parts[1], 320)]
         for d in range(6):
             inverse_ref[d, c] = parts[d]
-
-
-def row_image(recv_ref, pick_ref):
-    products = jnp.concatenate(
-        [recv_ref[:, 8 * j : 8 * j + 8, :].reshape(64, LANES) for j in range(3)], axis=1
-    )
-    image = select_sum(pick_ref[:, 0:64], products)
-    sub = lax.broadcasted_iota(jnp.int32, (8, LANES), 0)
-    rows = []
-    for c in range(8):
-        one, two = recv_ref[c, 24:32, :], recv_ref[c, 32:40, :]
-        after = recv_ref[(c + 1) % 8, 32:40, :]
-        parts = [one, pltpu.roll(one, 4, 0), two]
-        onward = [pltpu.roll(after, 7 - j, 0) for j in range(3)]
-        parts = [
-            jnp.where(sub < 4, x, 0.0) + jnp.where(sub == 3, y, 0.0) for x, y in zip(parts, onward)
-        ]
-        rows.append(image[8 * c : 8 * c + 8] + jnp.concatenate(parts, axis=1))
-    return jnp.concatenate(rows, axis=0).reshape(8, 8, 384)
+    own = (device * 8 + lane % 4).astype(F32)
+    onward = ((device + 7) % 8 * 8 + 3).astype(F32)
+    at = lane % 8
+    none = jnp.full((1, LANES), -1.0, F32)
+    index = lax.broadcasted_iota(jnp.int32, (64, LANES), 0).astype(F32)
+    for j in range(3):
+        three = jnp.where((at < 4) == (j == 0), own, none) if j < 2 else none
+        four = jnp.where(at == 4 + j, onward, jnp.where(at < 4, own, none) if j == 2 else none)
+        for half, wanted in enumerate((jnp.where(lane < 64, target, three), jnp.where(lane < 64, four, none))):
+            found = (index == jnp.broadcast_to(wanted, (64, LANES))).astype(F32)
+            pick_ref[j, :, half * LANES : (half + 1) * LANES] = found
+
+
+def row_image(refs, pick_ref):
+    parts = []
+    for j in range(3):
+        rows = [ref[at + first : at + first + 8, :] for first in (8 * j, 24, 32) for _, ref, at in blocks(refs)]
+        parts.append(select_sum(pick_ref[j, :, 0:192], jnp.concatenate(rows, axis=0)))
+    return jnp.concatenate(parts, axis=1).reshape(8, 8, 384)
 
 
 def folded(x):
@@ -364,9 +371,9 @@
     return x[:, 0:128] + x[:, 128:256] + x[:, 256:384]
 
 
-def advance(recv_ref, pick_ref, inverse_ref, before_ref, row_ref, image_ref, moment_ref, picked):
-    col = lax.axis_index("cols")
-    image = row_image(recv_ref, pick_ref)
+def advance(refs, pick_ref, inverse_ref, before_ref, row_ref, image_ref, moment_ref, picked):
+    col = lax.axis_index("cols")
+    image = row_image(refs, pick_ref)
     flat = image.reshape(64, 384)
     vector = inverse_ref[0].reshape(64, 384) * flat
     for d in range(1, 6):
@@ -382,37 +389,37 @@
 
 
 def second_kernel(
-    recv_ref, before_ref, edge_ref, masked_ref, early_ref, late_ref, rows_ref, cols_ref, count_ref,
+    recv0, recv1, recv2, recv3, before_ref, edge_ref, masked_ref, early_ref, late_ref, rows_ref, cols_ref, count_ref,
     send_ref, band_ref, row_ref, image_ref, moment_ref, pick_ref, inverse_ref, *scratch,
 ):
-    unpack(recv_ref, pick_ref, inverse_ref)
-    total = recv_ref[0, 39:40, :]
-    for c in range(1, 8):
-        total = total + recv_ref[c, 39:40, :]
+    unpack((recv0, recv1, recv2, recv3), pick_ref, inverse_ref)
+    total = jnp.zeros((1, LANES), F32)
+    for _, ref, at in blocks((recv0, recv1, recv2, recv3)):
+        total = total + ref[at + 39 : at + 40, :]
     sub = lax.broadcasted_iota(jnp.int32, (8, LANES), 0)
     lane = lax.broadcasted_iota(jnp.int32, (8, LANES), 1)
     moment_ref[2] = jnp.where((sub == 0) & (lane == 8), jnp.broadcast_to(total, (8, LANES)), 0.0)
-    advance(recv_ref, pick_ref, inverse_ref, before_ref, row_ref, image_ref, moment_ref, scratch[0])
+    advance((recv0, recv1, recv2, recv3), pick_ref, inverse_ref, before_ref, row_ref, image_ref, moment_ref, scratch[0])
     ids_refs = (rows_ref, cols_ref, count_ref)
     tiles_refs = (early_ref, late_ref)
     send_frames(row_ref, edge_ref, masked_ref, tiles_refs, ids_refs, send_ref, band_ref, scratch)
 
 
 def next_kernel(
-    recv_ref, before_ref, edge_ref, masked_ref, early_ref, late_ref, rows_ref, cols_ref, count_ref,
+    recv0, recv1, recv2, recv3, before_ref, edge_ref, masked_ref, early_ref, late_ref, rows_ref, cols_ref, count_ref,
     pick_ref, inverse_ref, send_ref, band_ref, row_ref, image_ref, moment_ref, *scratch,
 ):
-    advance(recv_ref, pick_ref, inverse_ref, before_ref, row_ref, image_ref, moment_ref, scratch[0])
+    advance((recv0, recv1, recv2, recv3), pick_ref, inverse_ref, before_ref, row_ref, image_ref, moment_ref, scratch[0])
     ids_refs = (rows_ref, cols_ref, count_ref)
     tiles_refs = (early_ref, late_ref)
     send_frames(row_ref, edge_ref, masked_ref, tiles_refs, ids_refs, send_ref, band_ref, scratch)
 
 
 def last_kernel(
-    recv_ref, before_ref, edge_ref, masked_ref, early_ref, late_ref, rows_ref, cols_ref, count_ref,
+    recv0, recv1, recv2, recv3, before_ref, edge_ref, masked_ref, early_ref, late_ref, rows_ref, cols_ref, count_ref,
     pick_ref, inverse_ref, m1_ref, m2_ref, send_ref, band_ref, row_ref, image_ref, *scratch,
 ):
-    moments = advance(recv_ref, pick_ref, inverse_ref, before_ref, row_ref, image_ref, None, scratch[0])
+    moments = advance((recv0, recv1, recv2, recv3), pick_ref, inverse_ref, before_ref, row_ref, image_ref, None, scratch[0])
     known = [m1_ref[2], m1_ref[0], m1_ref[1], m2_ref[0], m2_ref[1]] + moments
     ids_refs = (rows_ref, cols_ref, count_ref)
     tiles_refs = (early_ref, late_ref)
@@ -451,10 +458,15 @@
 
 
 def cols_kernel(recv_ref, early_ref, late_ref, row_ref, edge_ref, band_ref, cols_ref, count_ref, *rest):
-    extra_ref, rows_ref = rest[:2] if len(rest) == 4 else (None, None)
-    send_ref, pack = rest[-2:]
+    extra_ref, rows_ref = rest[:2] if len(rest) == 3 else (None, None)
+    pack = rest[-1]
     frame = lax.axis_index("frames")
     col = lax.axis_index("cols")
+    def piece_of(s):
+        q = cols_ref[0, s]
+        return recv_ref[q // 4, pl.ds(q % 4, 1), :]
+
+    tile_products((early_ref, late_ref), piece_of, count_ref[0, 0], pack)
     total = recv_ref[0]
     for f in range(1, 32):
         total = total + recv_ref[f]
@@ -475,16 +487,8 @@
             misc = jnp.where(lane_ids(1) == s, ((r // 4) * 8 + r % 4).astype(F32), misc)
     pack[39:40, :] = misc
 
-    def piece_of(s):
-        q = cols_ref[0, s]
-        return recv_ref[q // 4, pl.ds(q % 4, 1), :]
-
-    tile_products((early_ref, late_ref), piece_of, count_ref[0, 0], pack)
-    whole = pack[...]
-    for c in range(8):
-        send_ref[c, 0:40, :] = whole
-        if extra_ref is not None:
-            send_ref[c, 40:88, :] = extra_ref[0:48, :]
+    if extra_ref is not None:
+        pack[40:88, :] = extra_ref[0:48, :]
 
 
 def finish_kernel(
@@ -639,6 +643,16 @@
     def exchange(x, axis):
         return lax.all_to_all(x, axis, 0, 0, tiled=True)
 
+    def share(x):
+        chips = lax.axis_size("cols") // 2
+        swap = [(i, i ^ 1) for i in range(2 * chips)]
+        pair = jnp.concatenate([x, lax.ppermute(x, "cols", swap)], axis=0)
+        others = []
+        for d in range(1, chips):
+            ahead = [(i, (i + 2 * d) % (2 * chips)) for i in range(2 * chips)]
+            others.append(lax.ppermute(pair, "cols", ahead))
+        return [pair, *others]
+
     def in_hbm(x):
         return pltpu.with_memory_space_constraint(x, pltpu.HBM)
 
@@ -649,43 +663,43 @@
     send, masked, extra, *ids = call(
         start_kernel,
         [HB] * 6,
-        [shape(8, 32, LANES), shape(48, 6, 256), shape(56, LANES)]
+        [shape(32, LANES), shape(48, 6, 256), shape(56, LANES)]
         + [shape(1, 8, kind=jnp.int32)] * 2,
-        [(6, 256), (6, 6, 256), (6, 6, 8, 256), pltpu.VMEM((1, 256), jnp.int32), (8, 384), (32, LANES)]
+        [(6, 256), (6, 6, 256), (6, 6, 8, 256), pltpu.VMEM((1, 256), jnp.int32), (8, 384)]
         + [sem] * 6,
         "start",
     )(*[in_hbm(x) for x in inputs])
     ids.append(tile_count)
-    recv = exchange(send, "cols")
+    recv = share(send)
     (early,) = call(load_kernel, [HB], [shape(EARLY, 384, 384)], [sem] * EARLY, "load")(stored)
     frames_out = [shape(32, 8, 384), shape(8, 384), shape(8, 8, 384)]
     scratch = [(LANES, 384), (8, 256), (8, 256), (384, 512)]
     send, band, row, edges, late = call(
         first_kernel,
-        [VM] * 2 + [HB, VM] + [SM] * 3,
+        [VM] * 5 + [HB, VM] + [SM] * 3,
         frames_out + [shape(48, 6, LANES), shape(8 - EARLY, 384, 384)],
         scratch + [sem] * (8 - EARLY),
         "first",
-    )(recv, masked, stored, early, *ids)
+    )(*recv, masked, stored, early, *ids)
     vectors, images, moments = [row], [], []
     for it in range(ITERS - 1):
         recv = exchange(send, "frames")
         (send,) = call(
             cols_kernel,
             [VM] * 6 + [SM] * 2 + ([VM, SM] if it == 0 else []),
-            [shape(8, 88 if it == 0 else 40, LANES)],
-            [(40, LANES)],
+            [shape(88 if it == 0 else 40, LANES)],
+            [],
             "products",
         )(recv, early, late, row, edges, band, *ids[1:], *((extra, ids[0]) if it == 0 else ()))
-        recv = exchange(send, "cols")
-        given = (recv, row, edges, masked, early, late, *ids)
-        specs = [VM] * 6 + [SM] * 3
+        recv = share(send)
+        given = (*recv, row, edges, masked, early, late, *ids)
+        specs = [VM] * 9 + [SM] * 3
         if it == 0:
             send, band, row, image, moment, pick, inverse = call(
                 second_kernel,
                 specs,
                 frames_out
-                + [shape(8, 384), shape(3, 8, LANES), shape(64, LANES), shape(6, 8, 8, 384)],
+                + [shape(8, 384), shape(3, 8, LANES), shape(3, 64, 256), shape(6, 8, 8, 384)],
                 scratch,
                 "second",
             )(*given)

time: 153 us -> 149 us (0.974)
  blocking collectives: 125 us -> 89.8 us
  starting transfers between devices: 6.48 us -> 22.1 us
  waiting for transfers between devices: 2.97 us -> 18.3 us
    all_to_all x8 -> x5, blocking collectives: 125 us -> 89.8 us  [exchange(): return lax.all_to_all(x, axis, 0, 0, tiled=True)]
    ppermute x0 -> x16, starting transfers between devices: none -> 22.1 us  [the longest x4 13.4 us: share(): pair = jnp.concatenate([x, lax.ppermute(x, 'cols', swap)], axis=0)]
    ppermute x0 -> x16, waiting for transfers between devices: none -> 18.3 us  [the longest x12 14.9 us: share(): others.append(lax.ppermute(pair, 'cols', ahead))]
    all_to_all x1 -> x0, starting transfers between devices: 6.48 us -> none  [exchange(): return lax.all_to_all(x, axis, 0, 0, tiled=True)]
    all_to_all x1 -> x0, waiting for transfers between devices: 2.97 us -> none  [exchange(): return lax.all_to_all(x, axis, 0, 0, tiled=True)]
  transfers between devices with their start and end apart: 1 -> 16, of which waited for: 1 -> 15; matrix products, arithmetic and copies ran while one was open for 0% -> 0% of each run, Pallas kernels for 1% -> 1%
where the time goes in v4:
time: 149 us; the launch traced here: 148 us
  blocking collectives  89.8 us (60%)
  starting transfers between devices  22.1 us (15%)
  waiting for transfers between devices  18.3 us (12%)
  Pallas kernels  16.8 us (11%)
    all_to_all x5, blocking collectives, exchange(): return lax.all_to_all(x, axis, 0, 0, tiled=True)  89.8 us
    ppermute x12, waiting for transfers between devices, share(): others.append(lax.ppermute(pair, 'cols', ahead))  14.9 us
    ppermute x4, starting transfers between devices, share(): pair = jnp.concatenate([x, lax.ppermute(x, 'cols', swap)], axis=0)  13.4 us
    ppermute x12, starting transfers between devices, share(): others.append(lax.ppermute(pair, 'cols', ahead))  8.71 us
    ppermute x4, waiting for transfers between devices, share(): pair = jnp.concatenate([x, lax.ppermute(x, 'cols', swap)], axis=0)  3.4 us
    pallas_call x3, Pallas kernels, per_device(): call(cols_kernel, [VM] * 6 + [SM] * 2 + ([VM, SM] if it == 0 else []), [s...  3.39 us
  transfers between devices with their start and end apart: 16, of which 15 were waited for; matrix products, arithmetic and copies ran while one was open for 0% of the time, Pallas kernels for 1%

profile of v4, /device:TPU:1, one launch (start us, length us, event | category | flops | bytes accessed | tf_op | source)
XLA Modules:
  0.0 148.4 jit_solution(13483103252369841628)
XLA Ops:
  0.6 1.3 start.1
  1.9 3.3 %collective-permute-start = (f32[32,128]{1,0:T(8,128)S(1)}, f32[32,128]{1,0:T(8,128)S(1)}, u32[]{:S(2)}, u32[]{:S(2)}) collective-permute-start(f32[32,128]{1,0:T(8,128)S(1)} %get-tuple-element.31), channel_id=1, source_target_pairs={{0,1},{1,0},{2,3},{3,2},{4,5},{5,4},{6,7},{7,6},{8,9},{9,8},{10,11... | collective-permute-start | bytes 49160 | tf_op jit(solution)/shard_map/ppermute | solution.py:649
  6.1 1.0 collective-permute-start.3
  8.8 1.8 %load.1.early_ref = f32[5,384,384]{2,1,0:T(8,128)S(1)} custom-call(f32[8,384,384]{2,1,0:T(8,128)} %bitcast.5), custom_call_target="tpu_custom_call" | custom-call | tf_op jit(solution)/shard_map/load/pallas_call | solution.py:674
  11.7 2.4 %first.1 = (f32[32,8,384]{2,1,0:T(8,128)S(1)}, f32[8,384]{1,0:T(8,128)S(1)}, f32[8,8,384]{2,1,0:T(8,128)S(1)}, f32[48,6,128]{2,1,0:T(8,128)S(1)}, f32[3,384,384]{2,1,0:T(8,128)S(1)}) custom-call(f32[64,128]{1,0:T(8,128)S(1)} %constant_dynamic-update-slice_fusion.recv0, f32[64,128]{1,0:T(8,128)S(1)} %collective-permute-done.1.recv1, ...), custom_call_target="tpu_custom_call" | custom-call | tf_op jit(solution)/shard_map/first/pallas_call | solution.py:677
  14.2 23.5 %all_to_all.25.recv_ref = f32[32,8,384]{2,1,0:T(8,128)S(1)} all-to-all(f32[32,8,384]{2,1,0:T(8,128)S(1)} %get-tuple-element.35), channel_id=1, replica_groups=mesh['frames'=32,'cols'=8] {'frames'}, dimensions={0} | all-to-all | bytes 786432 | tf_op jit(solution)/shard_map/all_to_all | solution.py:644
  37.6 1.1 products.3
  38.8 3.7 %collective-permute-start.4 = (f32[88,128]{1,0:T(8,128)S(1)}, f32[88,128]{1,0:T(8,128)S(1)}, u32[]{:S(2)}, u32[]{:S(2)}) collective-permute-start(f32[88,128]{1,0:T(8,128)S(1)} %products.3), channel_id=1, source_target_pairs={{0,1},{1,0},{2,3},{3,2},{4,5},{5,4},{6,7},{7,6},{8,9},{9,8},{10,11... | collective-permute-start | bytes 135176 | tf_op jit(solution)/shard_map/ppermute | solution.py:649
  43.3 1.1 collective-permute-start.7
  44.5 1.4 collective-permute-start.6
  45.9 1.2 collective-permute-done.7.recv3
  47.1 2.3 %collective-permute-done.6.recv2 = f32[176,128]{1,0:T(8,128)S(1)} collective-permute-done((f32[176,128]{1,0:T(8,128)S(1)}, f32[176,128]{1,0:T(8,128)S(1)}, u32[]{:S(2)}, u32[]{:S(2)}) %collective-permute-start.6) | collective-permute-done | bytes 90144 | tf_op jit(solution)/shard_map/ppermute | solution.py:653
  49.3 2.6 %collective-permute-done.5.recv1 = f32[176,128]{1,0:T(8,128)S(1)} collective-permute-done((f32[176,128]{1,0:T(8,128)S(1)}, f32[176,128]{1,0:T(8,128)S(1)}, u32[]{:S(2)}, u32[]{:S(2)}) %collective-permute-start.5) | collective-permute-done | bytes 90144 | tf_op jit(solution)/shard_map/ppermute | solution.py:653
  51.9 1.9 %second.1 = (f32[32,8,384]{2,1,0:T(8,128)S(1)}, f32[8,384]{1,0:T(8,128)S(1)}, f32[8,8,384]{2,1,0:T(8,128)S(1)}, f32[8,384]{1,0:T(8,128)S(1)}, f32[3,8,128]{2,1,0...) custom-call(f32[176,128]{1,0:T(8,128)S(1)} %pad_maximum_fusion.recv0, ...), custom_call_target="tpu_custom_call" | custom-call | tf_op jit(solution)/shard_map/second/pallas_call | solution.py:698
  53.8 17.0 %all_to_all.26.recv_ref = f32[32,8,384]{2,1,0:T(8,128)S(1)} all-to-all(f32[32,8,384]{2,1,0:T(8,128)S(1)} %get-tuple-element.41), channel_id=1, replica_groups=mesh['frames'=32,'cols'=8] {'frames'}, dimensions={0} | all-to-all | bytes 786432 | tf_op jit(solution)/shard_map/all_to_all | solution.py:644
  70.8 1.1 products.4
  72.0 3.1 %collective-permute-start.8 = (f32[40,128]{1,0:T(8,128)S(1)}, f32[40,128]{1,0:T(8,128)S(1)}, u32[]{:S(2)}, u32[]{:S(2)}) collective-permute-start(f32[40,128]{1,0:T(8,128)S(1)} %products.4), channel_id=1, source_target_pairs={{0,1},{1,0},{2,3},{3,2},{4,5},{5,4},{6,7},{7,6},{8,9},{9,8},{10,11... | collective-permute-start | bytes 61448 | tf_op jit(solution)/shard_map/ppermute | solution.py:649
  76.0 1.5 collective-permute-start.10
  78.7 1.6 %collective-permute-done.10.recv2 = f32[80,128]{1,0:T(8,128)S(1)} collective-permute-done((f32[80,128]{1,0:T(8,128)S(1)}, f32[80,128]{1,0:T(8,128)S(1)}, u32[]{:S(2)}, u32[]{:S(2)}) %collective-permute-start.10) | collective-permute-done | bytes 40992 | tf_op jit(solution)/shard_map/ppermute | solution.py:653
  80.3 1.5 %collective-permute-done.9.recv1 = f32[80,128]{1,0:T(8,128)S(1)} collective-permute-done((f32[80,128]{1,0:T(8,128)S(1)}, f32[80,128]{1,0:T(8,128)S(1)}, u32[]{:S(2)}, u32[]{:S(2)}) %collective-permute-start.9) | collective-permute-done | bytes 40992 | tf_op jit(solution)/shard_map/ppermute | solution.py:653
  81.9 1.8 %next.1 = (f32[32,8,384]{2,1,0:T(8,128)S(1)}, f32[8,384]{1,0:T(8,128)S(1)}, f32[8,8,384]{2,1,0:T(8,128)S(1)}, f32[8,384]{1,0:T(8,128)S(1)}, f32[2,8,128]{2,1,0:T(8,128)S(1)}) custom-call(f32[80,128]{1,0:T(8,128)S(1)} %pad_maximum_fusion.1.recv0, f32[80,128]{1,0:T(8,128)S(1)} %collective-permute-done.9.recv1, f32[80,128]{1,0:T(8,128)S(1)} %collective-permute-done.10.recv2, ...), custom_call_target="tpu_custom_call" | custom-call | tf_op jit(solution)/shard_map/next/pallas_call | solution.py:708
  83.7 16.6 %all_to_all.27.recv_ref = f32[32,8,384]{2,1,0:T(8,128)S(1)} all-to-all(f32[32,8,384]{2,1,0:T(8,128)S(1)} %get-tuple-element.46), channel_id=1, replica_groups=mesh['frames'=32,'cols'=8] {'frames'}, dimensions={0} | all-to-all | bytes 786432 | tf_op jit(solution)/shard_map/all_to_all | solution.py:644
  100.3 1.1 products.5
  101.4 3.4 %collective-permute-start.12 = (f32[40,128]{1,0:T(8,128)S(1)}, f32[40,128]{1,0:T(8,128)S(1)}, u32[]{:S(2)}, u32[]{:S(2)}) collective-permute-start(f32[40,128]{1,0:T(8,128)S(1)} %products.5), channel_id=1, source_target_pairs={{0,1},{1,0},{2,3},{3,2},{4,5},{5,4},{6,7},{7,6},{8,9},{9,8},{10,11... | collective-permute-start | bytes 61448 | tf_op jit(solution)/shard_map/ppermute | solution.py:649
  105.6 1.1 collective-permute-start.15
  107.3 1.2 collective-permute-done.15.recv3
  108.5 2.6 %collective-permute-done.14.recv2 = f32[80,128]{1,0:T(8,128)S(1)} collective-permute-done((f32[80,128]{1,0:T(8,128)S(1)}, f32[80,128]{1,0:T(8,128)S(1)}, u32[]{:S(2)}, u32[]{:S(2)}) %collective-permute-start.14) | collective-permute-done | bytes 40992 | tf_op jit(solution)/shard_map/ppermute | solution.py:653
  111.5 1.9 %last.1 = (f32[32,40,128]{2,1,0:T(8,128)S(1)}, f32[8,384]{1,0:T(8,128)S(1)}, f32[8,8,384]{2,1,0:T(8,128)S(1)}, f32[8,384]{1,0:T(8,128)S(1)}) custom-call(f32[80,128]{1,0:T(8,128)S(1)} %pad_maximum_fusion.2.recv0, f32[80,128]{1,0:T(8,128)S(1)} %collective-permute-done.13.recv1, f32[80,128]{1,0:T(8,128)S(1)} %collective-permute-done.14.recv2, ...), custom_call_target="tpu_custom_call" | custom-call | tf_op jit(solution)/shard_map/last/pallas_call | solution.py:717
  113.4 21.0 %all_to_all.28.recv_ref = f32[32,40,128]{2,1,0:T(8,128)S(1)} all-to-all(f32[32,40,128]{2,1,0:T(8,128)S(1)} %get-tuple-element.51), channel_id=1, replica_groups=mesh['frames'=32,'cols'=8] {'frames'}, dimensions={0} | all-to-all | bytes 1310720 | tf_op jit(solution)/shard_map/all_to_all | solution.py:644
  134.3 1.4 finish.1
  135.7 11.8 %all_to_all.29.recv_ref = f32[8,16,128]{2,1,0:T(8,128)S(1)} all-to-all(f32[8,16,128]{2,1,0:T(8,128)S(1)} %get-tuple-element.54), channel_id=1, replica_groups=mesh['frames'=32,'cols'=8] {'cols'}, dimensions={0} | all-to-all | bytes 131072 | tf_op jit(solution)/shard_map/all_to_all | solution.py:644
  147.5 0.9 end.1
  (23 shorter events, 8.0 us)
Async XLA Ops:
  1.9 4.1 %collective-permute-start = (f32[32,128]{1,0:T(8,128)S(1)}, f32[32,128]{1,0:T(8,128)S(1)}, u32[]{:S(2)}, u32[]{:S(2)}) collective-permute-start(f32[32,128]{1,0:T(8,128)S(1)} %get-tuple-element.31), channel_id=1, source_target_pairs={{0,1},{1,0},{2,3},{3,2},{4,5},{5,4},{6,7},{7,6},{8,9},{9,8},{10,11... | collective-permute-start | bytes 49160 | tf_op jit(solution)/shard_map/ppermute | solution.py:649
  6.1 4.6 %collective-permute-start.3 = (f32[64,128]{1,0:T(8,128)S(1)}, f32[64,128]{1,0:T(8,128)S(1)}, u32[]{:S(2)}, u32[]{:S(2)}) collective-permute-start(f32[64,128]{1,0:T(8,128)S(1)} %constant_dynamic-update-slice_fusion.recv0), channel_id=1, source_target_pairs={{0,6},{1,7},{2,0},{3,1},{4,2},{5,3},{6,4},{7,5},{8,14},{9,15},{10,... | collective-permute-start | bytes 98312 | tf_op jit(solution)/shard_map/ppermute | solution.py:653
  7.1 4.3 %collective-permute-start.2 = (f32[64,128]{1,0:T(8,128)S(1)}, f32[64,128]{1,0:T(8,128)S(1)}, u32[]{:S(2)}, u32[]{:S(2)}) collective-permute-start(f32[64,128]{1,0:T(8,128)S(1)} %constant_dynamic-update-slice_fusion.recv0), channel_id=1, source_target_pairs={{0,4},{1,5},{2,6},{3,7},{4,0},{5,1},{6,2},{7,3},{8,12},{9,13},{10,... | collective-permute-start | bytes 98312 | tf_op jit(solution)/shard_map/ppermute | solution.py:653
  7.5 4.3 %collective-permute-start.1 = (f32[64,128]{1,0:T(8,128)S(1)}, f32[64,128]{1,0:T(8,128)S(1)}, u32[]{:S(2)}, u32[]{:S(2)}) collective-permute-start(f32[64,128]{1,0:T(8,128)S(1)} %constant_dynamic-update-slice_fusion.recv0), channel_id=1, source_target_pairs={{0,2},{1,3},{2,4},{3,5},{4,6},{5,7},{6,0},{7,1},{8,10},{9,11},{10,... | collective-permute-start | bytes 98312 | tf_op jit(solution)/shard_map/ppermute | solution.py:653
  38.8 4.6 %collective-permute-start.4 = (f32[88,128]{1,0:T(8,128)S(1)}, f32[88,128]{1,0:T(8,128)S(1)}, u32[]{:S(2)}, u32[]{:S(2)}) collective-permute-start(f32[88,128]{1,0:T(8,128)S(1)} %products.3), channel_id=1, source_target_pairs={{0,1},{1,0},{2,3},{3,2},{4,5},{5,4},{6,7},{7,6},{8,9},{9,8},{10,11... | collective-permute-start | bytes 135176 | tf_op jit(solution)/shard_map/ppermute | solution.py:649
  43.3 3.8 %collective-permute-start.7 = (f32[176,128]{1,0:T(8,128)S(1)}, f32[176,128]{1,0:T(8,128)S(1)}, u32[]{:S(2)}, u32[]{:S(2)}) collective-permute-start(f32[176,128]{1,0:T(8,128)S(1)} %pad_maximum_fusion.recv0), channel_id=1, source_target_pairs={{0,6},{1,7},{2,0},{3,1},{4,2},{5,3},{6,4},{7,5},{8,14},{9,15},{10,... | collective-permute-start | bytes 270344 | tf_op jit(solution)/shard_map/ppermute | solution.py:653
  44.5 4.9 %collective-permute-start.6 = (f32[176,128]{1,0:T(8,128)S(1)}, f32[176,128]{1,0:T(8,128)S(1)}, u32[]{:S(2)}, u32[]{:S(2)}) collective-permute-start(f32[176,128]{1,0:T(8,128)S(1)} %pad_maximum_fusion.recv0), channel_id=1, source_target_pairs={{0,4},{1,5},{2,6},{3,7},{4,0},{5,1},{6,2},{7,3},{8,12},{9,13},{10,... | collective-permute-start | bytes 270344 | tf_op jit(solution)/shard_map/ppermute | solution.py:653
  45.9 6.1 %collective-permute-start.5 = (f32[176,128]{1,0:T(8,128)S(1)}, f32[176,128]{1,0:T(8,128)S(1)}, u32[]{:S(2)}, u32[]{:S(2)}) collective-permute-start(f32[176,128]{1,0:T(8,128)S(1)} %pad_maximum_fusion.recv0), channel_id=1, source_target_pairs={{0,2},{1,3},{2,4},{3,5},{4,6},{5,7},{6,0},{7,1},{8,10},{9,11},{10,... | collective-permute-start | bytes 270344 | tf_op jit(solution)/shard_map/ppermute | solution.py:653
  72.0 3.9 %collective-permute-start.8 = (f32[40,128]{1,0:T(8,128)S(1)}, f32[40,128]{1,0:T(8,128)S(1)}, u32[]{:S(2)}, u32[]{:S(2)}) collective-permute-start(f32[40,128]{1,0:T(8,128)S(1)} %products.4), channel_id=1, source_target_pairs={{0,1},{1,0},{2,3},{3,2},{4,5},{5,4},{6,7},{7,6},{8,9},{9,8},{10,11... | collective-permute-start | bytes 61448 | tf_op jit(solution)/shard_map/ppermute | solution.py:649
  75.9 2.9 %collective-permute-start.11 = (f32[80,128]{1,0:T(8,128)S(1)}, f32[80,128]{1,0:T(8,128)S(1)}, u32[]{:S(2)}, u32[]{:S(2)}) collective-permute-start(f32[80,128]{1,0:T(8,128)S(1)} %pad_maximum_fusion.1.recv0), channel_id=1, source_target_pairs={{0,6},{1,7},{2,0},{3,1},{4,2},{5,3},{6,4},{7,5},{8,14},{9,15},{10,... | collective-permute-start | bytes 122888 | tf_op jit(solution)/shard_map/ppermute | solution.py:653
  76.0 4.4 %collective-permute-start.10 = (f32[80,128]{1,0:T(8,128)S(1)}, f32[80,128]{1,0:T(8,128)S(1)}, u32[]{:S(2)}, u32[]{:S(2)}) collective-permute-start(f32[80,128]{1,0:T(8,128)S(1)} %pad_maximum_fusion.1.recv0), channel_id=1, source_target_pairs={{0,4},{1,5},{2,6},{3,7},{4,0},{5,1},{6,2},{7,3},{8,12},{9,13},{10,... | collective-permute-start | bytes 122888 | tf_op jit(solution)/shard_map/ppermute | solution.py:653
  77.5 4.4 %collective-permute-start.9 = (f32[80,128]{1,0:T(8,128)S(1)}, f32[80,128]{1,0:T(8,128)S(1)}, u32[]{:S(2)}, u32[]{:S(2)}) collective-permute-start(f32[80,128]{1,0:T(8,128)S(1)} %pad_maximum_fusion.1.recv0), channel_id=1, source_target_pairs={{0,2},{1,3},{2,4},{3,5},{4,6},{5,7},{6,0},{7,1},{8,10},{9,11},{10,... | collective-permute-start | bytes 122888 | tf_op jit(solution)/shard_map/ppermute | solution.py:653
  101.4 4.2 %collective-permute-start.12 = (f32[40,128]{1,0:T(8,128)S(1)}, f32[40,128]{1,0:T(8,128)S(1)}, u32[]{:S(2)}, u32[]{:S(2)}) collective-permute-start(f32[40,128]{1,0:T(8,128)S(1)} %products.5), channel_id=1, source_target_pairs={{0,1},{1,0},{2,3},{3,2},{4,5},{5,4},{6,7},{7,6},{8,9},{9,8},{10,11... | collective-permute-start | bytes 61448 | tf_op jit(solution)/shard_map/ppermute | solution.py:649
  105.6 2.9 %collective-permute-start.15 = (f32[80,128]{1,0:T(8,128)S(1)}, f32[80,128]{1,0:T(8,128)S(1)}, u32[]{:S(2)}, u32[]{:S(2)}) collective-permute-start(f32[80,128]{1,0:T(8,128)S(1)} %pad_maximum_fusion.2.recv0), channel_id=1, source_target_pairs={{0,6},{1,7},{2,0},{3,1},{4,2},{5,3},{6,4},{7,5},{8,14},{9,15},{10,... | collective-permute-start | bytes 122888 | tf_op jit(solution)/shard_map/ppermute | solution.py:653
  106.7 4.4 %collective-permute-start.14 = (f32[80,128]{1,0:T(8,128)S(1)}, f32[80,128]{1,0:T(8,128)S(1)}, u32[]{:S(2)}, u32[]{:S(2)}) collective-permute-start(f32[80,128]{1,0:T(8,128)S(1)} %pad_maximum_fusion.2.recv0), channel_id=1, source_target_pairs={{0,4},{1,5},{2,6},{3,7},{4,0},{5,1},{6,2},{7,3},{8,12},{9,13},{10,... | collective-permute-start | bytes 122888 | tf_op jit(solution)/shard_map/ppermute | solution.py:653
  107.3 4.2 %collective-permute-start.13 = (f32[80,128]{1,0:T(8,128)S(1)}, f32[80,128]{1,0:T(8,128)S(1)}, u32[]{:S(2)}, u32[]{:S(2)}) collective-permute-start(f32[80,128]{1,0:T(8,128)S(1)} %pad_maximum_fusion.2.recv0), channel_id=1, source_target_pairs={{0,2},{1,3},{2,4},{3,5},{4,6},{5,7},{6,0},{7,1},{8,10},{9,11},{10,... | collective-permute-start | bytes 122888 | tf_op jit(solution)/shard_map/ppermute | solution.py:653
  134.3 13.2 %copy-start = (f32[6,256]{1,0:T(8,128)S(1)}, f32[6,256]{1,0:T(8,128)}, u32[]{:S(2)}) copy-start(f32[6,256]{1,0:T(8,128)} %right_ref.1) | copy-start | bytes 18436

commit v5 on v4

--- a/solution.py
+++ b/solution.py
@@ -62,7 +62,7 @@
 
 def start_kernel(
     right_hbm, diag_hbm, band_hbm, reach_hbm, rows_hbm, cols_hbm,
-    send_ref, masked_ref, extra_ref, rows_ref, cols_ref,
+    send_ref, masked_ref, rows_ref, cols_ref,
     right_ref, diag_ref, band_ref, reach_ref, pack, *sems,
 ):
     copies = [
@@ -102,12 +102,12 @@
         )
         store_as_tiles(pack, 0, turned)
         for j in range(3):
-            at = (3 * d + j) * 4
-            extra_ref[at : at + 4, :] = pack[0:4, j * LANES : (j + 1) * LANES]
+            at = 32 + (3 * d + j) * 4
+            send_ref[at : at + 4, :] = pack[0:4, j * LANES : (j + 1) * LANES]
     product = first * residual
     product = jnp.sum(product[:, 0:LANES] + product[:, LANES:256], axis=0, keepdims=True)
     product = jnp.sum(product, axis=1, keepdims=True)
-    extra_ref[48:49, :] = jnp.where(lane_ids(1) == 8, product, 0.0)
+    moment = jnp.where(lane_ids(1) == 8, product, 0.0)
     for copy in copies[2:6]:
         copy.wait()
     reach = reach_ref[...]
@@ -122,7 +122,10 @@
             block = masked_ref[j * 16 + i, :, LANES : 2 * LANES]
             packed = jnp.where(ids // 8 == i, right(block, i * 8 + 8), packed)
         send_ref[12 + 6 * j : 18 + 6 * j, :] = packed
-    send_ref[30:32, :] = jnp.zeros((2, LANES), F32)
+    rows = rows_ref[...]
+    send_ref[30:31, :] = moment
+    send_ref[30:31, 0:8] = ((rows // 4) * 8 + rows % 4).astype(F32)
+    send_ref[31:32, :] = jnp.zeros((1, LANES), F32)
 
 
 def blocks(refs):
@@ -315,7 +318,7 @@
             row_ref[c, 0:4, j * LANES : (j + 1) * LANES] = ref[at + 4 * j : at + 4 * j + 4, :]
     ids = lane_ids(6)
     for j in range(3):
-        at = 32 + 12 + 6 * j
+        at = 80 + 12 + 6 * j
         part = jnp.where(col % 2 == 1, recv0[at : at + 6, :], recv1[at : at + 6, :])
         for i in range(16):
             edge_ref[j * 16 + i] = jnp.where(ids >= 120, right(part, 120 - i * 8), 0.0)
@@ -326,7 +329,9 @@
     )
 
 
-def unpack(refs, pick_ref, inverse_ref):
+def layout_kernel(recv0, recv1, recv2, recv3, _, pick_ref, inverse_ref, moment_ref):
+    refs = (recv0, recv1, recv2, recv3)
+    total = jnp.zeros((1, LANES), F32)
     lane = lane_ids(1)
     group = lane % 64 // 8
     device = jnp.zeros((1, LANES), jnp.int32)
@@ -334,10 +339,11 @@
     low = lax.broadcasted_iota(jnp.int32, (8, LANES), 0) < 4
     for b, (c, ref, at) in enumerate(blocks(refs)):
         device = jnp.where(group == b, c, device)
-        target = jnp.where(group == b, right(ref[at + 39 : at + 40, :], 8 * b), target)
+        target = jnp.where(group == b, right(ref[at + 30 : at + 31, :], 8 * b), target)
+        total = total + ref[at + 30 : at + 31, :]
         parts = []
         for g in range(12):
-            first = at + 40 + 8 * (g // 2)
+            first = at + 32 + 8 * (g // 2)
             part = ref[first : first + 8, :]
             part = pltpu.roll(part, 4, 0) if g % 2 else part
             parts.append(jnp.where(low, part, 0.0))
@@ -356,13 +362,28 @@
         for half, wanted in enumerate((jnp.where(lane < 64, target, three), jnp.where(lane < 64, four, none))):
             found = (index == jnp.broadcast_to(wanted, (64, LANES))).astype(F32)
             pick_ref[j, :, half * LANES : (half + 1) * LANES] = found
+    sub = lax.broadcasted_iota(jnp.int32, (8, LANES), 0)
+    total = jnp.where(lane == 8, total, 0.0)
+    moment_ref[...] = jnp.where(sub == 0, jnp.broadcast_to(total, (8, LANES)), 0.0)
 
 
 def row_image(refs, pick_ref):
+    places = blocks(refs)
+
+    def rows_from(first):
+        return bfloat16_parts(
+            jnp.concatenate([ref[at + first : at + first + 8, :] for _, ref, at in places], axis=0)
+        )
+
+    three, four = rows_from(24), rows_from(32)
     parts = []
     for j in range(3):
-        rows = [ref[at + first : at + first + 8, :] for first in (8 * j, 24, 32) for _, ref, at in blocks(refs)]
-        parts.append(select_sum(pick_ref[j, :, 0:192], jnp.concatenate(rows, axis=0)))
+        pick = pick_ref[j, :, 0:192].astype(jnp.bfloat16)
+        high, middle, low = [
+            jnp.dot(pick, jnp.concatenate(x, axis=0), preferred_element_type=F32)
+            for x in zip(rows_from(8 * j), three, four)
+        ]
+        parts.append(low + middle + high)
     return jnp.concatenate(parts, axis=1).reshape(8, 8, 384)
 
 
@@ -388,23 +409,6 @@
     return moments
 
 
-def second_kernel(
-    recv0, recv1, recv2, recv3, before_ref, edge_ref, masked_ref, early_ref, late_ref, rows_ref, cols_ref, count_ref,
-    send_ref, band_ref, row_ref, image_ref, moment_ref, pick_ref, inverse_ref, *scratch,
-):
-    unpack((recv0, recv1, recv2, recv3), pick_ref, inverse_ref)
-    total = jnp.zeros((1, LANES), F32)
-    for _, ref, at in blocks((recv0, recv1, recv2, recv3)):
-        total = total + ref[at + 39 : at + 40, :]
-    sub = lax.broadcasted_iota(jnp.int32, (8, LANES), 0)
-    lane = lax.broadcasted_iota(jnp.int32, (8, LANES), 1)
-    moment_ref[2] = jnp.where((sub == 0) & (lane == 8), jnp.broadcast_to(total, (8, LANES)), 0.0)
-    advance((recv0, recv1, recv2, recv3), pick_ref, inverse_ref, before_ref, row_ref, image_ref, moment_ref, scratch[0])
-    ids_refs = (rows_ref, cols_ref, count_ref)
-    tiles_refs = (early_ref, late_ref)
-    send_frames(row_ref, edge_ref, masked_ref, tiles_refs, ids_refs, send_ref, band_ref, scratch)
-
-
 def next_kernel(
     recv0, recv1, recv2, recv3, before_ref, edge_ref, masked_ref, early_ref, late_ref, rows_ref, cols_ref, count_ref,
     pick_ref, inverse_ref, send_ref, band_ref, row_ref, image_ref, moment_ref, *scratch,
@@ -417,10 +421,10 @@
 
 def last_kernel(
     recv0, recv1, recv2, recv3, before_ref, edge_ref, masked_ref, early_ref, late_ref, rows_ref, cols_ref, count_ref,
-    pick_ref, inverse_ref, m1_ref, m2_ref, send_ref, band_ref, row_ref, image_ref, *scratch,
+    pick_ref, inverse_ref, m0_ref, m1_ref, m2_ref, send_ref, band_ref, row_ref, image_ref, *scratch,
 ):
     moments = advance((recv0, recv1, recv2, recv3), pick_ref, inverse_ref, before_ref, row_ref, image_ref, None, scratch[0])
-    known = [m1_ref[2], m1_ref[0], m1_ref[1], m2_ref[0], m2_ref[1]] + moments
+    known = [m0_ref[...], m1_ref[0], m1_ref[1], m2_ref[0], m2_ref[1]] + moments
     ids_refs = (rows_ref, cols_ref, count_ref)
     tiles_refs = (early_ref, late_ref)
     send_last(row_ref, edge_ref, masked_ref, tiles_refs, ids_refs, known, send_ref, band_ref, scratch)
@@ -457,9 +461,7 @@
             pack[8 * j + s : 8 * j + s + 1, :] = jnp.sum(part.T, axis=0, keepdims=True)
 
 
-def cols_kernel(recv_ref, early_ref, late_ref, row_ref, edge_ref, band_ref, cols_ref, count_ref, *rest):
-    extra_ref, rows_ref = rest[:2] if len(rest) == 3 else (None, None)
-    pack = rest[-1]
+def cols_kernel(recv_ref, early_ref, late_ref, row_ref, edge_ref, band_ref, cols_ref, count_ref, pack):
     frame = lax.axis_index("frames")
     col = lax.axis_index("cols")
     def piece_of(s):
@@ -479,16 +481,7 @@
         lanes = slice(j * LANES, (j + 1) * LANES)
         pack[24 + 4 * j : 28 + 4 * j, :] = terms[0:4, lanes]
         pack[36 + j : 37 + j, :] = onward[:, lanes]
-    misc = jnp.zeros((1, LANES), F32)
-    if extra_ref is not None:
-        misc = extra_ref[48:49, :]
-        for s in range(8):
-            r = rows_ref[0, s]
-            misc = jnp.where(lane_ids(1) == s, ((r // 4) * 8 + r % 4).astype(F32), misc)
-    pack[39:40, :] = misc
-
-    if extra_ref is not None:
-        pack[40:88, :] = extra_ref[0:48, :]
+    pack[39:40, :] = jnp.zeros((1, LANES), F32)
 
 
 def finish_kernel(
@@ -660,17 +653,17 @@
     stored = in_hbm(tiles.reshape(tiles.shape[2:]))
     inputs = (right_side, diag_blocks, jnp.transpose(band_blocks, (1, 2, 0, 3)), reach.reshape(1, -1))
     inputs += (tile_rows.reshape(1, 8), tile_cols.reshape(1, 8))
-    send, masked, extra, *ids = call(
+    send, masked, *ids = call(
         start_kernel,
         [HB] * 6,
-        [shape(32, LANES), shape(48, 6, 256), shape(56, LANES)]
+        [shape(80, LANES), shape(48, 6, 256)]
         + [shape(1, 8, kind=jnp.int32)] * 2,
         [(6, 256), (6, 6, 256), (6, 6, 8, 256), pltpu.VMEM((1, 256), jnp.int32), (8, 384)]
         + [sem] * 6,
         "start",
     )(*[in_hbm(x) for x in inputs])
     ids.append(tile_count)
-    recv = share(send)
+    recv = shared = share(send)
     (early,) = call(load_kernel, [HB], [shape(EARLY, 384, 384)], [sem] * EARLY, "load")(stored)
     frames_out = [shape(32, 8, 384), shape(8, 384), shape(8, 8, 384)]
     scratch = [(LANES, 384), (8, 256), (8, 256), (384, 512)]
@@ -686,25 +679,24 @@
         recv = exchange(send, "frames")
         (send,) = call(
             cols_kernel,
-            [VM] * 6 + [SM] * 2 + ([VM, SM] if it == 0 else []),
-            [shape(88 if it == 0 else 40, LANES)],
+            [VM] * 6 + [SM] * 2,
+            [shape(40, LANES)],
             [],
             "products",
-        )(recv, early, late, row, edges, band, *ids[1:], *((extra, ids[0]) if it == 0 else ()))
+        )(recv, early, late, row, edges, band, *ids[1:])
         recv = share(send)
+        if it == 0:
+            pick, inverse, moment = call(
+                layout_kernel,
+                [VM] * 5,
+                [shape(3, 64, 256), shape(6, 8, 8, 384), shape(8, LANES)],
+                [],
+                "layout",
+            )(*shared, send)
+            moments.append(moment)
         given = (*recv, row, edges, masked, early, late, *ids)
         specs = [VM] * 9 + [SM] * 3
-        if it == 0:
-            send, band, row, image, moment, pick, inverse = call(
-                second_kernel,
-                specs,
-                frames_out
-                + [shape(8, 384), shape(3, 8, LANES), shape(3, 64, 256), shape(6, 8, 8, 384)],
-                scratch,
-                "second",
-            )(*given)
-            moments.append(moment)
-        elif it + 2 < ITERS:
+        if it + 2 < ITERS:
             send, band, row, image, moment = call(
                 next_kernel,
                 specs + [VM] * 2,
@@ -716,7 +708,7 @@
         else:
             send, band, row, image = call(
                 last_kernel,
-                specs + [VM] * 4,
+                specs + [VM] * 5,
                 [shape(32, 40, LANES), shape(8, 384), shape(8, 8, 384), shape(8, 384)],
                 scratch + [(40, LANES)],
                 "last",

time: 149 us -> 149 us (level)
    pallas_call x1 -> x2, Pallas kernels: 1.79 us -> 3.59 us  [per_device(): call(next_kernel, specs + [VM] * 2, frames_out + [shape(8, 384), shape(2,...]
    pallas_call x6, Pallas kernels: 8.44 us -> 6.68 us  [the longest x3 3.39 us: per_device(): call(cols_kernel, [VM] * 6 + [SM] * 2, [shape(40, LANES)], [], 'products')]
where the time goes in v5:
time: 149 us; the launch traced here: 148 us
  blocking collectives  90 us (60%)
  starting transfers between devices  21.2 us (14%)
  waiting for transfers between devices  19 us (13%)
  Pallas kernels  16.8 us (11%)
    all_to_all x5, blocking collectives, exchange(): return lax.all_to_all(x, axis, 0, 0, tiled=True)  90 us
    ppermute x12, waiting for transfers between devices, share(): others.append(lax.ppermute(pair, 'cols', ahead))  15.6 us
    ppermute x4, starting transfers between devices, share(): pair = jnp.concatenate([x, lax.ppermute(x, 'cols', swap)], axis=0)  13.7 us
    ppermute x12, starting transfers between devices, share(): others.append(lax.ppermute(pair, 'cols', ahead))  7.49 us
    pallas_call x2, Pallas kernels, per_device(): call(next_kernel, specs + [VM] * 2, frames_out + [shape(8, 384), shape(2,...  3.59 us
    ppermute x4, waiting for transfers between devices, share(): pair = jnp.concatenate([x, lax.ppermute(x, 'cols', swap)], axis=0)  3.4 us
    pallas_call x3, Pallas kernels, per_device(): call(cols_kernel, [VM] * 6 + [SM] * 2, [shape(40, LANES)], [], 'products')  3.39 us
  transfers between devices with their start and end apart: 16, of which 15 were waited for; matrix products, arithmetic and copies ran while one was open for 0% of the time, Pallas kernels for 1%

profile of v5, /device:TPU:1, one launch (start us, length us, event | category | flops | bytes accessed | tf_op | source)
XLA Modules:
  0.0 148.3 jit_solution(13681633572502799246)
XLA Ops:
  0.6 1.3 start.1
  2.0 3.3 %collective-permute-start = (f32[80,128]{1,0:T(8,128)S(1)}, f32[80,128]{1,0:T(8,128)S(1)}, u32[]{:S(2)}, u32[]{:S(2)}) collective-permute-start(f32[80,128]{1,0:T(8,128)S(1)} %get-tuple-element.31), channel_id=1, source_target_pairs={{0,1},{1,0},{2,3},{3,2},{4,5},{5,4},{6,7},{7,6},{8,9},{9,8},{10,11... | collective-permute-start | bytes 122888 | tf_op jit(solution)/shard_map/ppermute | solution.py:642
  6.1 1.0 collective-permute-start.3
  8.8 1.8 %load.1.early_ref = f32[5,384,384]{2,1,0:T(8,128)S(1)} custom-call(f32[8,384,384]{2,1,0:T(8,128)} %bitcast.5), custom_call_target="tpu_custom_call" | custom-call | tf_op jit(solution)/shard_map/load/pallas_call | solution.py:667
  10.7 1.4 collective-permute-done.2.recv2
  12.0 2.5 %collective-permute-done.1.recv1 = f32[160,128]{1,0:T(8,128)S(1)} collective-permute-done((f32[160,128]{1,0:T(8,128)S(1)}, f32[160,128]{1,0:T(8,128)S(1)}, u32[]{:S(2)}, u32[]{:S(2)}) %collective-permute-start.1) | collective-permute-done | bytes 81952 | tf_op jit(solution)/shard_map/ppermute | solution.py:646
  14.5 2.4 %first.1 = (f32[32,8,384]{2,1,0:T(8,128)S(1)}, f32[8,384]{1,0:T(8,128)S(1)}, f32[8,8,384]{2,1,0:T(8,128)S(1)}, f32[48,6,128]{2,1,0:T(8,128)S(1)}, f32[3,384,384]{2,1,0:T(8,128)S(1)}) custom-call(f32[160,128]{1,0:T(8,128)S(1)} %constant_dynamic-update-slice_fusion.recv0, f32[160,128]{1,0:T(8,128)S(1)} %collective-permute-done.1.recv1, ...), custom_call_target="tpu_custom_call" | custom-call | tf_op jit(solution)/shard_map/first/pallas_call | solution.py:670
  16.9 24.7 %all_to_all.25.recv_ref = f32[32,8,384]{2,1,0:T(8,128)S(1)} all-to-all(f32[32,8,384]{2,1,0:T(8,128)S(1)} %get-tuple-element.35), channel_id=1, replica_groups=mesh['frames'=32,'cols'=8] {'frames'}, dimensions={0} | all-to-all | bytes 786432 | tf_op jit(solution)/shard_map/all_to_all | solution.py:637
  41.7 1.1 products.3._
  42.8 2.5 %collective-permute-start.4 = (f32[40,128]{1,0:T(8,128)S(1)}, f32[40,128]{1,0:T(8,128)S(1)}, u32[]{:S(2)}, u32[]{:S(2)}) collective-permute-start(f32[40,128]{1,0:T(8,128)S(1)} %products.3._), channel_id=1, source_target_pairs={{0,1},{1,0},{2,3},{3,2},{4,5},{5,4},{6,7},{7,6},{8,9},{9,8},{10,11... | collective-permute-start | bytes 61448 | tf_op jit(solution)/shard_map/ppermute | solution.py:642
  46.4 1.2 collective-permute-start.5
  47.7 1.3 collective-permute-done.7.recv3
  49.0 1.5 %collective-permute-done.6.recv2 = f32[80,128]{1,0:T(8,128)S(1)} collective-permute-done((f32[80,128]{1,0:T(8,128)S(1)}, f32[80,128]{1,0:T(8,128)S(1)}, u32[]{:S(2)}, u32[]{:S(2)}) %collective-permute-start.6) | collective-permute-done | bytes 40992 | tf_op jit(solution)/shard_map/ppermute | solution.py:646
  50.5 1.3 collective-permute-done.5.recv1
  51.8 1.8 %next.2 = (f32[32,8,384]{2,1,0:T(8,128)S(1)}, f32[8,384]{1,0:T(8,128)S(1)}, f32[8,8,384]{2,1,0:T(8,128)S(1)}, f32[8,384]{1,0:T(8,128)S(1)}, f32[2,8,128]{2,1,0:T(8,128)S(1)}) custom-call(f32[80,128]{1,0:T(8,128)S(1)} %pad_maximum_fusion.recv0, f32[80,128]{1,0:T(8,128)S(1)} %collective-permute-done.5.recv1, f32[80,128]{1,0:T(8,128)S(1)} %collective-permute-done.6.recv2, ...), custom_call_target="tpu_custom_call" | custom-call | tf_op jit(solution)/shard_map/next/pallas_call | solution.py:700
  53.6 16.7 %all_to_all.26.recv_ref = f32[32,8,384]{2,1,0:T(8,128)S(1)} all-to-all(f32[32,8,384]{2,1,0:T(8,128)S(1)} %get-tuple-element.42), channel_id=1, replica_groups=mesh['frames'=32,'cols'=8] {'frames'}, dimensions={0} | all-to-all | bytes 786432 | tf_op jit(solution)/shard_map/all_to_all | solution.py:637
  70.4 1.1 products.4
  71.5 3.4 %collective-permute-start.8 = (f32[40,128]{1,0:T(8,128)S(1)}, f32[40,128]{1,0:T(8,128)S(1)}, u32[]{:S(2)}, u32[]{:S(2)}) collective-permute-start(f32[40,128]{1,0:T(8,128)S(1)} %products.4), channel_id=1, source_target_pairs={{0,1},{1,0},{2,3},{3,2},{4,5},{5,4},{6,7},{7,6},{8,9},{9,8},{10,11... | collective-permute-start | bytes 61448 | tf_op jit(solution)/shard_map/ppermute | solution.py:642
  75.8 1.0 collective-permute-start.11
  77.6 1.1 collective-permute-done.11.recv3
  78.6 2.5 %collective-permute-done.10.recv2 = f32[80,128]{1,0:T(8,128)S(1)} collective-permute-done((f32[80,128]{1,0:T(8,128)S(1)}, f32[80,128]{1,0:T(8,128)S(1)}, u32[]{:S(2)}, u32[]{:S(2)}) %collective-permute-start.10) | collective-permute-done | bytes 40992 | tf_op jit(solution)/shard_map/ppermute | solution.py:646
  81.7 1.8 %next.3 = (f32[32,8,384]{2,1,0:T(8,128)S(1)}, f32[8,384]{1,0:T(8,128)S(1)}, f32[8,8,384]{2,1,0:T(8,128)S(1)}, f32[8,384]{1,0:T(8,128)S(1)}, f32[2,8,128]{2,1,0:T(8,128)S(1)}) custom-call(f32[80,128]{1,0:T(8,128)S(1)} %pad_maximum_fusion.1.recv0, f32[80,128]{1,0:T(8,128)S(1)} %collective-permute-done.9.recv1, f32[80,128]{1,0:T(8,128)S(1)} %collective-permute-done.10.recv2, ...), custom_call_target="tpu_custom_call" | custom-call | tf_op jit(solution)/shard_map/next/pallas_call | solution.py:700
  83.4 15.7 %all_to_all.27.recv_ref = f32[32,8,384]{2,1,0:T(8,128)S(1)} all-to-all(f32[32,8,384]{2,1,0:T(8,128)S(1)} %get-tuple-element.45), channel_id=1, replica_groups=mesh['frames'=32,'cols'=8] {'frames'}, dimensions={0} | all-to-all | bytes 786432 | tf_op jit(solution)/shard_map/all_to_all | solution.py:637
  99.2 1.1 products.5
  100.3 4.5 %collective-permute-start.12 = (f32[40,128]{1,0:T(8,128)S(1)}, f32[40,128]{1,0:T(8,128)S(1)}, u32[]{:S(2)}, u32[]{:S(2)}) collective-permute-start(f32[40,128]{1,0:T(8,128)S(1)} %products.5), channel_id=1, source_target_pairs={{0,1},{1,0},{2,3},{3,2},{4,5},{5,4},{6,7},{7,6},{8,9},{9,8},{10,11... | collective-permute-start | bytes 61448 | tf_op jit(solution)/shard_map/ppermute | solution.py:642
  105.6 1.0 collective-permute-start.15
  108.4 2.5 %collective-permute-done.14.recv2 = f32[80,128]{1,0:T(8,128)S(1)} collective-permute-done((f32[80,128]{1,0:T(8,128)S(1)}, f32[80,128]{1,0:T(8,128)S(1)}, u32[]{:S(2)}, u32[]{:S(2)}) %collective-permute-start.14) | collective-permute-done | bytes 40992 | tf_op jit(solution)/shard_map/ppermute | solution.py:646
  111.3 1.9 %last.1 = (f32[32,40,128]{2,1,0:T(8,128)S(1)}, f32[8,384]{1,0:T(8,128)S(1)}, f32[8,8,384]{2,1,0:T(8,128)S(1)}, f32[8,384]{1,0:T(8,128)S(1)}) custom-call(f32[80,128]{1,0:T(8,128)S(1)} %pad_maximum_fusion.2.recv0, f32[80,128]{1,0:T(8,128)S(1)} %collective-permute-done.13.recv1, f32[80,128]{1,0:T(8,128)S(1)} %collective-permute-done.14.recv2, ...), custom_call_target="tpu_custom_call" | custom-call | tf_op jit(solution)/shard_map/last/pallas_call | solution.py:709
  113.2 21.0 %all_to_all.28.recv_ref = f32[32,40,128]{2,1,0:T(8,128)S(1)} all-to-all(f32[32,40,128]{2,1,0:T(8,128)S(1)} %get-tuple-element.51), channel_id=1, replica_groups=mesh['frames'=32,'cols'=8] {'frames'}, dimensions={0} | all-to-all | bytes 1310720 | tf_op jit(solution)/shard_map/all_to_all | solution.py:637
  134.2 1.4 finish.1
  135.6 11.8 %all_to_all.29.recv_ref = f32[8,16,128]{2,1,0:T(8,128)S(1)} all-to-all(f32[8,16,128]{2,1,0:T(8,128)S(1)} %get-tuple-element.54), channel_id=1, replica_groups=mesh['frames'=32,'cols'=8] {'cols'}, dimensions={0} | all-to-all | bytes 131072 | tf_op jit(solution)/shard_map/all_to_all | solution.py:637
  147.4 0.9 end.1
  (24 shorter events, 8.4 us)
Async XLA Ops:
  2.0 4.2 %collective-permute-start = (f32[80,128]{1,0:T(8,128)S(1)}, f32[80,128]{1,0:T(8,128)S(1)}, u32[]{:S(2)}, u32[]{:S(2)}) collective-permute-start(f32[80,128]{1,0:T(8,128)S(1)} %get-tuple-element.31), channel_id=1, source_target_pairs={{0,1},{1,0},{2,3},{3,2},{4,5},{5,4},{6,7},{7,6},{8,9},{9,8},{10,11... | collective-permute-start | bytes 122888 | tf_op jit(solution)/shard_map/ppermute | solution.py:642
  6.1 4.6 %collective-permute-start.3 = (f32[160,128]{1,0:T(8,128)S(1)}, f32[160,128]{1,0:T(8,128)S(1)}, u32[]{:S(2)}, u32[]{:S(2)}) collective-permute-start(f32[160,128]{1,0:T(8,128)S(1)} %constant_dynamic-update-slice_fusion.recv0), channel_id=1, source_target_pairs={{0,6},{1,7},{2,0},{3,1},{4,2},{5,3},{6,4},{7,5},{8,14},{9,15},{10,... | collective-permute-start | bytes 245768 | tf_op jit(solution)/shard_map/ppermute | solution.py:646
  7.1 4.9 %collective-permute-start.2 = (f32[160,128]{1,0:T(8,128)S(1)}, f32[160,128]{1,0:T(8,128)S(1)}, u32[]{:S(2)}, u32[]{:S(2)}) collective-permute-start(f32[160,128]{1,0:T(8,128)S(1)} %constant_dynamic-update-slice_fusion.recv0), channel_id=1, source_target_pairs={{0,4},{1,5},{2,6},{3,7},{4,0},{5,1},{6,2},{7,3},{8,12},{9,13},{10,... | collective-permute-start | bytes 245768 | tf_op jit(solution)/shard_map/ppermute | solution.py:646
  7.5 7.0 %collective-permute-start.1 = (f32[160,128]{1,0:T(8,128)S(1)}, f32[160,128]{1,0:T(8,128)S(1)}, u32[]{:S(2)}, u32[]{:S(2)}) collective-permute-start(f32[160,128]{1,0:T(8,128)S(1)} %constant_dynamic-update-slice_fusion.recv0), channel_id=1, source_target_pairs={{0,2},{1,3},{2,4},{3,5},{4,6},{5,7},{6,0},{7,1},{8,10},{9,11},{10,... | collective-permute-start | bytes 245768 | tf_op jit(solution)/shard_map/ppermute | solution.py:646
  42.8 3.3 %collective-permute-start.4 = (f32[40,128]{1,0:T(8,128)S(1)}, f32[40,128]{1,0:T(8,128)S(1)}, u32[]{:S(2)}, u32[]{:S(2)}) collective-permute-start(f32[40,128]{1,0:T(8,128)S(1)} %products.3._), channel_id=1, source_target_pairs={{0,1},{1,0},{2,3},{3,2},{4,5},{5,4},{6,7},{7,6},{8,9},{9,8},{10,11... | collective-permute-start | bytes 61448 | tf_op jit(solution)/shard_map/ppermute | solution.py:642
  46.1 2.9 %collective-permute-start.7 = (f32[80,128]{1,0:T(8,128)S(1)}, f32[80,128]{1,0:T(8,128)S(1)}, u32[]{:S(2)}, u32[]{:S(2)}) collective-permute-start(f32[80,128]{1,0:T(8,128)S(1)} %pad_maximum_fusion.recv0), channel_id=1, source_target_pairs={{0,6},{1,7},{2,0},{3,1},{4,2},{5,3},{6,4},{7,5},{8,14},{9,15},{10,... | collective-permute-start | bytes 122888 | tf_op jit(solution)/shard_map/ppermute | solution.py:646
  46.1 4.4 %collective-permute-start.6 = (f32[80,128]{1,0:T(8,128)S(1)}, f32[80,128]{1,0:T(8,128)S(1)}, u32[]{:S(2)}, u32[]{:S(2)}) collective-permute-start(f32[80,128]{1,0:T(8,128)S(1)} %pad_maximum_fusion.recv0), channel_id=1, source_target_pairs={{0,4},{1,5},{2,6},{3,7},{4,0},{5,1},{6,2},{7,3},{8,12},{9,13},{10,... | collective-permute-start | bytes 122888 | tf_op jit(solution)/shard_map/ppermute | solution.py:646
  46.4 5.4 %collective-permute-start.5 = (f32[80,128]{1,0:T(8,128)S(1)}, f32[80,128]{1,0:T(8,128)S(1)}, u32[]{:S(2)}, u32[]{:S(2)}) collective-permute-start(f32[80,128]{1,0:T(8,128)S(1)} %pad_maximum_fusion.recv0), channel_id=1, source_target_pairs={{0,2},{1,3},{2,4},{3,5},{4,6},{5,7},{6,0},{7,1},{8,10},{9,11},{10,... | collective-permute-start | bytes 122888 | tf_op jit(solution)/shard_map/ppermute | solution.py:646
  71.5 4.3 %collective-permute-start.8 = (f32[40,128]{1,0:T(8,128)S(1)}, f32[40,128]{1,0:T(8,128)S(1)}, u32[]{:S(2)}, u32[]{:S(2)}) collective-permute-start(f32[40,128]{1,0:T(8,128)S(1)} %products.4), channel_id=1, source_target_pairs={{0,1},{1,0},{2,3},{3,2},{4,5},{5,4},{6,7},{7,6},{8,9},{9,8},{10,11... | collective-permute-start | bytes 61448 | tf_op jit(solution)/shard_map/ppermute | solution.py:642
  75.8 2.9 %collective-permute-start.11 = (f32[80,128]{1,0:T(8,128)S(1)}, f32[80,128]{1,0:T(8,128)S(1)}, u32[]{:S(2)}, u32[]{:S(2)}) collective-permute-start(f32[80,128]{1,0:T(8,128)S(1)} %pad_maximum_fusion.1.recv0), channel_id=1, source_target_pairs={{0,6},{1,7},{2,0},{3,1},{4,2},{5,3},{6,4},{7,5},{8,14},{9,15},{10,... | collective-permute-start | bytes 122888 | tf_op jit(solution)/shard_map/ppermute | solution.py:646
  76.8 4.4 %collective-permute-start.10 = (f32[80,128]{1,0:T(8,128)S(1)}, f32[80,128]{1,0:T(8,128)S(1)}, u32[]{:S(2)}, u32[]{:S(2)}) collective-permute-start(f32[80,128]{1,0:T(8,128)S(1)} %pad_maximum_fusion.1.recv0), channel_id=1, source_target_pairs={{0,4},{1,5},{2,6},{3,7},{4,0},{5,1},{6,2},{7,3},{8,12},{9,13},{10,... | collective-permute-start | bytes 122888 | tf_op jit(solution)/shard_map/ppermute | solution.py:646
  77.6 4.1 %collective-permute-start.9 = (f32[80,128]{1,0:T(8,128)S(1)}, f32[80,128]{1,0:T(8,128)S(1)}, u32[]{:S(2)}, u32[]{:S(2)}) collective-permute-start(f32[80,128]{1,0:T(8,128)S(1)} %pad_maximum_fusion.1.recv0), channel_id=1, source_target_pairs={{0,2},{1,3},{2,4},{3,5},{4,6},{5,7},{6,0},{7,1},{8,10},{9,11},{10,... | collective-permute-start | bytes 122888 | tf_op jit(solution)/shard_map/ppermute | solution.py:646
  100.3 5.3 %collective-permute-start.12 = (f32[40,128]{1,0:T(8,128)S(1)}, f32[40,128]{1,0:T(8,128)S(1)}, u32[]{:S(2)}, u32[]{:S(2)}) collective-permute-start(f32[40,128]{1,0:T(8,128)S(1)} %products.5), channel_id=1, source_target_pairs={{0,1},{1,0},{2,3},{3,2},{4,5},{5,4},{6,7},{7,6},{8,9},{9,8},{10,11... | collective-permute-start | bytes 61448 | tf_op jit(solution)/shard_map/ppermute | solution.py:642
  105.6 2.9 %collective-permute-start.15 = (f32[80,128]{1,0:T(8,128)S(1)}, f32[80,128]{1,0:T(8,128)S(1)}, u32[]{:S(2)}, u32[]{:S(2)}) collective-permute-start(f32[80,128]{1,0:T(8,128)S(1)} %pad_maximum_fusion.2.recv0), channel_id=1, source_target_pairs={{0,6},{1,7},{2,0},{3,1},{4,2},{5,3},{6,4},{7,5},{8,14},{9,15},{10,... | collective-permute-start | bytes 122888 | tf_op jit(solution)/shard_map/ppermute | solution.py:646
  106.6 4.4 %collective-permute-start.14 = (f32[80,128]{1,0:T(8,128)S(1)}, f32[80,128]{1,0:T(8,128)S(1)}, u32[]{:S(2)}, u32[]{:S(2)}) collective-permute-start(f32[80,128]{1,0:T(8,128)S(1)} %pad_maximum_fusion.2.recv0), channel_id=1, source_target_pairs={{0,4},{1,5},{2,6},{3,7},{4,0},{5,1},{6,2},{7,3},{8,12},{9,13},{10,... | collective-permute-start | bytes 122888 | tf_op jit(solution)/shard_map/ppermute | solution.py:646
  107.2 4.2 %collective-permute-start.13 = (f32[80,128]{1,0:T(8,128)S(1)}, f32[80,128]{1,0:T(8,128)S(1)}, u32[]{:S(2)}, u32[]{:S(2)}) collective-permute-start(f32[80,128]{1,0:T(8,128)S(1)} %pad_maximum_fusion.2.recv0), channel_id=1, source_target_pairs={{0,2},{1,3},{2,4},{3,5},{4,6},{5,7},{6,0},{7,1},{8,10},{9,11},{10,... | collective-permute-start | bytes 122888 | tf_op jit(solution)/shard_map/ppermute | solution.py:646
  134.2 13.2 %copy-start = (f32[6,256]{1,0:T(8,128)S(1)}, f32[6,256]{1,0:T(8,128)}, u32[]{:S(2)}) copy-start(f32[6,256]{1,0:T(8,128)} %right_ref.1) | copy-start | bytes 18436

commit v6 on v5

--- a/solution.py
+++ b/solution.py
@@ -11,7 +11,7 @@
 LANES = 128
 F32 = jnp.float32
 ROWS = ("frames", "cols")
-EARLY = 5
+EARLY = 7
 
 
 def lane_ids(rows):

time: 149 us -> 149 us (level)
  transfers between devices with their start and end apart: 16 -> 16, of which waited for: 15 -> 15; matrix products, arithmetic and copies ran while one was open for 0% -> 0% of each run, Pallas kernels for 1% -> 2%
where the time goes in v6:
time: 149 us; the launch traced here: 148 us
  blocking collectives  89.9 us (60%)
  starting transfers between devices  21.2 us (14%)
  waiting for transfers between devices  18.6 us (12%)
  Pallas kernels  17 us (11%)
    all_to_all x5, blocking collectives, exchange(): return lax.all_to_all(x, axis, 0, 0, tiled=True)  89.9 us
    ppermute x12, waiting for transfers between devices, share(): others.append(lax.ppermute(pair, 'cols', ahead))  15.2 us
    ppermute x4, starting transfers between devices, share(): pair = jnp.concatenate([x, lax.ppermute(x, 'cols', swap)], axis=0)  13.7 us
    ppermute x12, starting transfers between devices, share(): others.append(lax.ppermute(pair, 'cols', ahead))  7.47 us
    pallas_call x2, Pallas kernels, per_device(): call(next_kernel, specs + [VM] * 2, frames_out + [shape(8, 384), shape(2,...  3.58 us
    ppermute x4, waiting for transfers between devices, share(): pair = jnp.concatenate([x, lax.ppermute(x, 'cols', swap)], axis=0)  3.4 us
    pallas_call x3, Pallas kernels, per_device(): call(cols_kernel, [VM] * 6 + [SM] * 2, [shape(40, LANES)], [], 'products')  3.38 us
  transfers between devices with their start and end apart: 16, of which 15 were waited for; matrix products, arithmetic and copies ran while one was open for 0% of the time, Pallas kernels for 2%

profile of v6, /device:TPU:1, one launch (start us, length us, event | category | flops | bytes accessed | tf_op | source)
XLA Modules:
  0.0 148.1 jit_solution(1641079473038578329)
XLA Ops:
  0.6 1.3 start.1
  2.0 3.3 %collective-permute-start = (f32[80,128]{1,0:T(8,128)S(1)}, f32[80,128]{1,0:T(8,128)S(1)}, u32[]{:S(2)}, u32[]{:S(2)}) collective-permute-start(f32[80,128]{1,0:T(8,128)S(1)} %get-tuple-element.31), channel_id=1, source_target_pairs={{0,1},{1,0},{2,3},{3,2},{4,5},{5,4},{6,7},{7,6},{8,9},{9,8},{10,11... | collective-permute-start | bytes 122888 | tf_op jit(solution)/shard_map/ppermute | solution.py:642
  6.1 1.0 collective-permute-start.3
  8.8 2.2 %load.1.early_ref = f32[7,384,384]{2,1,0:T(8,128)S(1)} custom-call(f32[8,384,384]{2,1,0:T(8,128)} %bitcast.5), custom_call_target="tpu_custom_call" | custom-call | tf_op jit(solution)/shard_map/load/pallas_call | solution.py:667
  11.0 1.0 collective-permute-done.2.recv2
  12.0 2.5 %collective-permute-done.1.recv1 = f32[160,128]{1,0:T(8,128)S(1)} collective-permute-done((f32[160,128]{1,0:T(8,128)S(1)}, f32[160,128]{1,0:T(8,128)S(1)}, u32[]{:S(2)}, u32[]{:S(2)}) %collective-permute-start.1) | collective-permute-done | bytes 81952 | tf_op jit(solution)/shard_map/ppermute | solution.py:646
  14.5 2.3 %first.1 = (f32[32,8,384]{2,1,0:T(8,128)S(1)}, f32[8,384]{1,0:T(8,128)S(1)}, f32[8,8,384]{2,1,0:T(8,128)S(1)}, f32[48,6,128]{2,1,0:T(8,128)S(1)}, f32[1,384,384]{2,1,0:T(8,128)S(1)}) custom-call(f32[160,128]{1,0:T(8,128)S(1)} %constant_dynamic-update-slice_fusion.recv0, f32[160,128]{1,0:T(8,128)S(1)} %collective-permute-done.1.recv1, ...), custom_call_target="tpu_custom_call" | custom-call | tf_op jit(solution)/shard_map/first/pallas_call | solution.py:670
  16.8 24.7 %all_to_all.25.recv_ref = f32[32,8,384]{2,1,0:T(8,128)S(1)} all-to-all(f32[32,8,384]{2,1,0:T(8,128)S(1)} %get-tuple-element.35), channel_id=1, replica_groups=mesh['frames'=32,'cols'=8] {'frames'}, dimensions={0} | all-to-all | bytes 786432 | tf_op jit(solution)/shard_map/all_to_all | solution.py:637
  41.5 1.1 products.3._
  42.7 2.5 %collective-permute-start.4 = (f32[40,128]{1,0:T(8,128)S(1)}, f32[40,128]{1,0:T(8,128)S(1)}, u32[]{:S(2)}, u32[]{:S(2)}) collective-permute-start(f32[40,128]{1,0:T(8,128)S(1)} %products.3._), channel_id=1, source_target_pairs={{0,1},{1,0},{2,3},{3,2},{4,5},{5,4},{6,7},{7,6},{8,9},{9,8},{10,11... | collective-permute-start | bytes 61448 | tf_op jit(solution)/shard_map/ppermute | solution.py:642
  46.3 1.2 collective-permute-start.5
  47.6 1.3 collective-permute-done.7.recv3
  48.9 1.5 %collective-permute-done.6.recv2 = f32[80,128]{1,0:T(8,128)S(1)} collective-permute-done((f32[80,128]{1,0:T(8,128)S(1)}, f32[80,128]{1,0:T(8,128)S(1)}, u32[]{:S(2)}, u32[]{:S(2)}) %collective-permute-start.6) | collective-permute-done | bytes 40992 | tf_op jit(solution)/shard_map/ppermute | solution.py:646
  50.4 1.3 collective-permute-done.5.recv1
  51.7 1.8 %next.2 = (f32[32,8,384]{2,1,0:T(8,128)S(1)}, f32[8,384]{1,0:T(8,128)S(1)}, f32[8,8,384]{2,1,0:T(8,128)S(1)}, f32[8,384]{1,0:T(8,128)S(1)}, f32[2,8,128]{2,1,0:T(8,128)S(1)}) custom-call(f32[80,128]{1,0:T(8,128)S(1)} %pad_maximum_fusion.recv0, f32[80,128]{1,0:T(8,128)S(1)} %collective-permute-done.5.recv1, f32[80,128]{1,0:T(8,128)S(1)} %collective-permute-done.6.recv2, ...), custom_call_target="tpu_custom_call" | custom-call | tf_op jit(solution)/shard_map/next/pallas_call | solution.py:700
  53.5 16.7 %all_to_all.26.recv_ref = f32[32,8,384]{2,1,0:T(8,128)S(1)} all-to-all(f32[32,8,384]{2,1,0:T(8,128)S(1)} %get-tuple-element.42), channel_id=1, replica_groups=mesh['frames'=32,'cols'=8] {'frames'}, dimensions={0} | all-to-all | bytes 786432 | tf_op jit(solution)/shard_map/all_to_all | solution.py:637
  70.2 1.1 products.4
  71.3 3.5 %collective-permute-start.8 = (f32[40,128]{1,0:T(8,128)S(1)}, f32[40,128]{1,0:T(8,128)S(1)}, u32[]{:S(2)}, u32[]{:S(2)}) collective-permute-start(f32[40,128]{1,0:T(8,128)S(1)} %products.4), channel_id=1, source_target_pairs={{0,1},{1,0},{2,3},{3,2},{4,5},{5,4},{6,7},{7,6},{8,9},{9,8},{10,11... | collective-permute-start | bytes 61448 | tf_op jit(solution)/shard_map/ppermute | solution.py:642
  75.6 1.0 collective-permute-start.11
  77.5 1.0 collective-permute-done.11.recv3
  78.5 2.5 %collective-permute-done.10.recv2 = f32[80,128]{1,0:T(8,128)S(1)} collective-permute-done((f32[80,128]{1,0:T(8,128)S(1)}, f32[80,128]{1,0:T(8,128)S(1)}, u32[]{:S(2)}, u32[]{:S(2)}) %collective-permute-start.10) | collective-permute-done | bytes 40992 | tf_op jit(solution)/shard_map/ppermute | solution.py:646
  81.5 1.8 %next.3 = (f32[32,8,384]{2,1,0:T(8,128)S(1)}, f32[8,384]{1,0:T(8,128)S(1)}, f32[8,8,384]{2,1,0:T(8,128)S(1)}, f32[8,384]{1,0:T(8,128)S(1)}, f32[2,8,128]{2,1,0:T(8,128)S(1)}) custom-call(f32[80,128]{1,0:T(8,128)S(1)} %pad_maximum_fusion.1.recv0, f32[80,128]{1,0:T(8,128)S(1)} %collective-permute-done.9.recv1, f32[80,128]{1,0:T(8,128)S(1)} %collective-permute-done.10.recv2, ...), custom_call_target="tpu_custom_call" | custom-call | tf_op jit(solution)/shard_map/next/pallas_call | solution.py:700
  83.3 15.7 %all_to_all.27.recv_ref = f32[32,8,384]{2,1,0:T(8,128)S(1)} all-to-all(f32[32,8,384]{2,1,0:T(8,128)S(1)} %get-tuple-element.45), channel_id=1, replica_groups=mesh['frames'=32,'cols'=8] {'frames'}, dimensions={0} | all-to-all | bytes 786432 | tf_op jit(solution)/shard_map/all_to_all | solution.py:637
  99.0 1.1 products.5
  100.1 4.5 %collective-permute-start.12 = (f32[40,128]{1,0:T(8,128)S(1)}, f32[40,128]{1,0:T(8,128)S(1)}, u32[]{:S(2)}, u32[]{:S(2)}) collective-permute-start(f32[40,128]{1,0:T(8,128)S(1)} %products.5), channel_id=1, source_target_pairs={{0,1},{1,0},{2,3},{3,2},{4,5},{5,4},{6,7},{7,6},{8,9},{9,8},{10,11... | collective-permute-start | bytes 61448 | tf_op jit(solution)/shard_map/ppermute | solution.py:642
  105.4 0.9 collective-permute-start.15
  108.3 2.5 %collective-permute-done.14.recv2 = f32[80,128]{1,0:T(8,128)S(1)} collective-permute-done((f32[80,128]{1,0:T(8,128)S(1)}, f32[80,128]{1,0:T(8,128)S(1)}, u32[]{:S(2)}, u32[]{:S(2)}) %collective-permute-start.14) | collective-permute-done | bytes 40992 | tf_op jit(solution)/shard_map/ppermute | solution.py:646
  111.2 1.8 %last.1 = (f32[32,40,128]{2,1,0:T(8,128)S(1)}, f32[8,384]{1,0:T(8,128)S(1)}, f32[8,8,384]{2,1,0:T(8,128)S(1)}, f32[8,384]{1,0:T(8,128)S(1)}) custom-call(f32[80,128]{1,0:T(8,128)S(1)} %pad_maximum_fusion.2.recv0, f32[80,128]{1,0:T(8,128)S(1)} %collective-permute-done.13.recv1, f32[80,128]{1,0:T(8,128)S(1)} %collective-permute-done.14.recv2, ...), custom_call_target="tpu_custom_call" | custom-call | tf_op jit(solution)/shard_map/last/pallas_call | solution.py:709
  113.1 21.0 %all_to_all.28.recv_ref = f32[32,40,128]{2,1,0:T(8,128)S(1)} all-to-all(f32[32,40,128]{2,1,0:T(8,128)S(1)} %get-tuple-element.51), channel_id=1, replica_groups=mesh['frames'=32,'cols'=8] {'frames'}, dimensions={0} | all-to-all | bytes 1310720 | tf_op jit(solution)/shard_map/all_to_all | solution.py:637
  134.0 1.4 finish.1
  135.4 11.8 %all_to_all.29.recv_ref = f32[8,16,128]{2,1,0:T(8,128)S(1)} all-to-all(f32[8,16,128]{2,1,0:T(8,128)S(1)} %get-tuple-element.54), channel_id=1, replica_groups=mesh['frames'=32,'cols'=8] {'cols'}, dimensions={0} | all-to-all | bytes 131072 | tf_op jit(solution)/shard_map/all_to_all | solution.py:637
  147.3 0.9 end.1
  (24 shorter events, 8.5 us)
Async XLA Ops:
  2.0 4.2 %collective-permute-start = (f32[80,128]{1,0:T(8,128)S(1)}, f32[80,128]{1,0:T(8,128)S(1)}, u32[]{:S(2)}, u32[]{:S(2)}) collective-permute-start(f32[80,128]{1,0:T(8,128)S(1)} %get-tuple-element.31), channel_id=1, source_target_pairs={{0,1},{1,0},{2,3},{3,2},{4,5},{5,4},{6,7},{7,6},{8,9},{9,8},{10,11... | collective-permute-start | bytes 122888 | tf_op jit(solution)/shard_map/ppermute | solution.py:642
  6.1 4.9 %collective-permute-start.3 = (f32[160,128]{1,0:T(8,128)S(1)}, f32[160,128]{1,0:T(8,128)S(1)}, u32[]{:S(2)}, u32[]{:S(2)}) collective-permute-start(f32[160,128]{1,0:T(8,128)S(1)} %constant_dynamic-update-slice_fusion.recv0), channel_id=1, source_target_pairs={{0,6},{1,7},{2,0},{3,1},{4,2},{5,3},{6,4},{7,5},{8,14},{9,15},{10,... | collective-permute-start | bytes 245768 | tf_op jit(solution)/shard_map/ppermute | solution.py:646
  7.1 4.9 %collective-permute-start.2 = (f32[160,128]{1,0:T(8,128)S(1)}, f32[160,128]{1,0:T(8,128)S(1)}, u32[]{:S(2)}, u32[]{:S(2)}) collective-permute-start(f32[160,128]{1,0:T(8,128)S(1)} %constant_dynamic-update-slice_fusion.recv0), channel_id=1, source_target_pairs={{0,4},{1,5},{2,6},{3,7},{4,0},{5,1},{6,2},{7,3},{8,12},{9,13},{10,... | collective-permute-start | bytes 245768 | tf_op jit(solution)/shard_map/ppermute | solution.py:646
  7.5 7.0 %collective-permute-start.1 = (f32[160,128]{1,0:T(8,128)S(1)}, f32[160,128]{1,0:T(8,128)S(1)}, u32[]{:S(2)}, u32[]{:S(2)}) collective-permute-start(f32[160,128]{1,0:T(8,128)S(1)} %constant_dynamic-update-slice_fusion.recv0), channel_id=1, source_target_pairs={{0,2},{1,3},{2,4},{3,5},{4,6},{5,7},{6,0},{7,1},{8,10},{9,11},{10,... | collective-permute-start | bytes 245768 | tf_op jit(solution)/shard_map/ppermute | solution.py:646
  42.7 3.4 %collective-permute-start.4 = (f32[40,128]{1,0:T(8,128)S(1)}, f32[40,128]{1,0:T(8,128)S(1)}, u32[]{:S(2)}, u32[]{:S(2)}) collective-permute-start(f32[40,128]{1,0:T(8,128)S(1)} %products.3._), channel_id=1, source_target_pairs={{0,1},{1,0},{2,3},{3,2},{4,5},{5,4},{6,7},{7,6},{8,9},{9,8},{10,11... | collective-permute-start | bytes 61448 | tf_op jit(solution)/shard_map/ppermute | solution.py:642
  46.0 2.9 %collective-permute-start.7 = (f32[80,128]{1,0:T(8,128)S(1)}, f32[80,128]{1,0:T(8,128)S(1)}, u32[]{:S(2)}, u32[]{:S(2)}) collective-permute-start(f32[80,128]{1,0:T(8,128)S(1)} %pad_maximum_fusion.recv0), channel_id=1, source_target_pairs={{0,6},{1,7},{2,0},{3,1},{4,2},{5,3},{6,4},{7,5},{8,14},{9,15},{10,... | collective-permute-start | bytes 122888 | tf_op jit(solution)/shard_map/ppermute | solution.py:646
  46.0 4.4 %collective-permute-start.6 = (f32[80,128]{1,0:T(8,128)S(1)}, f32[80,128]{1,0:T(8,128)S(1)}, u32[]{:S(2)}, u32[]{:S(2)}) collective-permute-start(f32[80,128]{1,0:T(8,128)S(1)} %pad_maximum_fusion.recv0), channel_id=1, source_target_pairs={{0,4},{1,5},{2,6},{3,7},{4,0},{5,1},{6,2},{7,3},{8,12},{9,13},{10,... | collective-permute-start | bytes 122888 | tf_op jit(solution)/shard_map/ppermute | solution.py:646
  46.3 5.4 %collective-permute-start.5 = (f32[80,128]{1,0:T(8,128)S(1)}, f32[80,128]{1,0:T(8,128)S(1)}, u32[]{:S(2)}, u32[]{:S(2)}) collective-permute-start(f32[80,128]{1,0:T(8,128)S(1)} %pad_maximum_fusion.recv0), channel_id=1, source_target_pairs={{0,2},{1,3},{2,4},{3,5},{4,6},{5,7},{6,0},{7,1},{8,10},{9,11},{10,... | collective-permute-start | bytes 122888 | tf_op jit(solution)/shard_map/ppermute | solution.py:646
  71.3 4.3 %collective-permute-start.8 = (f32[40,128]{1,0:T(8,128)S(1)}, f32[40,128]{1,0:T(8,128)S(1)}, u32[]{:S(2)}, u32[]{:S(2)}) collective-permute-start(f32[40,128]{1,0:T(8,128)S(1)} %products.4), channel_id=1, source_target_pairs={{0,1},{1,0},{2,3},{3,2},{4,5},{5,4},{6,7},{7,6},{8,9},{9,8},{10,11... | collective-permute-start | bytes 61448 | tf_op jit(solution)/shard_map/ppermute | solution.py:642
  75.6 2.9 %collective-permute-start.11 = (f32[80,128]{1,0:T(8,128)S(1)}, f32[80,128]{1,0:T(8,128)S(1)}, u32[]{:S(2)}, u32[]{:S(2)}) collective-permute-start(f32[80,128]{1,0:T(8,128)S(1)} %pad_maximum_fusion.1.recv0), channel_id=1, source_target_pairs={{0,6},{1,7},{2,0},{3,1},{4,2},{5,3},{6,4},{7,5},{8,14},{9,15},{10,... | collective-permute-start | bytes 122888 | tf_op jit(solution)/shard_map/ppermute | solution.py:646
  76.7 4.4 %collective-permute-start.10 = (f32[80,128]{1,0:T(8,128)S(1)}, f32[80,128]{1,0:T(8,128)S(1)}, u32[]{:S(2)}, u32[]{:S(2)}) collective-permute-start(f32[80,128]{1,0:T(8,128)S(1)} %pad_maximum_fusion.1.recv0), channel_id=1, source_target_pairs={{0,4},{1,5},{2,6},{3,7},{4,0},{5,1},{6,2},{7,3},{8,12},{9,13},{10,... | collective-permute-start | bytes 122888 | tf_op jit(solution)/shard_map/ppermute | solution.py:646
  77.5 4.1 %collective-permute-start.9 = (f32[80,128]{1,0:T(8,128)S(1)}, f32[80,128]{1,0:T(8,128)S(1)}, u32[]{:S(2)}, u32[]{:S(2)}) collective-permute-start(f32[80,128]{1,0:T(8,128)S(1)} %pad_maximum_fusion.1.recv0), channel_id=1, source_target_pairs={{0,2},{1,3},{2,4},{3,5},{4,6},{5,7},{6,0},{7,1},{8,10},{9,11},{10,... | collective-permute-start | bytes 122888 | tf_op jit(solution)/shard_map/ppermute | solution.py:646
  100.1 5.3 %collective-permute-start.12 = (f32[40,128]{1,0:T(8,128)S(1)}, f32[40,128]{1,0:T(8,128)S(1)}, u32[]{:S(2)}, u32[]{:S(2)}) collective-permute-start(f32[40,128]{1,0:T(8,128)S(1)} %products.5), channel_id=1, source_target_pairs={{0,1},{1,0},{2,3},{3,2},{4,5},{5,4},{6,7},{7,6},{8,9},{9,8},{10,11... | collective-permute-start | bytes 61448 | tf_op jit(solution)/shard_map/ppermute | solution.py:642
  105.4 2.9 %collective-permute-start.15 = (f32[80,128]{1,0:T(8,128)S(1)}, f32[80,128]{1,0:T(8,128)S(1)}, u32[]{:S(2)}, u32[]{:S(2)}) collective-permute-start(f32[80,128]{1,0:T(8,128)S(1)} %pad_maximum_fusion.2.recv0), channel_id=1, source_target_pairs={{0,6},{1,7},{2,0},{3,1},{4,2},{5,3},{6,4},{7,5},{8,14},{9,15},{10,... | collective-permute-start | bytes 122888 | tf_op jit(solution)/shard_map/ppermute | solution.py:646
  106.4 4.4 %collective-permute-start.14 = (f32[80,128]{1,0:T(8,128)S(1)}, f32[80,128]{1,0:T(8,128)S(1)}, u32[]{:S(2)}, u32[]{:S(2)}) collective-permute-start(f32[80,128]{1,0:T(8,128)S(1)} %pad_maximum_fusion.2.recv0), channel_id=1, source_target_pairs={{0,4},{1,5},{2,6},{3,7},{4,0},{5,1},{6,2},{7,3},{8,12},{9,13},{10,... | collective-permute-start | bytes 122888 | tf_op jit(solution)/shard_map/ppermute | solution.py:646
  107.0 4.1 %collective-permute-start.13 = (f32[80,128]{1,0:T(8,128)S(1)}, f32[80,128]{1,0:T(8,128)S(1)}, u32[]{:S(2)}, u32[]{:S(2)}) collective-permute-start(f32[80,128]{1,0:T(8,128)S(1)} %pad_maximum_fusion.2.recv0), channel_id=1, source_target_pairs={{0,2},{1,3},{2,4},{3,5},{4,6},{5,7},{6,0},{7,1},{8,10},{9,11},{10,... | collective-permute-start | bytes 122888 | tf_op jit(solution)/shard_map/ppermute | solution.py:646
  113.0 34.2 %copy-start = (f32[6,256]{1,0:T(8,128)S(1)}, f32[6,256]{1,0:T(8,128)}, u32[]{:S(2)}) copy-start(f32[6,256]{1,0:T(8,128)} %right_ref.1) | copy-start | bytes 18436

commit v7 on v6

--- a/solution.py
+++ b/solution.py
@@ -11,7 +11,7 @@
 LANES = 128
 F32 = jnp.float32
 ROWS = ("frames", "cols")
-EARLY = 7
+EARLY = 4
 
 
 def lane_ids(rows):
@@ -138,8 +138,11 @@
     ]
 
 
-def load_kernel(tiles_hbm, tiles_ref, *sems):
-    copies = [pltpu.make_async_copy(tiles_hbm.at[s], tiles_ref.at[s], sems[s]) for s in range(EARLY)]
+def load_kernel(tiles_hbm, early_ref, late_ref, *sems):
+    copies = [
+        pltpu.make_async_copy(tiles_hbm.at[s], slot_of((early_ref, late_ref), s), sems[s])
+        for s in range(8)
+    ]
     for copy in copies:
         copy.start()
     for copy in copies:
@@ -186,7 +189,7 @@
     return tiles_refs[0].at[s] if s < EARLY else tiles_refs[1].at[s - EARLY]
 
 
-def transposed_products(row_ref, tiles_refs, ids_refs, picked, spread, copies=()):
+def transposed_products(row_ref, tiles_refs, ids_refs, picked, spread):
     rows_ref, _, count_ref = ids_refs
     count = count_ref[0, 0]
     picked[...] = jnp.zeros((LANES, 384), F32)
@@ -205,8 +208,6 @@
         )
     products = []
     for s in range(8):
-        if copies and s >= EARLY:
-            copies[s - EARLY].wait()
         tile = slot_of(tiles_refs, s)
         sums = [[None] * 3, [None] * 3]
         for i in range(48):
@@ -256,7 +257,7 @@
     out_ref[0:1, :] = out_ref[0:1, :] + edge
 
 
-def send_frames(row_ref, edge_ref, masked_ref, tiles_refs, ids_refs, send_ref, band_ref, scratch, copies=()):
+def send_frames(row_ref, edge_ref, masked_ref, tiles_refs, ids_refs, send_ref, band_ref, scratch):
     picked, natural, sums, spread = scratch
     col = lax.axis_index("cols")
     sub = lax.broadcasted_iota(jnp.int32, (8, 384), 0)
@@ -266,7 +267,7 @@
     mine, onward = edge_terms(row_ref, edge_ref)
     send_ref[jnp.minimum(lax.axis_index("frames") + 1, 31), 4:5, :] = onward
     band_terms(row_ref, masked_ref, mine, band_ref, natural, sums)
-    for s, product in enumerate(transposed_products(row_ref, tiles_refs, ids_refs, picked, spread, copies)):
+    for s, product in enumerate(transposed_products(row_ref, tiles_refs, ids_refs, picked, spread)):
         q = ids_refs[1][0, s]
         send_ref[q // 4, pl.ds(4 + q % 4, 1), :] += product
 
@@ -302,15 +303,9 @@
 
 
 def first_kernel(
-    recv0, recv1, recv2, recv3, masked_ref, tiles_hbm, early_ref, rows_ref, cols_ref, count_ref,
-    send_ref, band_ref, row_ref, edge_ref, late_ref, picked, natural, sums, spread, *sems,
+    recv0, recv1, recv2, recv3, masked_ref, early_ref, late_ref, rows_ref, cols_ref, count_ref,
+    send_ref, band_ref, row_ref, edge_ref, *scratch,
 ):
-    copies = [
-        pltpu.make_async_copy(tiles_hbm.at[EARLY + s], late_ref.at[s], sems[s])
-        for s in range(8 - EARLY)
-    ]
-    for copy in copies:
-        copy.start()
     col = lax.axis_index("cols")
     row_ref[...] = jnp.zeros((8, 8, 384), F32)
     for c, ref, at in blocks((recv0, recv1, recv2, recv3)):
@@ -322,10 +317,9 @@
         part = jnp.where(col % 2 == 1, recv0[at : at + 6, :], recv1[at : at + 6, :])
         for i in range(16):
             edge_ref[j * 16 + i] = jnp.where(ids >= 120, right(part, 120 - i * 8), 0.0)
-    scratch = (picked, natural, sums, spread)
     send_frames(
         row_ref, edge_ref, masked_ref, (early_ref, late_ref), (rows_ref, cols_ref, count_ref),
-        send_ref, band_ref, scratch, copies,
+        send_ref, band_ref, scratch,
     )
 
 
@@ -664,16 +658,18 @@
     )(*[in_hbm(x) for x in inputs])
     ids.append(tile_count)
     recv = shared = share(send)
-    (early,) = call(load_kernel, [HB], [shape(EARLY, 384, 384)], [sem] * EARLY, "load")(stored)
+    early, late = call(
+        load_kernel, [HB], [shape(n, 384, 384) for n in (EARLY, 8 - EARLY)], [sem] * 8, "load"
+    )(stored)
     frames_out = [shape(32, 8, 384), shape(8, 384), shape(8, 8, 384)]
     scratch = [(LANES, 384), (8, 256), (8, 256), (384, 512)]
-    send, band, row, edges, late = call(
+    send, band, row, edges = call(
         first_kernel,
-        [VM] * 5 + [HB, VM] + [SM] * 3,
-        frames_out + [shape(48, 6, LANES), shape(8 - EARLY, 384, 384)],
-        scratch + [sem] * (8 - EARLY),
+        [VM] * 7 + [SM] * 3,
+        frames_out + [shape(48, 6, LANES)],
+        scratch,
         "first",
-    )(*recv, masked, stored, early, *ids)
+    )(*recv, masked, early, late, *ids)
     vectors, images, moments = [row], [], []
     for it in range(ITERS - 1):
         recv = exchange(send, "frames")

time: 149 us -> 148 us (level)
  no operation moved by 1% of the time
where the time goes in v7:
time: 148 us; the launch traced here: 147 us
  blocking collectives  90 us (61%)
  starting transfers between devices  21.2 us (14%)
  waiting for transfers between devices  18.4 us (12%)
  Pallas kernels  16.3 us (11%)
    all_to_all x5, blocking collectives, exchange(): return lax.all_to_all(x, axis, 0, 0, tiled=True)  90 us
    ppermute x12, waiting for transfers between devices, share(): others.append(lax.ppermute(pair, 'cols', ahead))  15 us
    ppermute x4, starting transfers between devices, share(): pair = jnp.concatenate([x, lax.ppermute(x, 'cols', swap)], axis=0)  13.7 us
    ppermute x12, starting transfers between devices, share(): others.append(lax.ppermute(pair, 'cols', ahead))  7.49 us
    pallas_call x2, Pallas kernels, per_device(): call(next_kernel, specs + [VM] * 2, frames_out + [shape(8, 384), shape(2,...  3.56 us
    ppermute x4, waiting for transfers between devices, share(): pair = jnp.concatenate([x, lax.ppermute(x, 'cols', swap)], axis=0)  3.4 us
    pallas_call x3, Pallas kernels, per_device(): call(cols_kernel, [VM] * 6 + [SM] * 2, [shape(40, LANES)], [], 'products')  3.35 us
  transfers between devices with their start and end apart: 16, of which 15 were waited for; matrix products, arithmetic and copies ran while one was open for 0% of the time, Pallas kernels for 2%

profile of v7, /device:TPU:1, one launch (start us, length us, event | category | flops | bytes accessed | tf_op | source)
XLA Modules:
  0.0 147.2 jit_solution(9862385022328190663)
XLA Ops:
  0.6 1.3 start.1
  2.0 3.3 %collective-permute-start = (f32[80,128]{1,0:T(8,128)S(1)}, f32[80,128]{1,0:T(8,128)S(1)}, u32[]{:S(2)}, u32[]{:S(2)}) collective-permute-start(f32[80,128]{1,0:T(8,128)S(1)} %get-tuple-element.32), channel_id=1, source_target_pairs={{0,1},{1,0},{2,3},{3,2},{4,5},{5,4},{6,7},{7,6},{8,9},{9,8},{10,11... | collective-permute-start | bytes 122888 | tf_op jit(solution)/shard_map/ppermute | solution.py:636
  5.2 0.9 collective-permute-done
  6.1 1.0 collective-permute-start.3
  8.8 2.4 %load.1 = (f32[4,384,384]{2,1,0:T(8,128)S(1)}, f32[4,384,384]{2,1,0:T(8,128)S(1)}) custom-call(f32[8,384,384]{2,1,0:T(8,128)} %bitcast.5), custom_call_target="tpu_custom_call" | custom-call | tf_op jit(solution)/shard_map/load/pallas_call | solution.py:661
  12.0 2.5 %collective-permute-done.1.recv1 = f32[160,128]{1,0:T(8,128)S(1)} collective-permute-done((f32[160,128]{1,0:T(8,128)S(1)}, f32[160,128]{1,0:T(8,128)S(1)}, u32[]{:S(2)}, u32[]{:S(2)}) %collective-permute-start.1) | collective-permute-done | bytes 81952 | tf_op jit(solution)/shard_map/ppermute | solution.py:640
  14.5 1.5 first.1
  15.9 24.7 %all_to_all.25.recv_ref = f32[32,8,384]{2,1,0:T(8,128)S(1)} all-to-all(f32[32,8,384]{2,1,0:T(8,128)S(1)} %get-tuple-element.38), channel_id=1, replica_groups=mesh['frames'=32,'cols'=8] {'frames'}, dimensions={0} | all-to-all | bytes 786432 | tf_op jit(solution)/shard_map/all_to_all | solution.py:631
  40.7 1.1 products.3._
  41.8 2.5 %collective-permute-start.4 = (f32[40,128]{1,0:T(8,128)S(1)}, f32[40,128]{1,0:T(8,128)S(1)}, u32[]{:S(2)}, u32[]{:S(2)}) collective-permute-start(f32[40,128]{1,0:T(8,128)S(1)} %products.3._), channel_id=1, source_target_pairs={{0,1},{1,0},{2,3},{3,2},{4,5},{5,4},{6,7},{7,6},{8,9},{9,8},{10,11... | collective-permute-start | bytes 61448 | tf_op jit(solution)/shard_map/ppermute | solution.py:636
  45.4 1.2 collective-permute-start.5
  46.7 1.3 collective-permute-done.7.recv3
  48.0 1.5 %collective-permute-done.6.recv2 = f32[80,128]{1,0:T(8,128)S(1)} collective-permute-done((f32[80,128]{1,0:T(8,128)S(1)}, f32[80,128]{1,0:T(8,128)S(1)}, u32[]{:S(2)}, u32[]{:S(2)}) %collective-permute-start.6) | collective-permute-done | bytes 40992 | tf_op jit(solution)/shard_map/ppermute | solution.py:640
  49.5 1.3 collective-permute-done.5.recv1
  50.8 1.8 %next.2 = (f32[32,8,384]{2,1,0:T(8,128)S(1)}, f32[8,384]{1,0:T(8,128)S(1)}, f32[8,8,384]{2,1,0:T(8,128)S(1)}, f32[8,384]{1,0:T(8,128)S(1)}, f32[2,8,128]{2,1,0:T(8,128)S(1)}) custom-call(f32[80,128]{1,0:T(8,128)S(1)} %pad_maximum_fusion.recv0, f32[80,128]{1,0:T(8,128)S(1)} %collective-permute-done.5.recv1, f32[80,128]{1,0:T(8,128)S(1)} %collective-permute-done.6.recv2, ...), custom_call_target="tpu_custom_call" | custom-call | tf_op jit(solution)/shard_map/next/pallas_call | solution.py:696
  52.6 16.7 %all_to_all.26.recv_ref = f32[32,8,384]{2,1,0:T(8,128)S(1)} all-to-all(f32[32,8,384]{2,1,0:T(8,128)S(1)} %get-tuple-element.44), channel_id=1, replica_groups=mesh['frames'=32,'cols'=8] {'frames'}, dimensions={0} | all-to-all | bytes 786432 | tf_op jit(solution)/shard_map/all_to_all | solution.py:631
  69.3 1.1 products.4
  70.4 3.5 %collective-permute-start.8 = (f32[40,128]{1,0:T(8,128)S(1)}, f32[40,128]{1,0:T(8,128)S(1)}, u32[]{:S(2)}, u32[]{:S(2)}) collective-permute-start(f32[40,128]{1,0:T(8,128)S(1)} %products.4), channel_id=1, source_target_pairs={{0,1},{1,0},{2,3},{3,2},{4,5},{5,4},{6,7},{7,6},{8,9},{9,8},{10,11... | collective-permute-start | bytes 61448 | tf_op jit(solution)/shard_map/ppermute | solution.py:636
  74.8 1.0 collective-permute-start.11
  76.6 1.1 collective-permute-done.11.recv3
  77.6 2.5 %collective-permute-done.10.recv2 = f32[80,128]{1,0:T(8,128)S(1)} collective-permute-done((f32[80,128]{1,0:T(8,128)S(1)}, f32[80,128]{1,0:T(8,128)S(1)}, u32[]{:S(2)}, u32[]{:S(2)}) %collective-permute-start.10) | collective-permute-done | bytes 40992 | tf_op jit(solution)/shard_map/ppermute | solution.py:640
  80.6 1.8 %next.3 = (f32[32,8,384]{2,1,0:T(8,128)S(1)}, f32[8,384]{1,0:T(8,128)S(1)}, f32[8,8,384]{2,1,0:T(8,128)S(1)}, f32[8,384]{1,0:T(8,128)S(1)}, f32[2,8,128]{2,1,0:T(8,128)S(1)}) custom-call(f32[80,128]{1,0:T(8,128)S(1)} %pad_maximum_fusion.1.recv0, f32[80,128]{1,0:T(8,128)S(1)} %collective-permute-done.9.recv1, f32[80,128]{1,0:T(8,128)S(1)} %collective-permute-done.10.recv2, ...), custom_call_target="tpu_custom_call" | custom-call | tf_op jit(solution)/shard_map/next/pallas_call | solution.py:696
  82.4 15.7 %all_to_all.27.recv_ref = f32[32,8,384]{2,1,0:T(8,128)S(1)} all-to-all(f32[32,8,384]{2,1,0:T(8,128)S(1)} %get-tuple-element.47), channel_id=1, replica_groups=mesh['frames'=32,'cols'=8] {'frames'}, dimensions={0} | all-to-all | bytes 786432 | tf_op jit(solution)/shard_map/all_to_all | solution.py:631
  98.1 1.1 products.5
  99.2 4.5 %collective-permute-start.12 = (f32[40,128]{1,0:T(8,128)S(1)}, f32[40,128]{1,0:T(8,128)S(1)}, u32[]{:S(2)}, u32[]{:S(2)}) collective-permute-start(f32[40,128]{1,0:T(8,128)S(1)} %products.5), channel_id=1, source_target_pairs={{0,1},{1,0},{2,3},{3,2},{4,5},{5,4},{6,7},{7,6},{8,9},{9,8},{10,11... | collective-permute-start | bytes 61448 | tf_op jit(solution)/shard_map/ppermute | solution.py:636
  104.5 0.9 collective-permute-start.15
  107.4 2.5 %collective-permute-done.14.recv2 = f32[80,128]{1,0:T(8,128)S(1)} collective-permute-done((f32[80,128]{1,0:T(8,128)S(1)}, f32[80,128]{1,0:T(8,128)S(1)}, u32[]{:S(2)}, u32[]{:S(2)}) %collective-permute-start.14) | collective-permute-done | bytes 40992 | tf_op jit(solution)/shard_map/ppermute | solution.py:640
  110.3 1.8 %last.1 = (f32[32,40,128]{2,1,0:T(8,128)S(1)}, f32[8,384]{1,0:T(8,128)S(1)}, f32[8,8,384]{2,1,0:T(8,128)S(1)}, f32[8,384]{1,0:T(8,128)S(1)}) custom-call(f32[80,128]{1,0:T(8,128)S(1)} %pad_maximum_fusion.2.recv0, f32[80,128]{1,0:T(8,128)S(1)} %collective-permute-done.13.recv1, f32[80,128]{1,0:T(8,128)S(1)} %collective-permute-done.14.recv2, ...), custom_call_target="tpu_custom_call" | custom-call | tf_op jit(solution)/shard_map/last/pallas_call | solution.py:705
  112.1 21.0 %all_to_all.28.recv_ref = f32[32,40,128]{2,1,0:T(8,128)S(1)} all-to-all(f32[32,40,128]{2,1,0:T(8,128)S(1)} %get-tuple-element.53), channel_id=1, replica_groups=mesh['frames'=32,'cols'=8] {'frames'}, dimensions={0} | all-to-all | bytes 1310720 | tf_op jit(solution)/shard_map/all_to_all | solution.py:631
  133.1 1.4 finish.1
  134.5 11.9 %all_to_all.29.recv_ref = f32[8,16,128]{2,1,0:T(8,128)S(1)} all-to-all(f32[8,16,128]{2,1,0:T(8,128)S(1)} %get-tuple-element.56), channel_id=1, replica_groups=mesh['frames'=32,'cols'=8] {'cols'}, dimensions={0} | all-to-all | bytes 131072 | tf_op jit(solution)/shard_map/all_to_all | solution.py:631
  146.3 0.9 end.1
  (24 shorter events, 8.4 us)
Async XLA Ops:
  2.0 4.2 %collective-permute-start = (f32[80,128]{1,0:T(8,128)S(1)}, f32[80,128]{1,0:T(8,128)S(1)}, u32[]{:S(2)}, u32[]{:S(2)}) collective-permute-start(f32[80,128]{1,0:T(8,128)S(1)} %get-tuple-element.32), channel_id=1, source_target_pairs={{0,1},{1,0},{2,3},{3,2},{4,5},{5,4},{6,7},{7,6},{8,9},{9,8},{10,11... | collective-permute-start | bytes 122888 | tf_op jit(solution)/shard_map/ppermute | solution.py:636
  6.1 5.1 %collective-permute-start.3 = (f32[160,128]{1,0:T(8,128)S(1)}, f32[160,128]{1,0:T(8,128)S(1)}, u32[]{:S(2)}, u32[]{:S(2)}) collective-permute-start(f32[160,128]{1,0:T(8,128)S(1)} %constant_dynamic-update-slice_fusion.recv0), channel_id=1, source_target_pairs={{0,6},{1,7},{2,0},{3,1},{4,2},{5,3},{6,4},{7,5},{8,14},{9,15},{10,... | collective-permute-start | bytes 245768 | tf_op jit(solution)/shard_map/ppermute | solution.py:640
  7.1 4.9 %collective-permute-start.2 = (f32[160,128]{1,0:T(8,128)S(1)}, f32[160,128]{1,0:T(8,128)S(1)}, u32[]{:S(2)}, u32[]{:S(2)}) collective-permute-start(f32[160,128]{1,0:T(8,128)S(1)} %constant_dynamic-update-slice_fusion.recv0), channel_id=1, source_target_pairs={{0,4},{1,5},{2,6},{3,7},{4,0},{5,1},{6,2},{7,3},{8,12},{9,13},{10,... | collective-permute-start | bytes 245768 | tf_op jit(solution)/shard_map/ppermute | solution.py:640
  7.5 7.0 %collective-permute-start.1 = (f32[160,128]{1,0:T(8,128)S(1)}, f32[160,128]{1,0:T(8,128)S(1)}, u32[]{:S(2)}, u32[]{:S(2)}) collective-permute-start(f32[160,128]{1,0:T(8,128)S(1)} %constant_dynamic-update-slice_fusion.recv0), channel_id=1, source_target_pairs={{0,2},{1,3},{2,4},{3,5},{4,6},{5,7},{6,0},{7,1},{8,10},{9,11},{10,... | collective-permute-start | bytes 245768 | tf_op jit(solution)/shard_map/ppermute | solution.py:640
  41.8 3.3 %collective-permute-start.4 = (f32[40,128]{1,0:T(8,128)S(1)}, f32[40,128]{1,0:T(8,128)S(1)}, u32[]{:S(2)}, u32[]{:S(2)}) collective-permute-start(f32[40,128]{1,0:T(8,128)S(1)} %products.3._), channel_id=1, source_target_pairs={{0,1},{1,0},{2,3},{3,2},{4,5},{5,4},{6,7},{7,6},{8,9},{9,8},{10,11... | collective-permute-start | bytes 61448 | tf_op jit(solution)/shard_map/ppermute | solution.py:636
  45.1 2.9 %collective-permute-start.7 = (f32[80,128]{1,0:T(8,128)S(1)}, f32[80,128]{1,0:T(8,128)S(1)}, u32[]{:S(2)}, u32[]{:S(2)}) collective-permute-start(f32[80,128]{1,0:T(8,128)S(1)} %pad_maximum_fusion.recv0), channel_id=1, source_target_pairs={{0,6},{1,7},{2,0},{3,1},{4,2},{5,3},{6,4},{7,5},{8,14},{9,15},{10,... | collective-permute-start | bytes 122888 | tf_op jit(solution)/shard_map/ppermute | solution.py:640
  45.1 4.4 %collective-permute-start.6 = (f32[80,128]{1,0:T(8,128)S(1)}, f32[80,128]{1,0:T(8,128)S(1)}, u32[]{:S(2)}, u32[]{:S(2)}) collective-permute-start(f32[80,128]{1,0:T(8,128)S(1)} %pad_maximum_fusion.recv0), channel_id=1, source_target_pairs={{0,4},{1,5},{2,6},{3,7},{4,0},{5,1},{6,2},{7,3},{8,12},{9,13},{10,... | collective-permute-start | bytes 122888 | tf_op jit(solution)/shard_map/ppermute | solution.py:640
  45.4 5.4 %collective-permute-start.5 = (f32[80,128]{1,0:T(8,128)S(1)}, f32[80,128]{1,0:T(8,128)S(1)}, u32[]{:S(2)}, u32[]{:S(2)}) collective-permute-start(f32[80,128]{1,0:T(8,128)S(1)} %pad_maximum_fusion.recv0), channel_id=1, source_target_pairs={{0,2},{1,3},{2,4},{3,5},{4,6},{5,7},{6,0},{7,1},{8,10},{9,11},{10,... | collective-permute-start | bytes 122888 | tf_op jit(solution)/shard_map/ppermute | solution.py:640
  70.4 4.3 %collective-permute-start.8 = (f32[40,128]{1,0:T(8,128)S(1)}, f32[40,128]{1,0:T(8,128)S(1)}, u32[]{:S(2)}, u32[]{:S(2)}) collective-permute-start(f32[40,128]{1,0:T(8,128)S(1)} %products.4), channel_id=1, source_target_pairs={{0,1},{1,0},{2,3},{3,2},{4,5},{5,4},{6,7},{7,6},{8,9},{9,8},{10,11... | collective-permute-start | bytes 61448 | tf_op jit(solution)/shard_map/ppermute | solution.py:636
  74.8 2.9 %collective-permute-start.11 = (f32[80,128]{1,0:T(8,128)S(1)}, f32[80,128]{1,0:T(8,128)S(1)}, u32[]{:S(2)}, u32[]{:S(2)}) collective-permute-start(f32[80,128]{1,0:T(8,128)S(1)} %pad_maximum_fusion.1.recv0), channel_id=1, source_target_pairs={{0,6},{1,7},{2,0},{3,1},{4,2},{5,3},{6,4},{7,5},{8,14},{9,15},{10,... | collective-permute-start | bytes 122888 | tf_op jit(solution)/shard_map/ppermute | solution.py:640
  75.8 4.4 %collective-permute-start.10 = (f32[80,128]{1,0:T(8,128)S(1)}, f32[80,128]{1,0:T(8,128)S(1)}, u32[]{:S(2)}, u32[]{:S(2)}) collective-permute-start(f32[80,128]{1,0:T(8,128)S(1)} %pad_maximum_fusion.1.recv0), channel_id=1, source_target_pairs={{0,4},{1,5},{2,6},{3,7},{4,0},{5,1},{6,2},{7,3},{8,12},{9,13},{10,... | collective-permute-start | bytes 122888 | tf_op jit(solution)/shard_map/ppermute | solution.py:640
  76.6 4.1 %collective-permute-start.9 = (f32[80,128]{1,0:T(8,128)S(1)}, f32[80,128]{1,0:T(8,128)S(1)}, u32[]{:S(2)}, u32[]{:S(2)}) collective-permute-start(f32[80,128]{1,0:T(8,128)S(1)} %pad_maximum_fusion.1.recv0), channel_id=1, source_target_pairs={{0,2},{1,3},{2,4},{3,5},{4,6},{5,7},{6,0},{7,1},{8,10},{9,11},{10,... | collective-permute-start | bytes 122888 | tf_op jit(solution)/shard_map/ppermute | solution.py:640
  99.2 5.3 %collective-permute-start.12 = (f32[40,128]{1,0:T(8,128)S(1)}, f32[40,128]{1,0:T(8,128)S(1)}, u32[]{:S(2)}, u32[]{:S(2)}) collective-permute-start(f32[40,128]{1,0:T(8,128)S(1)} %products.5), channel_id=1, source_target_pairs={{0,1},{1,0},{2,3},{3,2},{4,5},{5,4},{6,7},{7,6},{8,9},{9,8},{10,11... | collective-permute-start | bytes 61448 | tf_op jit(solution)/shard_map/ppermute | solution.py:636
  104.5 2.9 %collective-permute-start.15 = (f32[80,128]{1,0:T(8,128)S(1)}, f32[80,128]{1,0:T(8,128)S(1)}, u32[]{:S(2)}, u32[]{:S(2)}) collective-permute-start(f32[80,128]{1,0:T(8,128)S(1)} %pad_maximum_fusion.2.recv0), channel_id=1, source_target_pairs={{0,6},{1,7},{2,0},{3,1},{4,2},{5,3},{6,4},{7,5},{8,14},{9,15},{10,... | collective-permute-start | bytes 122888 | tf_op jit(solution)/shard_map/ppermute | solution.py:640
  105.5 4.4 %collective-permute-start.14 = (f32[80,128]{1,0:T(8,128)S(1)}, f32[80,128]{1,0:T(8,128)S(1)}, u32[]{:S(2)}, u32[]{:S(2)}) collective-permute-start(f32[80,128]{1,0:T(8,128)S(1)} %pad_maximum_fusion.2.recv0), channel_id=1, source_target_pairs={{0,4},{1,5},{2,6},{3,7},{4,0},{5,1},{6,2},{7,3},{8,12},{9,13},{10,... | collective-permute-start | bytes 122888 | tf_op jit(solution)/shard_map/ppermute | solution.py:640
  106.1 4.1 %collective-permute-start.13 = (f32[80,128]{1,0:T(8,128)S(1)}, f32[80,128]{1,0:T(8,128)S(1)}, u32[]{:S(2)}, u32[]{:S(2)}) collective-permute-start(f32[80,128]{1,0:T(8,128)S(1)} %pad_maximum_fusion.2.recv0), channel_id=1, source_target_pairs={{0,2},{1,3},{2,4},{3,5},{4,6},{5,7},{6,0},{7,1},{8,10},{9,11},{10,... | collective-permute-start | bytes 122888 | tf_op jit(solution)/shard_map/ppermute | solution.py:640
  133.1 13.2 %copy-start = (f32[6,256]{1,0:T(8,128)S(1)}, f32[6,256]{1,0:T(8,128)}, u32[]{:S(2)}) copy-start(f32[6,256]{1,0:T(8,128)} %right_ref.1) | copy-start | bytes 18436

commit v8 on v7

--- a/solution.py
+++ b/solution.py
@@ -11,6 +11,7 @@
 LANES = 128
 F32 = jnp.float32
 ROWS = ("frames", "cols")
+SPREAD = 6
 EARLY = 4
 
 
@@ -196,12 +197,12 @@
     for s in range(8):
         r = rows_ref[0, s]
         picked[s : s + 1, :] = row_ref[r // 4, pl.ds(r % 4, 1), :]
-    for i, part in enumerate(bfloat16_parts(picked[4:8, :])):
-        picked[8 + 4 * i : 12 + 4 * i, :] = part.astype(F32)
+    for i, part in enumerate(bfloat16_parts(picked[8 - SPREAD : 8, :])):
+        picked[8 + SPREAD * i : 8 + SPREAD * (i + 1), :] = part.astype(F32)
     upright = [picked[:, j * LANES : (j + 1) * LANES].T for j in range(3)]
-    at = lax.broadcasted_iota(jnp.int32, (LANES, 512), 0)
-    to = lax.broadcasted_iota(jnp.int32, (LANES, 512), 1)
-    ones = ((at >= 8) & (at < 20) & (at % 4 == to // LANES)).astype(jnp.bfloat16)
+    at = lax.broadcasted_iota(jnp.int32, (LANES, SPREAD * LANES), 0) - 8
+    to = lax.broadcasted_iota(jnp.int32, (LANES, SPREAD * LANES), 1)
+    ones = ((at >= 0) & (at < 3 * SPREAD) & (at % SPREAD == to // LANES)).astype(jnp.bfloat16)
     for j in range(3):
         spread[j * LANES : (j + 1) * LANES, :] = jnp.dot(
             upright[j].astype(jnp.bfloat16), ones, preferred_element_type=F32
@@ -211,11 +212,11 @@
         tile = slot_of(tiles_refs, s)
         sums = [[None] * 3, [None] * 3]
         for i in range(48):
-            if s < 4:
+            if s < 8 - SPREAD:
                 column = upright[i // 16][8 * (i % 16) : 8 * (i % 16) + 8, s : s + 1]
                 column = jnp.broadcast_to(column, (8, LANES))
             else:
-                column = spread[8 * i : 8 * i + 8, (s - 4) * LANES : (s - 3) * LANES]
+                column = spread[8 * i : 8 * i + 8, (s + SPREAD - 8) * LANES : (s + SPREAD - 7) * LANES]
             for j in range(3):
                 part = tile[8 * i : 8 * i + 8, j * LANES : (j + 1) * LANES] * column
                 before = sums[i % 2][j]
@@ -662,7 +663,7 @@
         load_kernel, [HB], [shape(n, 384, 384) for n in (EARLY, 8 - EARLY)], [sem] * 8, "load"
     )(stored)
     frames_out = [shape(32, 8, 384), shape(8, 384), shape(8, 8, 384)]
-    scratch = [(LANES, 384), (8, 256), (8, 256), (384, 512)]
+    scratch = [(LANES, 384), (8, 256), (8, 256), (384, SPREAD * LANES)]
     send, band, row, edges = call(
         first_kernel,
         [VM] * 7 + [SM] * 3,

time: 148 us -> 147 us (level)
  no operation moved by 1% of the time
where the time goes in v8:
time: 147 us
  blocking collectives  89.9 us (61%)
  starting transfers between devices  21.2 us (14%)
  waiting for transfers between devices  18.4 us (13%)
  Pallas kernels  16.2 us (11%)
    all_to_all x5, blocking collectives, exchange(): return lax.all_to_all(x, axis, 0, 0, tiled=True)  89.9 us
    ppermute x12, waiting for transfers between devices, share(): others.append(lax.ppermute(pair, 'cols', ahead))  15 us
    ppermute x4, starting transfers between devices, share(): pair = jnp.concatenate([x, lax.ppermute(x, 'cols', swap)], axis=0)  13.7 us
    ppermute x12, starting transfers between devices, share(): others.append(lax.ppermute(pair, 'cols', ahead))  7.49 us
    pallas_call x2, Pallas kernels, per_device(): call(next_kernel, specs + [VM] * 2, frames_out + [shape(8, 384), shape(2,...  3.42 us
    ppermute x4, waiting for transfers between devices, share(): pair = jnp.concatenate([x, lax.ppermute(x, 'cols', swap)], axis=0)  3.4 us
    pallas_call x3, Pallas kernels, per_device(): call(cols_kernel, [VM] * 6 + [SM] * 2, [shape(40, LANES)], [], 'products')  3.35 us
  transfers between devices with their start and end apart: 16, of which 15 were waited for; matrix products, arithmetic and copies ran while one was open for 0% of the time, Pallas kernels for 2%

profile of v8, /device:TPU:1, one launch (start us, length us, event | category | flops | bytes accessed | tf_op | source)
XLA Modules:
  0.0 147.1 jit_solution(4837821216537195352)
XLA Ops:
  0.6 1.3 start.1
  2.0 3.3 %collective-permute-start = (f32[80,128]{1,0:T(8,128)S(1)}, f32[80,128]{1,0:T(8,128)S(1)}, u32[]{:S(2)}, u32[]{:S(2)}) collective-permute-start(f32[80,128]{1,0:T(8,128)S(1)} %get-tuple-element.32), channel_id=1, source_target_pairs={{0,1},{1,0},{2,3},{3,2},{4,5},{5,4},{6,7},{7,6},{8,9},{9,8},{10,11... | collective-permute-start | bytes 122888 | tf_op jit(solution)/shard_map/ppermute | solution.py:637
  5.2 0.9 collective-permute-done
  6.1 1.0 collective-permute-start.3
  8.8 2.4 %load.1 = (f32[4,384,384]{2,1,0:T(8,128)S(1)}, f32[4,384,384]{2,1,0:T(8,128)S(1)}) custom-call(f32[8,384,384]{2,1,0:T(8,128)} %bitcast.5), custom_call_target="tpu_custom_call" | custom-call | tf_op jit(solution)/shard_map/load/pallas_call | solution.py:662
  12.0 2.5 %collective-permute-done.1.recv1 = f32[160,128]{1,0:T(8,128)S(1)} collective-permute-done((f32[160,128]{1,0:T(8,128)S(1)}, f32[160,128]{1,0:T(8,128)S(1)}, u32[]{:S(2)}, u32[]{:S(2)}) %collective-permute-start.1) | collective-permute-done | bytes 81952 | tf_op jit(solution)/shard_map/ppermute | solution.py:641
  14.5 1.5 %first.1 = (f32[32,8,384]{2,1,0:T(8,128)S(1)}, f32[8,384]{1,0:T(8,128)S(1)}, f32[8,8,384]{2,1,0:T(8,128)S(1)}, f32[48,6,128]{2,1,0:T(8,128)S(1)}) custom-call(f32[160,128]{1,0:T(8,128)S(1)} %constant_dynamic-update-slice_fusion.recv0, f32[160,128]{1,0:T(8,128)S(1)} %collective-permute-done.1.recv1, f32[160,128]{1,0:T(8,128)S(1)} %collective-permute-done.2.recv2, ...), custom_call_target="tpu_custom_call" | custom-call | tf_op jit(solution)/shard_map/first/pallas_call | solution.py:667
  16.0 24.7 %all_to_all.25.recv_ref = f32[32,8,384]{2,1,0:T(8,128)S(1)} all-to-all(f32[32,8,384]{2,1,0:T(8,128)S(1)} %get-tuple-element.38), channel_id=1, replica_groups=mesh['frames'=32,'cols'=8] {'frames'}, dimensions={0} | all-to-all | bytes 786432 | tf_op jit(solution)/shard_map/all_to_all | solution.py:632
  40.7 1.1 products.3._
  41.8 2.5 %collective-permute-start.4 = (f32[40,128]{1,0:T(8,128)S(1)}, f32[40,128]{1,0:T(8,128)S(1)}, u32[]{:S(2)}, u32[]{:S(2)}) collective-permute-start(f32[40,128]{1,0:T(8,128)S(1)} %products.3._), channel_id=1, source_target_pairs={{0,1},{1,0},{2,3},{3,2},{4,5},{5,4},{6,7},{7,6},{8,9},{9,8},{10,11... | collective-permute-start | bytes 61448 | tf_op jit(solution)/shard_map/ppermute | solution.py:637
  45.5 1.2 collective-permute-start.5
  46.8 1.3 collective-permute-done.7.recv3
  48.0 1.5 %collective-permute-done.6.recv2 = f32[80,128]{1,0:T(8,128)S(1)} collective-permute-done((f32[80,128]{1,0:T(8,128)S(1)}, f32[80,128]{1,0:T(8,128)S(1)}, u32[]{:S(2)}, u32[]{:S(2)}) %collective-permute-start.6) | collective-permute-done | bytes 40992 | tf_op jit(solution)/shard_map/ppermute | solution.py:641
  49.5 1.3 collective-permute-done.5.recv1
  50.9 1.7 %next.2 = (f32[32,8,384]{2,1,0:T(8,128)S(1)}, f32[8,384]{1,0:T(8,128)S(1)}, f32[8,8,384]{2,1,0:T(8,128)S(1)}, f32[8,384]{1,0:T(8,128)S(1)}, f32[2,8,128]{2,1,0:T(8,128)S(1)}) custom-call(f32[80,128]{1,0:T(8,128)S(1)} %pad_maximum_fusion.recv0, f32[80,128]{1,0:T(8,128)S(1)} %collective-permute-done.5.recv1, f32[80,128]{1,0:T(8,128)S(1)} %collective-permute-done.6.recv2, ...), custom_call_target="tpu_custom_call" | custom-call | tf_op jit(solution)/shard_map/next/pallas_call | solution.py:697
  52.6 16.7 %all_to_all.26.recv_ref = f32[32,8,384]{2,1,0:T(8,128)S(1)} all-to-all(f32[32,8,384]{2,1,0:T(8,128)S(1)} %get-tuple-element.44), channel_id=1, replica_groups=mesh['frames'=32,'cols'=8] {'frames'}, dimensions={0} | all-to-all | bytes 786432 | tf_op jit(solution)/shard_map/all_to_all | solution.py:632
  69.3 1.1 products.4
  70.4 3.5 %collective-permute-start.8 = (f32[40,128]{1,0:T(8,128)S(1)}, f32[40,128]{1,0:T(8,128)S(1)}, u32[]{:S(2)}, u32[]{:S(2)}) collective-permute-start(f32[40,128]{1,0:T(8,128)S(1)} %products.4), channel_id=1, source_target_pairs={{0,1},{1,0},{2,3},{3,2},{4,5},{5,4},{6,7},{7,6},{8,9},{9,8},{10,11... | collective-permute-start | bytes 61448 | tf_op jit(solution)/shard_map/ppermute | solution.py:637
  74.7 1.0 collective-permute-start.11
  76.5 1.1 collective-permute-done.11.recv3
  77.6 2.5 %collective-permute-done.10.recv2 = f32[80,128]{1,0:T(8,128)S(1)} collective-permute-done((f32[80,128]{1,0:T(8,128)S(1)}, f32[80,128]{1,0:T(8,128)S(1)}, u32[]{:S(2)}, u32[]{:S(2)}) %collective-permute-start.10) | collective-permute-done | bytes 40992 | tf_op jit(solution)/shard_map/ppermute | solution.py:641
  80.6 1.7 %next.3 = (f32[32,8,384]{2,1,0:T(8,128)S(1)}, f32[8,384]{1,0:T(8,128)S(1)}, f32[8,8,384]{2,1,0:T(8,128)S(1)}, f32[8,384]{1,0:T(8,128)S(1)}, f32[2,8,128]{2,1,0:T(8,128)S(1)}) custom-call(f32[80,128]{1,0:T(8,128)S(1)} %pad_maximum_fusion.1.recv0, f32[80,128]{1,0:T(8,128)S(1)} %collective-permute-done.9.recv1, f32[80,128]{1,0:T(8,128)S(1)} %collective-permute-done.10.recv2, ...), custom_call_target="tpu_custom_call" | custom-call | tf_op jit(solution)/shard_map/next/pallas_call | solution.py:697
  82.3 15.7 %all_to_all.27.recv_ref = f32[32,8,384]{2,1,0:T(8,128)S(1)} all-to-all(f32[32,8,384]{2,1,0:T(8,128)S(1)} %get-tuple-element.47), channel_id=1, replica_groups=mesh['frames'=32,'cols'=8] {'frames'}, dimensions={0} | all-to-all | bytes 786432 | tf_op jit(solution)/shard_map/all_to_all | solution.py:632
  98.0 1.1 products.5
  99.1 4.5 %collective-permute-start.12 = (f32[40,128]{1,0:T(8,128)S(1)}, f32[40,128]{1,0:T(8,128)S(1)}, u32[]{:S(2)}, u32[]{:S(2)}) collective-permute-start(f32[40,128]{1,0:T(8,128)S(1)} %products.5), channel_id=1, source_target_pairs={{0,1},{1,0},{2,3},{3,2},{4,5},{5,4},{6,7},{7,6},{8,9},{9,8},{10,11... | collective-permute-start | bytes 61448 | tf_op jit(solution)/shard_map/ppermute | solution.py:637
  104.4 1.0 collective-permute-start.15
  107.3 2.5 %collective-permute-done.14.recv2 = f32[80,128]{1,0:T(8,128)S(1)} collective-permute-done((f32[80,128]{1,0:T(8,128)S(1)}, f32[80,128]{1,0:T(8,128)S(1)}, u32[]{:S(2)}, u32[]{:S(2)}) %collective-permute-start.14) | collective-permute-done | bytes 40992 | tf_op jit(solution)/shard_map/ppermute | solution.py:641
  110.2 1.8 %last.1 = (f32[32,40,128]{2,1,0:T(8,128)S(1)}, f32[8,384]{1,0:T(8,128)S(1)}, f32[8,8,384]{2,1,0:T(8,128)S(1)}, f32[8,384]{1,0:T(8,128)S(1)}) custom-call(f32[80,128]{1,0:T(8,128)S(1)} %pad_maximum_fusion.2.recv0, f32[80,128]{1,0:T(8,128)S(1)} %collective-permute-done.13.recv1, f32[80,128]{1,0:T(8,128)S(1)} %collective-permute-done.14.recv2, ...), custom_call_target="tpu_custom_call" | custom-call | tf_op jit(solution)/shard_map/last/pallas_call | solution.py:706
  112.0 21.0 %all_to_all.28.recv_ref = f32[32,40,128]{2,1,0:T(8,128)S(1)} all-to-all(f32[32,40,128]{2,1,0:T(8,128)S(1)} %get-tuple-element.53), channel_id=1, replica_groups=mesh['frames'=32,'cols'=8] {'frames'}, dimensions={0} | all-to-all | bytes 1310720 | tf_op jit(solution)/shard_map/all_to_all | solution.py:632
  133.0 1.4 finish.1
  134.4 11.8 %all_to_all.29.recv_ref = f32[8,16,128]{2,1,0:T(8,128)S(1)} all-to-all(f32[8,16,128]{2,1,0:T(8,128)S(1)} %get-tuple-element.56), channel_id=1, replica_groups=mesh['frames'=32,'cols'=8] {'cols'}, dimensions={0} | all-to-all | bytes 131072 | tf_op jit(solution)/shard_map/all_to_all | solution.py:632
  146.2 0.9 end.1
  (24 shorter events, 8.3 us)
Async XLA Ops:
  2.0 4.2 %collective-permute-start = (f32[80,128]{1,0:T(8,128)S(1)}, f32[80,128]{1,0:T(8,128)S(1)}, u32[]{:S(2)}, u32[]{:S(2)}) collective-permute-start(f32[80,128]{1,0:T(8,128)S(1)} %get-tuple-element.32), channel_id=1, source_target_pairs={{0,1},{1,0},{2,3},{3,2},{4,5},{5,4},{6,7},{7,6},{8,9},{9,8},{10,11... | collective-permute-start | bytes 122888 | tf_op jit(solution)/shard_map/ppermute | solution.py:637
  6.1 5.1 %collective-permute-start.3 = (f32[160,128]{1,0:T(8,128)S(1)}, f32[160,128]{1,0:T(8,128)S(1)}, u32[]{:S(2)}, u32[]{:S(2)}) collective-permute-start(f32[160,128]{1,0:T(8,128)S(1)} %constant_dynamic-update-slice_fusion.recv0), channel_id=1, source_target_pairs={{0,6},{1,7},{2,0},{3,1},{4,2},{5,3},{6,4},{7,5},{8,14},{9,15},{10,... | collective-permute-start | bytes 245768 | tf_op jit(solution)/shard_map/ppermute | solution.py:641
  7.1 4.9 %collective-permute-start.2 = (f32[160,128]{1,0:T(8,128)S(1)}, f32[160,128]{1,0:T(8,128)S(1)}, u32[]{:S(2)}, u32[]{:S(2)}) collective-permute-start(f32[160,128]{1,0:T(8,128)S(1)} %constant_dynamic-update-slice_fusion.recv0), channel_id=1, source_target_pairs={{0,4},{1,5},{2,6},{3,7},{4,0},{5,1},{6,2},{7,3},{8,12},{9,13},{10,... | collective-permute-start | bytes 245768 | tf_op jit(solution)/shard_map/ppermute | solution.py:641
  7.5 7.0 %collective-permute-start.1 = (f32[160,128]{1,0:T(8,128)S(1)}, f32[160,128]{1,0:T(8,128)S(1)}, u32[]{:S(2)}, u32[]{:S(2)}) collective-permute-start(f32[160,128]{1,0:T(8,128)S(1)} %constant_dynamic-update-slice_fusion.recv0), channel_id=1, source_target_pairs={{0,2},{1,3},{2,4},{3,5},{4,6},{5,7},{6,0},{7,1},{8,10},{9,11},{10,... | collective-permute-start | bytes 245768 | tf_op jit(solution)/shard_map/ppermute | solution.py:641
  41.8 3.3 %collective-permute-start.4 = (f32[40,128]{1,0:T(8,128)S(1)}, f32[40,128]{1,0:T(8,128)S(1)}, u32[]{:S(2)}, u32[]{:S(2)}) collective-permute-start(f32[40,128]{1,0:T(8,128)S(1)} %products.3._), channel_id=1, source_target_pairs={{0,1},{1,0},{2,3},{3,2},{4,5},{5,4},{6,7},{7,6},{8,9},{9,8},{10,11... | collective-permute-start | bytes 61448 | tf_op jit(solution)/shard_map/ppermute | solution.py:637
  45.2 2.9 %collective-permute-start.7 = (f32[80,128]{1,0:T(8,128)S(1)}, f32[80,128]{1,0:T(8,128)S(1)}, u32[]{:S(2)}, u32[]{:S(2)}) collective-permute-start(f32[80,128]{1,0:T(8,128)S(1)} %pad_maximum_fusion.recv0), channel_id=1, source_target_pairs={{0,6},{1,7},{2,0},{3,1},{4,2},{5,3},{6,4},{7,5},{8,14},{9,15},{10,... | collective-permute-start | bytes 122888 | tf_op jit(solution)/shard_map/ppermute | solution.py:641
  45.2 4.4 %collective-permute-start.6 = (f32[80,128]{1,0:T(8,128)S(1)}, f32[80,128]{1,0:T(8,128)S(1)}, u32[]{:S(2)}, u32[]{:S(2)}) collective-permute-start(f32[80,128]{1,0:T(8,128)S(1)} %pad_maximum_fusion.recv0), channel_id=1, source_target_pairs={{0,4},{1,5},{2,6},{3,7},{4,0},{5,1},{6,2},{7,3},{8,12},{9,13},{10,... | collective-permute-start | bytes 122888 | tf_op jit(solution)/shard_map/ppermute | solution.py:641
  45.5 5.4 %collective-permute-start.5 = (f32[80,128]{1,0:T(8,128)S(1)}, f32[80,128]{1,0:T(8,128)S(1)}, u32[]{:S(2)}, u32[]{:S(2)}) collective-permute-start(f32[80,128]{1,0:T(8,128)S(1)} %pad_maximum_fusion.recv0), channel_id=1, source_target_pairs={{0,2},{1,3},{2,4},{3,5},{4,6},{5,7},{6,0},{7,1},{8,10},{9,11},{10,... | collective-permute-start | bytes 122888 | tf_op jit(solution)/shard_map/ppermute | solution.py:641
  70.4 4.3 %collective-permute-start.8 = (f32[40,128]{1,0:T(8,128)S(1)}, f32[40,128]{1,0:T(8,128)S(1)}, u32[]{:S(2)}, u32[]{:S(2)}) collective-permute-start(f32[40,128]{1,0:T(8,128)S(1)} %products.4), channel_id=1, source_target_pairs={{0,1},{1,0},{2,3},{3,2},{4,5},{5,4},{6,7},{7,6},{8,9},{9,8},{10,11... | collective-permute-start | bytes 61448 | tf_op jit(solution)/shard_map/ppermute | solution.py:637
  74.7 2.9 %collective-permute-start.11 = (f32[80,128]{1,0:T(8,128)S(1)}, f32[80,128]{1,0:T(8,128)S(1)}, u32[]{:S(2)}, u32[]{:S(2)}) collective-permute-start(f32[80,128]{1,0:T(8,128)S(1)} %pad_maximum_fusion.1.recv0), channel_id=1, source_target_pairs={{0,6},{1,7},{2,0},{3,1},{4,2},{5,3},{6,4},{7,5},{8,14},{9,15},{10,... | collective-permute-start | bytes 122888 | tf_op jit(solution)/shard_map/ppermute | solution.py:641
  75.8 4.4 %collective-permute-start.10 = (f32[80,128]{1,0:T(8,128)S(1)}, f32[80,128]{1,0:T(8,128)S(1)}, u32[]{:S(2)}, u32[]{:S(2)}) collective-permute-start(f32[80,128]{1,0:T(8,128)S(1)} %pad_maximum_fusion.1.recv0), channel_id=1, source_target_pairs={{0,4},{1,5},{2,6},{3,7},{4,0},{5,1},{6,2},{7,3},{8,12},{9,13},{10,... | collective-permute-start | bytes 122888 | tf_op jit(solution)/shard_map/ppermute | solution.py:641
  76.5 4.1 %collective-permute-start.9 = (f32[80,128]{1,0:T(8,128)S(1)}, f32[80,128]{1,0:T(8,128)S(1)}, u32[]{:S(2)}, u32[]{:S(2)}) collective-permute-start(f32[80,128]{1,0:T(8,128)S(1)} %pad_maximum_fusion.1.recv0), channel_id=1, source_target_pairs={{0,2},{1,3},{2,4},{3,5},{4,6},{5,7},{6,0},{7,1},{8,10},{9,11},{10,... | collective-permute-start | bytes 122888 | tf_op jit(solution)/shard_map/ppermute | solution.py:641
  99.1 5.3 %collective-permute-start.12 = (f32[40,128]{1,0:T(8,128)S(1)}, f32[40,128]{1,0:T(8,128)S(1)}, u32[]{:S(2)}, u32[]{:S(2)}) collective-permute-start(f32[40,128]{1,0:T(8,128)S(1)} %products.5), channel_id=1, source_target_pairs={{0,1},{1,0},{2,3},{3,2},{4,5},{5,4},{6,7},{7,6},{8,9},{9,8},{10,11... | collective-permute-start | bytes 61448 | tf_op jit(solution)/shard_map/ppermute | solution.py:637
  104.4 2.9 %collective-permute-start.15 = (f32[80,128]{1,0:T(8,128)S(1)}, f32[80,128]{1,0:T(8,128)S(1)}, u32[]{:S(2)}, u32[]{:S(2)}) collective-permute-start(f32[80,128]{1,0:T(8,128)S(1)} %pad_maximum_fusion.2.recv0), channel_id=1, source_target_pairs={{0,6},{1,7},{2,0},{3,1},{4,2},{5,3},{6,4},{7,5},{8,14},{9,15},{10,... | collective-permute-start | bytes 122888 | tf_op jit(solution)/shard_map/ppermute | solution.py:641
  105.4 4.4 %collective-permute-start.14 = (f32[80,128]{1,0:T(8,128)S(1)}, f32[80,128]{1,0:T(8,128)S(1)}, u32[]{:S(2)}, u32[]{:S(2)}) collective-permute-start(f32[80,128]{1,0:T(8,128)S(1)} %pad_maximum_fusion.2.recv0), channel_id=1, source_target_pairs={{0,4},{1,5},{2,6},{3,7},{4,0},{5,1},{6,2},{7,3},{8,12},{9,13},{10,... | collective-permute-start | bytes 122888 | tf_op jit(solution)/shard_map/ppermute | solution.py:641
  106.0 4.2 %collective-permute-start.13 = (f32[80,128]{1,0:T(8,128)S(1)}, f32[80,128]{1,0:T(8,128)S(1)}, u32[]{:S(2)}, u32[]{:S(2)}) collective-permute-start(f32[80,128]{1,0:T(8,128)S(1)} %pad_maximum_fusion.2.recv0), channel_id=1, source_target_pairs={{0,2},{1,3},{2,4},{3,5},{4,6},{5,7},{6,0},{7,1},{8,10},{9,11},{10,... | collective-permute-start | bytes 122888 | tf_op jit(solution)/shard_map/ppermute | solution.py:641
  133.0 13.2 %copy-start = (f32[6,256]{1,0:T(8,128)S(1)}, f32[6,256]{1,0:T(8,128)}, u32[]{:S(2)}) copy-start(f32[6,256]{1,0:T(8,128)} %right_ref.1) | copy-start | bytes 18436
